TPU v7x, 256 devices: a whole 4x4x8 slice. The times are simulated.
256 devices in a mesh: pix: 128 (over x_hi, z, y, core), tm: 2 (over x_lo).
Axes of the slice: x: 4 (x_hi: 2, x_lo: 2; x = x_hi * 2 + x_lo), y: 4, z: 8, core: 2. Of those that a mesh axis runs over, the one named last changes fastest.
Arguments:
- iq: bfloat16 [600, 2, 524288], P('tm', None, 'pix'), as said below
- tail_frames: bfloat16 [150, 2, 524288], P(None, None, 'pix'), as said below
- start_basis: float32 [300, 128], replicated, may hold values from -6 to 6
- low_rank: int32 [4], P('tm'), may hold values from 1 to 32
- high_rank: int32 [4], P('tm'), may hold values from 64 to 128
Outputs:
- power: float32 [4, 524288], P('tm', 'pix')
- basis: float32 [4, 300, 128], P('tm')
Inputs may be any that keep to these rules, and one draw needn't show every extreme that they name: low_rank[w] < high_rank[w] <= 128 for every window. `iq`: real-valued samples of order one. `tail_frames`: real-valued samples of order one, continuing iq.
All inputs are finite; a program needn't handle non-finite values.
Results may differ from a plain program's by a relative error of at most 0.0008.
Values may be sent and summed in bfloat16 or wider, within the bound.
No kernel may reach another device: no remote copies, remote signals or barrier semaphores. Data moves between devices by JAX's collectives and lax.ppermute only.
A program may use at most 128 MiB of HBM per device.

v0:
```python
import jax
import jax.numpy as jnp
from jax import lax
from jax.sharding import Mesh
from jax.sharding import PartitionSpec as P

K = 128
ITERS = 3
WIN_DEV = 2
PIX = ("pix_0", "pix_1", "pix_2", "pix_3")


def from_behind(block, axis, distance):
    devices = range(lax.axis_size(axis))
    route = [(i - distance, i) for i in devices if i - distance in devices]
    return lax.ppermute(block, axis, route)


def split_up(value, dim, peers):
    dims = value.shape
    tiles = value.reshape(*dims[:dim], peers, dims[dim] // peers, *dims[dim + 1 :])
    return jnp.moveaxis(tiles, dim, 0)


def sent_and_summed(value, axis, dim):
    tiles = split_up(value, dim, lax.axis_size(axis))
    arrived = lax.all_to_all(tiles, axis, split_axis=0, concat_axis=0, tiled=True)
    return arrived.sum(axis=0)


def sum_in_two_steps(value, axes, dim):
    far, near = axes
    tiles = split_up(value, dim, lax.axis_size(far))
    nearer = sent_and_summed(tiles, near, dim + 1)
    arrived = lax.all_to_all(nearer, far, split_axis=0, concat_axis=0, tiled=True)
    return arrived.sum(axis=0)


def filled_up(lines, peers):
    spare = -lines.shape[0] % peers
    if not spare:
        return lines
    return jnp.concatenate([lines, jnp.zeros((spare, *lines.shape[1:]), lines.dtype)])


def sent_to_all(value, axis):
    peers = lax.axis_size(axis)
    return lax.all_to_all(
        jnp.broadcast_to(value[None], (peers, *value.shape)), axis, 0, 0, tiled=True
    )


def laid_out(tiles, dim):
    tiles = jnp.moveaxis(tiles, 0, dim)
    dims = tiles.shape
    return tiles.reshape(*dims[:dim], dims[dim] * dims[dim + 1], *dims[dim + 2 :])


def gather_axes(value, axes, dim):
    far, near = axes
    leading = sent_to_all(value, far)
    tiles = jnp.swapaxes(sent_to_all(leading, near), 0, 1)
    return laid_out(tiles.reshape(-1, *value.shape), dim)


def nested_sum(value, axes):
    lines = value.reshape(-1)
    own = sum_in_two_steps(
        filled_up(lines, lax.axis_size(axes[0]) * lax.axis_size(axes[1])), axes, 0
    )
    whole = gather_axes(own, axes, 0)
    return whole[: len(lines)].reshape(value.shape)


def iterate(gram, start):
    basis = start
    for step in range(ITERS):
        image = jnp.dot(gram, basis, precision=lax.Precision.HIGHEST)
        inner = jnp.dot(image.T, image, precision=lax.Precision.HIGHEST)
        factor = jnp.linalg.cholesky(inner)
        basis = lax.linalg.triangular_solve(
            factor, image, left_side=False, lower=True, transpose_a=True
        )
    return basis


def body(iq, tail_frames, start_basis, low_rank, high_rank):
    half = iq.shape[0] // WIN_DEV
    width = 2 * half
    incoming = from_behind(iq[:half], "tm", -1)
    at_end = lax.axis_index("tm") == lax.axis_size("tm") - 1
    following = jnp.where(at_end, tail_frames, incoming)
    extended = jnp.concatenate([iq, following], axis=0)
    casoratis = [
        extended[window * half : window * half + width].reshape(width, -1)
        for window in range(WIN_DEV)
    ]

    def local_gram(matrix):
        return lax.dot_general(
            matrix, matrix, (((1,), (1,)), ((), ())), preferred_element_type=jnp.float32
        )

    stacked = jnp.stack([local_gram(matrix) for matrix in casoratis])
    summed = nested_sum(stacked, (("pix_0", "pix_1", "pix_2"), "pix_3"))
    grams = [summed[window] for window in range(WIN_DEV)]
    columns = jnp.arange(K, dtype=jnp.int32)
    powers = []
    bases = []
    for window in range(WIN_DEV):
        basis = iterate(grams[window], start_basis)
        keep = ((columns >= low_rank[window]) & (columns < high_rank[window])).astype(jnp.float32)
        proj = jnp.dot(basis * keep[None, :], basis.T, precision=lax.Precision.HIGHEST).astype(
            jnp.bfloat16
        )
        filtered = jnp.dot(proj, casoratis[window], preferred_element_type=jnp.float32)
        powers.append(jnp.sum((filtered * filtered).reshape(width, 2, -1), axis=(0, 1)) / width)
        bases.append(basis)
    return (jnp.stack(powers), jnp.stack(bases))


def solution(mesh):
    torus = Mesh(
        mesh.devices.reshape(2, 8, 4, 2, mesh.shape["tm"]),
        ("pix_0", "pix_1", "pix_2", "pix_3", "tm"),
    )
    return jax.shard_map(
        body,
        mesh=torus,
        in_specs=(P("tm", None, PIX), P(None, None, PIX), P(), P("tm"), P("tm")),
        out_specs=(P("tm", PIX), P("tm", None, None)),
        check_vma=False,
    )
```

profile of v0, /device:TPU:1, one launch (start us, length us, event | category | flops | bytes accessed | tf_op | source)
XLA Modules:
  0.0 340.2 jit_solution(5225296486359567458)
XLA Ops:
  0.7 4.3 %slice.35 = bf16[150,2,4096]{2,1,0:T(2,128)(2,1)S(1)} slice(bf16[300,2,4096]{2,1,0:T(2,128)(2,1)} %param.8), slice={[0:150], [0:2], [0:4096]} | slice | bytes 4915200 | tf_op jit(solution)/shard_map/slice | solution.py:90
  4.9 1.3 collective-permute-start
  6.3 5.7 %copy.61 = bf16[300,2,4096]{2,0,1:T(8,128)(2,1)} copy(bf16[300,2,4096]{2,1,0:T(2,128)(2,1)S(1)} %copy-done.1) | data formatting | bytes 9830400 | tf_op args[0]
  11.9 22.0 %convolution_bitcast_fusion.1 = f32[1,300,300]{2,1,0:T(8,128)S(1)} fusion(bf16[300,2,4096]{2,1,0:T(2,128)(2,1)} %param.8), kind=kOutput, calls=%fused_computation.7 | convolution fusion | flops 1474560000 | bytes 5275200 | tf_op jit(solution)/shard_map/dot_general | solution.py:100
  34.0 24.7 %collective-permute-done = bf16[150,2,4096]{2,1,0:T(2,128)(2,1)} collective-permute-done((bf16[150,2,4096]{2,1,0:T(2,128)(2,1)S(1)}, bf16[150,2,4096]{2,1,0:T(2,128)(2,1)}, u32[]{:S(2)}, u32[]{:S(2)}) %collective-permute-start) | collective-permute-done | bytes 2457632 | tf_op jit(solution)/shard_map/ppermute | solution.py:16
  58.7 6.9 %copy_select_fusion = bf16[150,2,4096]{2,0,1:T(8,128)(2,1)S(1)} fusion(bf16[150,2,4096]{2,1,0:T(2,128)(2,1)} %collective-permute-done, bf16[150,2,4096]{2,1,0:T(2,128)(2,1)S(1)} %copy-done.4, pred[]{:T(512)S(6)} %eq.3), kind=kLoop, calls=%fused_computation.3 | loop fusion | flops 1228800 | bytes 7372801 | tf_op jit(solution)/shard_map/jit(_where)/select_n | solution.py:92
  65.6 1.5 pad_maximum_fusion
  67.1 2.7 convolution_bitcast_fusion
  69.9 0.7 reshape.77
  70.8 1.0 reshape_reshape.6
  71.8 8.0 %all_to_all.25 = f32[2,64,1407]{2,1,0:T(8,128)S(1)} all-to-all(f32[2,64,1407]{2,1,0:T(8,128)S(1)} %copy.66), channel_id=1, replica_groups=mesh['pix_0'=2,'pix_1'=8,'pix_2'=4,'pix_3'=2,'tm'=2] {'pix_3'}, dimensions={0} | all-to-all | bytes 1440768 | tf_op jit(solution)/shard_map/all_to_all | solution.py:27
  80.1 28.9 %all_to_all.26 = f32[64,1,1407]{2,1,0:T(1,128)S(1)} all-to-all(f32[64,1,1407]{2,1,0:T(1,128)S(1)} %all_to_all.17), channel_id=1, replica_groups=mesh['pix_0'=2,'pix_1'=8,'pix_2'=4,'pix_3'=2,'tm'=2] {'pix_0','pix_1','p..., dimensions={0} | all-to-all | bytes 720384 | tf_op jit(solution)/shard_map/all_to_all | solution.py:35
  109.2 0.9 broadcast_in_dim.6
  110.2 7.5 %all-to-all-start.2 = ((f32[64,1,1407]{2,1,0:T(1,128)}), f32[64,1,1407]{2,1,0:T(1,128)S(1)}, u32[]{:S(2)}, u32[]{:S(2)}) async-start(f32[64,1,1407]{2,1,0:T(1,128)} %broadcast_in_dim.6), calls=%async_computation.2 | async-start | bytes 720896 | tf_op jit(solution)/shard_map/all_to_all | solution.py:48
  117.7 9.8 %pad.11 = bf16[304,2,4096]{2,1,0:T(2,128)(2,1)} pad(bf16[300,2,4096]{2,1,0:T(2,128)(2,1)} %param.8, bf16[]{:T(256)} %constant.48), padding=0_4x0_0x0_0 | pad | bytes 9895938
  127.5 10.3 %copy.77 = bf16[38,8,2,4096]{3,1,2,0:T(8,128)(2,1)} copy(bf16[38,8,2,4096]{3,2,1,0:T(2,128)(2,1)} %bitcast.136) | data formatting | bytes 9961472
  137.8 0.6 fusion.35
  138.4 0.6 fusion.34
  139.0 1.2 and_convert_fusion
  140.2 1.2 and_convert_fusion.1
  141.4 10.0 %copy.74 = bf16[300,2,4096]{2,1,0:T(2,128)(2,1)} copy(bf16[300,2,4096]{2,0,1:T(8,128)(2,1)} %copy-done.2) | data formatting | bytes 9830400 | tf_op jit(solution)/shard_map/slice | solution.py:95
  151.4 9.8 %pad.12 = bf16[304,2,4096]{2,1,0:T(2,128)(2,1)} pad(bf16[300,2,4096]{2,1,0:T(2,128)(2,1)} %copy.74, bf16[]{:T(256)} %constant.48), padding=0_4x0_0x0_0 | pad | bytes 9895938
  161.2 10.8 %copy.78 = bf16[38,8,2,4096]{3,1,2,0:T(8,128)(2,1)} copy(bf16[38,8,2,4096]{3,2,1,0:T(2,128)(2,1)} %bitcast.135) | data formatting | bytes 9961472
  172.1 5.5 %all_to_all.27 = f32[2,64,1407]{2,1,0:T(8,128)S(1)} all-to-all(f32[2,64,1407]{2,1,0:T(8,128)S(1)} %broadcast_in_dim.8), channel_id=1, replica_groups=mesh['pix_0'=2,'pix_1'=8,'pix_2'=4,'pix_3'=2,'tm'=2] {'pix_3'}, dimensions={0} | all-to-all | bytes 1440768 | tf_op jit(solution)/shard_map/all_to_all | solution.py:48
  177.5 0.6 copy.67
  178.1 0.6 reshape_reshape.7
  179.4 0.5 fusion.42
  180.6 11.7 %cholesky.137 = f32[128,128]{1,0:T(8,128)S(1)} custom-call(f32[128,128]{1,0:T(8,128)S(1)} %fusion.20), custom_call_target="Cholesky" | custom-call | tf_op jit(solution)/shard_map/jit(cholesky)/cholesky | solution.py:80
  192.3 0.6 compare_reduce_fusion.2
  192.9 0.7 fusion.11
  193.6 9.8 %custom-call.13 = f32[1,128,128]{1,2,0:T(8,128)S(1)} custom-call(f32[1,128,128]{2,1,0:T(8,128)S(1)} %fusion.11), custom_call_target="InvertDiagBlocksLowerTriangular" | custom-call | tf_op jit(solution)/shard_map/triangular_solve/custom-call.0 | solution.py:81
  203.7 0.5 fusion.44
  204.2 0.5 fusion.45
  204.9 11.9 %cholesky.148 = f32[128,128]{1,0:T(8,128)S(1)} custom-call(f32[128,128]{1,0:T(8,128)S(1)} %fusion.18), custom_call_target="Cholesky" | custom-call | tf_op jit(solution)/shard_map/jit(cholesky)/cholesky | solution.py:80
  216.8 0.6 compare_reduce_fusion.1
  217.4 0.7 fusion.12
  218.1 9.8 %custom-call.14 = f32[1,128,128]{1,2,0:T(8,128)S(1)} custom-call(f32[1,128,128]{2,1,0:T(8,128)S(1)} %fusion.12), custom_call_target="InvertDiagBlocksLowerTriangular" | custom-call | tf_op jit(solution)/shard_map/triangular_solve/custom-call.0 | solution.py:81
  228.2 0.5 fusion.46
  228.7 0.5 fusion.47
  229.3 11.7 %cholesky.159 = f32[128,128]{1,0:T(8,128)S(1)} custom-call(f32[128,128]{1,0:T(8,128)S(1)} %fusion.16), custom_call_target="Cholesky" | custom-call | tf_op jit(solution)/shard_map/jit(cholesky)/cholesky | solution.py:80
  241.1 0.6 compare_reduce_fusion
  241.7 0.7 fusion.13
  242.4 9.8 %custom-call.15 = f32[1,128,128]{1,2,0:T(8,128)S(1)} custom-call(f32[1,128,128]{2,1,0:T(8,128)S(1)} %fusion.13), custom_call_target="InvertDiagBlocksLowerTriangular" | custom-call | tf_op jit(solution)/shard_map/triangular_solve/custom-call.0 | solution.py:81
  252.5 0.9 convolution_convert_fusion
  253.4 5.4 %fusion.1 = f32[8192]{0:T(1024)S(1)} fusion(bf16[300,300]{1,0:T(8,128)(2,1)S(1)} %convolution_convert_fusion, bf16[300,8192]{1,0:T(8,128)(2,1)} %bitcast.138), kind=kOutput, calls=%fused_computation.5 | convolution fusion | flops 1479467008 | bytes 5127968 | tf_op jit(solution)/shard_map/dot_general | solution.py:116
  259.4 0.5 fusion.36
  260.5 11.7 %cholesky.104 = f32[128,128]{1,0:T(8,128)S(1)} custom-call(f32[128,128]{1,0:T(8,128)S(1)} %fusion.27), custom_call_target="Cholesky" | custom-call | tf_op jit(solution)/shard_map/jit(cholesky)/cholesky | solution.py:80
  272.3 0.6 compare_reduce_fusion.5
  272.9 0.7 fusion.8
  273.6 9.8 %custom-call.10 = f32[1,128,128]{1,2,0:T(8,128)S(1)} custom-call(f32[1,128,128]{2,1,0:T(8,128)S(1)} %fusion.8), custom_call_target="InvertDiagBlocksLowerTriangular" | custom-call | tf_op jit(solution)/shard_map/triangular_solve/custom-call.0 | solution.py:81
  283.7 0.5 fusion.38
  284.9 11.9 %cholesky.115 = f32[128,128]{1,0:T(8,128)S(1)} custom-call(f32[128,128]{1,0:T(8,128)S(1)} %fusion.25), custom_call_target="Cholesky" | custom-call | tf_op jit(solution)/shard_map/jit(cholesky)/cholesky | solution.py:80
  296.8 0.6 compare_reduce_fusion.4
  297.4 0.7 fusion.9
  298.1 9.8 %custom-call.11 = f32[1,128,128]{1,2,0:T(8,128)S(1)} custom-call(f32[1,128,128]{2,1,0:T(8,128)S(1)} %fusion.9), custom_call_target="InvertDiagBlocksLowerTriangular" | custom-call | tf_op jit(solution)/shard_map/triangular_solve/custom-call.0 | solution.py:81
  308.2 0.5 fusion.40
  309.3 11.7 %cholesky.126 = f32[128,128]{1,0:T(8,128)S(1)} custom-call(f32[128,128]{1,0:T(8,128)S(1)} %fusion.23), custom_call_target="Cholesky" | custom-call | tf_op jit(solution)/shard_map/jit(cholesky)/cholesky | solution.py:80
  321.1 0.6 compare_reduce_fusion.3
  321.7 0.7 fusion.10
  322.4 9.8 %custom-call.12 = f32[1,128,128]{1,2,0:T(8,128)S(1)} custom-call(f32[1,128,128]{2,1,0:T(8,128)S(1)} %fusion.10), custom_call_target="InvertDiagBlocksLowerTriangular" | custom-call | tf_op jit(solution)/shard_map/triangular_solve/custom-call.0 | solution.py:81
  332.5 0.5 convolution_convert_fusion.1
  333.0 5.4 %fusion = f32[8192]{0:T(1024)S(1)} fusion(bf16[300,300]{1,0:T(8,128)(2,1)S(1)} %convolution_convert_fusion.1, bf16[300,8192]{1,0:T(8,128)(2,1)} %bitcast.137), kind=kOutput, calls=%fused_computation.4 | convolution fusion | flops 1479467008 | bytes 5127968 | tf_op jit(solution)/shard_map/dot_general | solution.py:116
  338.5 0.9 copy.75
  339.4 0.6 pad_maximum_fusion.3
  (61 shorter events, 6.6 us)
Async XLA Ops:
  0.6 178.8 %copy-start = (f32[300,128]{1,0:T(8,128)S(1)}, f32[300,128]{1,0:T(8,128)}, u32[]{:S(2)}) copy-start(f32[300,128]{1,0:T(8,128)} %param.10) | copy-start | bytes 460804
  0.6 5.6 %copy-start.1 = (bf16[300,2,4096]{2,1,0:T(2,128)(2,1)S(1)}, bf16[300,2,4096]{2,1,0:T(2,128)(2,1)}, u32[]{:S(2)}) copy-start(bf16[300,2,4096]{2,1,0:T(2,128)(2,1)} %param.8) | copy-start | bytes 14745604
  4.9 53.7 %collective-permute-start = (bf16[150,2,4096]{2,1,0:T(2,128)(2,1)S(1)}, bf16[150,2,4096]{2,1,0:T(2,128)(2,1)}, u32[]{:S(2)}, u32[]{:S(2)}) collective-permute-start(bf16[150,2,4096]{2,1,0:T(2,128)(2,1)S(1)} %slice.35), channel_id=1, source_target_pairs={{1,0},{3,2},{5,4},{7,6},{9,8},{11,10},{13,12},{15,14},{17,16},{19,... | collective-permute-start | bytes 7372808 | tf_op jit(solution)/shard_map/ppermute | solution.py:16
  11.9 46.7 %copy-start.4 = (bf16[150,2,4096]{2,1,0:T(2,128)(2,1)S(1)}, bf16[150,2,4096]{2,1,0:T(2,128)(2,1)}, u32[]{:S(2)}) copy-start(bf16[150,2,4096]{2,1,0:T(2,128)(2,1)} %param.9) | copy-start | bytes 7372804
  33.9 31.6 %copy-start.3 = (bf16[300,2,4096]{2,0,1:T(8,128)(2,1)S(1)}, bf16[300,2,4096]{2,0,1:T(8,128)(2,1)}, u32[]{:S(2)}) copy-start(bf16[300,2,4096]{2,0,1:T(8,128)(2,1)} %copy.61) | copy-start | bytes 14745604
  67.1 2.8 copy-start.2
  110.2 61.8 %all-to-all-start.2 = ((f32[64,1,1407]{2,1,0:T(1,128)}), f32[64,1,1407]{2,1,0:T(1,128)S(1)}, u32[]{:S(2)}, u32[]{:S(2)}) async-start(f32[64,1,1407]{2,1,0:T(1,128)} %broadcast_in_dim.6), calls=%async_computation.2 | async-start | bytes 720896 | tf_op jit(solution)/shard_map/all_to_all | solution.py:48
  127.5 10.3 %copy-start.5 = (s32[2]{0:T(128)S(1)}, s32[2]{0:T(128)}, u32[]{:S(2)}) copy-start(s32[2]{0:T(128)} %param.12) | copy-start | bytes 28
  127.5 10.9 %copy-start.6 = (s32[2]{0:T(128)S(1)}, s32[2]{0:T(128)}, u32[]{:S(2)}) copy-start(s32[2]{0:T(128)} %param.11) | copy-start | bytes 28
where the time goes:
time: 346 us; the launch traced here: 340 us
  other arithmetic  149 us (43%)
  local copies, waits for them, and re-layouts  68.7 us (20%)
  matrix products  44.8 us (13%)
  blocking collectives  42.3 us (12%)
  waiting for transfers between devices  24.7 us (7%)
  starting transfers between devices  8.78 us (3%)
    another operation x18, other arithmetic, iterate(): factor = jnp.linalg.cholesky(inner)  74.6 us
    another operation x12, other arithmetic, iterate(): lax.linalg.triangular_solve(factor, image, left_side=False, lower=True, t...  62.8 us
    unnamed x21, local copies, waits for them, and re-layouts  47.3 us
    all_to_all x1, blocking collectives, sum_in_two_steps(): lax.all_to_all(nearer, far, split_axis=0, concat_axis=0, tiled=True)  28.9 us
    dot_general x2, matrix products, local_gram(): lax.dot_general(matrix, matrix, (((1,), (1,)), ((), ())), preferred_eleme...  24.7 us
    ppermute x1, waiting for transfers between devices, from_behind(): return lax.ppermute(block, axis, route)  24.7 us
    dot_general x2, matrix products, body(): jnp.dot(proj, casoratis[window], preferred_element_type=jnp.float32)  10.8 us
    slice x1, local copies, waits for them, and re-layouts, body(): extended[window * half:window * half + width].reshape(width, -1)  10 us
  transfers between devices with their start and end apart: 2, of which 1 were waited for; matrix products, arithmetic and copies ran while one was open for 24% of the time, Pallas kernels for 0%

commit v1 on v0

v1 whole, which is shorter than its diff:
```python
import functools

import jax
import jax.numpy as jnp
from jax import lax
from jax.experimental import pallas as pl
from jax.experimental.pallas import tpu as pltpu
from jax.sharding import Mesh
from jax.sharding import PartitionSpec as P

K = 128
ITERS = 3
WINDOW = 300
HALF = 150
MAIN = 128
REM = HALF - MAIN
SPAN = 384
USED = 320
TILE = 32
PACKED = 512
HI = lax.Precision.HIGHEST
F32 = jnp.float32
BF16 = jnp.bfloat16
PIX = ("pix_0", "pix_1", "pix_2", "pix_3")
CHIPS = ("pix_0", "pix_1", "pix_2")
SMEM = pl.BlockSpec(memory_space=pltpu.SMEM)
VMEM = pl.BlockSpec(memory_space=pltpu.VMEM)


def grid_of(shape, axis):
    return lax.broadcasted_iota(jnp.int32, shape, axis)


def across(a, b):
    return lax.dot_general(a, b, (((1,), (1,)), ((), ())), preferred_element_type=F32)


def pack(out, first, cross, second):
    row = grid_of((MAIN, 128), 0)
    lane = grid_of((MAIN, 128), 1)
    zero = jnp.zeros((152, 128), F32)
    one = zero if first is None else first[:, 128:256]
    two = zero if cross is None else pltpu.roll(cross[:, 128:256], 32, 1)
    three = zero if second is None else pltpu.roll(second[:, 128:256], 64, 1)
    upper = zero[:MAIN] if first is None else first[0:MAIN, 0:128]
    lower = zero[:MAIN] if second is None else second[0:MAIN, 0:128]
    out[0:MAIN, :] = jnp.where(lane >= row, upper, lower)
    out[128:280, :] = zero if cross is None else cross[:, 0:128]
    out[280:432, :] = one + two + three
    out[432:440, :] = jnp.where(
        grid_of((8, 128), 0) == 0,
        jnp.sum(jnp.where(lane == row, lower, 0.0), axis=0, keepdims=True),
        0.0,
    )
    out[440:, :] = jnp.zeros((PACKED - 440, 128), F32)


def local_kernel(place, frames, tail, even, odd, extra, sums):
    step = pl.program_id(0)

    @pl.when(step == 0)
    def _():
        sums[...] = jnp.zeros_like(sums)

    for part in range(2):
        a = frames[part, 0]
        b = frames[part, 1]
        c = tail[part]
        for index, (left, right) in enumerate(((a, a), (a, b), (b, b), (b, c), (c, c))):
            sums[index, 0:HALF, 0:HALF] += across(left, right)

    @pl.when(step == pl.num_programs(0) - 1)
    def _():
        pack(even, sums[0], sums[1], sums[2])
        scale = place[1].astype(F32)
        pack(odd, sums[2], sums[3] * scale, sums[4] * scale)
        pack(extra, None, None, sums[0])


def local_products(place, frames, tail):
    pixels = frames.shape[-1]
    steps = 4
    width = pixels // steps
    out = jax.ShapeDtypeStruct((PACKED, 128), F32)
    whole = pl.BlockSpec((PACKED, 128), lambda i: (0, 0))
    return pl.pallas_call(
        local_kernel,
        grid=(steps,),
        out_shape=(out, out, out),
        in_specs=[
            SMEM,
            pl.BlockSpec((2, 2, HALF, width), lambda i: (0, 0, 0, i)),
            pl.BlockSpec((2, HALF, width), lambda i: (0, 0, i)),
        ],
        out_specs=(whole, whole, whole),
        scratch_shapes=[pltpu.VMEM((5, 152, 256), F32)],
        cost_estimate=pl.CostEstimate(flops=4 * 10**9, bytes_accessed=8 * 10**6, transcendentals=0),
        name="local_products",
    )(place, frames, tail)


def cross_kernel(place, frames, arrived, even, odd, extra, keep, swap, send, sums, mix):
    last = place[1] == 1
    half = arrived.shape[-1]
    total = jnp.zeros((HALF, HALF), F32)
    for part in range(2):
        got = arrived[part]
        left = jnp.where(last, got, frames[part, 1, :, 0:half])
        right = jnp.where(last, frames[part, 0, :, half:], got)
        total += across(left, right)
    sums[...] = jnp.zeros_like(sums)
    sums[0:HALF, 0:HALF] = total
    pack(mix, None, sums[...], None)
    later = odd[...] + jnp.where(last, 0.0, mix[...])
    sooner = even[...]
    core = place[0] == 1
    keep[...] = jnp.where(core, later, sooner)
    swap[...] = jnp.where(core, sooner, later)
    send[...] = extra[...] + mix[...]


def cross_products(place, frames, arrived, even, odd, extra):
    out = jax.ShapeDtypeStruct((PACKED, 128), F32)
    return pl.pallas_call(
        cross_kernel,
        out_shape=(out, out, out),
        in_specs=[SMEM] + [VMEM] * 5,
        out_specs=(VMEM, VMEM, VMEM),
        scratch_shapes=[pltpu.VMEM((152, 256), F32), pltpu.VMEM((PACKED, 128), F32)],
        name="cross_products",
    )(place, frames, arrived, even, odd, extra)


def unpack(rows, gram):
    row = grid_of((128, 128), 0)
    lane = grid_of((128, 128), 1)
    both = rows[0:128]
    turned = both.T
    gram[0:128, 0:128] = jnp.where(lane >= row, both, turned)
    gram[128:256, 128:256] = jnp.where(
        lane < row, both, jnp.where(lane == row, rows[432:433], turned)
    )
    cross = rows[128:256]
    gram[0:128, 128:256] = cross
    gram[128:256, 0:128] = cross.T
    side = rows[280:408]
    turn = jnp.concatenate([rows[256:280], jnp.zeros((104, 128), F32)], axis=0).T
    first = jnp.where(lane < 64, side, 0.0)
    second = jnp.where(lane < 32, turn, jnp.where(lane < 64, pltpu.roll(side, 96, 1), 0.0))
    gram[0:128, 256:384] = first
    gram[128:256, 256:384] = second
    gram[256:384, 0:128] = first.T
    gram[256:384, 128:256] = second.T
    corner = rows[408:432]
    gram[256:384, 256:384] = jnp.zeros((128, 128), F32)
    short = grid_of((24, 128), 1)
    gram[256:280, 256:384] = jnp.where(short < 64, corner, 0.0)
    moved = pltpu.roll(corner, 96, 1)
    square = jnp.concatenate(
        [jnp.where(short < 32, moved, 0.0), jnp.zeros((104, 128), F32)], axis=0
    ).T[0:24]
    gram[288:312, 256:384] = jnp.where(
        short < 32, square, jnp.where(short < 64, moved, 0.0)
    )


def row_of(vector, index):
    return jnp.broadcast_to(vector[index : index + 1, :], vector.shape)


def eliminate(work, step):
    first = TILE * step
    sub = grid_of((8, 128), 0)
    lane = grid_of((8, 128), 1)
    groups = TILE // 8
    cols = {}
    for g in range(groups):
        top = first + 8 * g
        block = work[top : top + 8, 0:128]
        for k in range(8 * (g + 1)):
            at = first + k
            cols[g, k] = jnp.broadcast_to(block[:, at : at + 1], (8, 128))
    inverse = [jnp.where(lane == sub + 8 * g, 1.0, 0.0).astype(F32) for g in range(groups)]
    for j in range(TILE):
        gj, rj = divmod(j, 8)
        scale = lax.rsqrt(row_of(cols[gj, j], rj))
        for g in range(gj, groups):
            cols[g, j] = cols[g, j] * scale
        for k in range(j + 1, TILE):
            gk, rk = divmod(k, 8)
            factor = row_of(cols[gk, j], rk)
            for g in range(gk, groups):
                cols[g, k] = cols[g, k] - cols[g, j] * factor
        pivot = row_of(inverse[gj], rj) * scale
        for g in range(gj, groups):
            if g == gj:
                below = jnp.where(sub > rj, cols[g, j], 0.0)
                inverse[g] = jnp.where(sub == rj, pivot, inverse[g] - below * pivot)
            else:
                inverse[g] = inverse[g] - cols[g, j] * pivot
    lhs = jnp.concatenate(inverse, axis=0)[:, 0:TILE]
    rows = jnp.dot(
        lhs, work[first : first + TILE, :], precision=HI, preferred_element_type=F32
    )
    work[first : first + TILE, :] = rows
    if first + TILE < K:
        change = lax.dot_general(
            rows[:, 0:128], rows, (((0,), (0,)), ((), ())), precision=HI,
            preferred_element_type=F32,
        )
        work[first + TILE :, :] = work[first + TILE :, :] - change[first + TILE :, :]


def iterate_kernel(packed, start, basis, gram, work):
    unpack(packed[...], gram)
    work[:, K:] = start[...]

    def step(_, carry):
        image = jnp.dot(work[:, K:], gram[...], precision=HI, preferred_element_type=F32)
        work[:, 0:K] = lax.dot_general(
            image, image, (((1,), (1,)), ((), ())), precision=HI, preferred_element_type=F32
        )
        work[:, K:] = image
        for index in range(K // TILE):
            eliminate(work, index)
        return carry

    lax.fori_loop(0, ITERS, step, 0)
    basis[...] = work[:, K:]


def iterate(packed, start):
    return pl.pallas_call(
        iterate_kernel,
        out_shape=jax.ShapeDtypeStruct((K, SPAN), F32),
        in_specs=[VMEM, VMEM],
        out_specs=VMEM,
        scratch_shapes=[pltpu.VMEM((SPAN, SPAN), F32), pltpu.VMEM((K, K + SPAN), F32)],
        cost_estimate=pl.CostEstimate(flops=2 * 10**9, bytes_accessed=10**6, transcendentals=0),
        name="iterate",
    )(packed, start)


def finish_kernel(
    place, low, high, mine, other, frames, tail, near, far, power, basis, proj, chunk
):
    step = pl.program_id(0)
    core = place[0] == 1
    last = place[1] == 1
    half = pl.num_programs(0) // 2

    @pl.when(step == 0)
    def _():
        chunk[...] = jnp.zeros_like(chunk)
        index = grid_of((K, USED), 0)
        for window in range(2):
            own = core if window else jnp.logical_not(core)
            rows = jnp.where(own, mine[...], other[...])
            used = rows[:, 0:USED]
            kept = jnp.where((index >= low[window]) & (index < high[window]), used, 0.0)
            proj[window] = lax.dot_general(
                kept, used, (((0,), (0,)), ((), ())), precision=HI, preferred_element_type=F32
            ).astype(BF16)
            ends = rows[:, 256:384].T
            basis[window, 0:MAIN] = rows[:, 0:128].T
            basis[window, MAIN:HALF] = ends[0:REM]
            basis[window, HALF : HALF + MAIN] = rows[:, 128:256].T
            basis[window, HALF + MAIN : WINDOW] = ends[32 : 32 + REM]

    def fill(at, block):
        chunk[128 * at : 128 * at + MAIN, :] = block[0:MAIN]
        chunk[256 + 32 * at : 256 + 32 * at + REM, :] = block[MAIN:HALF]

    for window in range(2):
        total = jnp.zeros((1, chunk.shape[1]), F32)
        for part in range(2):
            if window == 0:
                one, two = frames[part, 0], frames[part, 1]
            else:
                one = frames[part, 1]
                two = jnp.where(last, tail[part], jnp.where(step < half, near[part], far[part]))
            fill(0, one)
            fill(1, two)
            out = jnp.dot(proj[window], chunk[...], preferred_element_type=F32)
            total += jnp.sum(out * out, axis=0, keepdims=True)
        power[window : window + 1, :] = total / WINDOW


def finish(place, low, high, mine, other, frames, tail, near, far):
    pixels = frames.shape[-1]
    steps = 8
    width = pixels // steps
    turn = steps // 2
    return pl.pallas_call(
        finish_kernel,
        grid=(steps,),
        out_shape=(
            jax.ShapeDtypeStruct((2, pixels), F32),
            jax.ShapeDtypeStruct((2, WINDOW, K), F32),
        ),
        in_specs=[
            SMEM,
            SMEM,
            SMEM,
            pl.BlockSpec((K, SPAN), lambda i: (0, 0)),
            pl.BlockSpec((K, SPAN), lambda i: (0, 0)),
            pl.BlockSpec((2, 2, HALF, width), lambda i: (0, 0, 0, i)),
            pl.BlockSpec((2, HALF, width), lambda i: (0, 0, i)),
            pl.BlockSpec((2, HALF, width), lambda i: (0, 0, jnp.minimum(i, turn - 1))),
            pl.BlockSpec((2, HALF, width), lambda i: (0, 0, jnp.maximum(i - turn, 0))),
        ],
        out_specs=(
            pl.BlockSpec((2, width), lambda i: (0, i)),
            pl.BlockSpec((2, WINDOW, K), lambda i: (0, 0, 0)),
        ),
        scratch_shapes=[pltpu.VMEM((2, USED, USED), BF16), pltpu.VMEM((USED, width), BF16)],
        cost_estimate=pl.CostEstimate(flops=7 * 10**9, bytes_accessed=10**7, transcendentals=0),
        name="finish",
    )(place, low, high, mine, other, frames, tail, near, far)


def in_lanes(start):
    rows = start.T
    gap = jnp.zeros((K, 32 - REM), F32)
    rest = jnp.zeros((K, 64), F32)
    return jnp.concatenate(
        [
            rows[:, 0:MAIN],
            rows[:, HALF : HALF + MAIN],
            rows[:, MAIN:HALF],
            gap,
            rows[:, HALF + MAIN :],
            gap,
            rest,
        ],
        axis=1,
    )


def body(iq, tail_frames, start_basis, low_rank, high_rank):
    pixels = iq.shape[-1]
    half = pixels // 2
    core = lax.axis_index("pix_3")
    block = lax.axis_index("tm")
    place = jnp.stack([core, block]).astype(jnp.int32)
    chips = lax.axis_size(CHIPS)

    sent = jnp.where(block == 1, iq[:HALF, :, :half], iq[HALF:, :, half:])
    near = lax.ppermute(jnp.swapaxes(sent, 0, 1), "tm", [(0, 1), (1, 0)])
    frames = jnp.transpose(iq.reshape(2, HALF, 2, pixels), (2, 0, 1, 3))
    tail = jnp.swapaxes(tail_frames, 0, 1)
    even, odd, extra = local_products(place, frames, tail)
    keep, swap, send = cross_products(place, frames, near, even, odd, extra)
    far = lax.ppermute(frames[:, 0, :, half:], "tm", [(1, 0)])
    swapped = lax.ppermute(swap, "pix_3", [(0, 1), (1, 0)])
    own = lax.ppermute(send, ("pix_3", "tm"), [(3, 2)])
    across_core = lax.ppermute(send, ("pix_3", "tm"), [(1, 2)])
    mine = keep + swapped + own + across_core
    pieces = lax.all_to_all(mine.reshape(chips, PACKED // chips, 128), CHIPS, 0, 0, tiled=True)
    piece = pieces.sum(axis=0)
    packed = lax.all_to_all(
        jnp.broadcast_to(piece[None], pieces.shape), CHIPS, 0, 0, tiled=True
    ).reshape(PACKED, 128)
    found = iterate(packed, in_lanes(start_basis))
    other = lax.ppermute(found, "pix_3", [(0, 1), (1, 0)])
    return finish(place, low_rank, high_rank, found, other, frames, tail, near, far)


def solution(mesh):
    torus = Mesh(
        mesh.devices.reshape(2, 8, 4, 2, mesh.shape["tm"]),
        ("pix_0", "pix_1", "pix_2", "pix_3", "tm"),
    )
    return jax.shard_map(
        body,
        mesh=torus,
        in_specs=(P("tm", None, PIX), P(None, None, PIX), P(), P("tm"), P("tm")),
        out_specs=(P("tm", PIX), P("tm", None, None)),
        check_vma=False,
    )
```

time: 346 us -> 142 us (0.41)
  the two profiles are of different devices: /device:TPU:1 before, /device:TPU:6 now
where the time goes in v1:
time: 142 us; the launch traced here: 139 us
  Pallas kernels  40.9 us (29%)
  waiting for transfers between devices  39.5 us (28%)
  starting transfers between devices  30.5 us (21%)
  local copies, waits for them, and re-layouts  21 us (15%)
  other arithmetic  6.67 us (5%)
    pallas_call x1, Pallas kernels, iterate(): pl.pallas_call(iterate_kernel, out_shape=jax.ShapeDtypeStruct((K, SPAN),...  17.5 us
    all_to_all x1, starting transfers between devices, body(): lax.all_to_all(mine.reshape(chips, PACKED // chips, 128), CHIPS, 0, 0, ti...  14.7 us
    all_to_all x1, waiting for transfers between devices, body(): lax.all_to_all(jnp.broadcast_to(piece[None], pieces.shape), CHIPS, 0, 0,...  14.3 us
    pallas_call x1, Pallas kernels, finish(): pl.pallas_call(finish_kernel, grid=(steps,), out_shape=(jax.ShapeDtypeStr...  11.6 us
    ppermute x1, waiting for transfers between devices, body(): near = lax.ppermute(jnp.swapaxes(sent, 0, 1), 'tm', [(0, 1), (1, 0)])  11.5 us
    all_to_all x1, starting transfers between devices, body(): lax.all_to_all(jnp.broadcast_to(piece[None], pieces.shape), CHIPS, 0, 0,...  8.35 us
    all_to_all x1, waiting for transfers between devices, body(): lax.all_to_all(mine.reshape(chips, PACKED // chips, 128), CHIPS, 0, 0, ti...  8.09 us
    pallas_call x1, Pallas kernels, local_products(): pl.pallas_call(local_kernel, grid=(steps,), out_shape=(out, out, out), in...  7.32 us
  transfers between devices with their start and end apart: 8, of which 4 were waited for; matrix products, arithmetic and copies ran while one was open for 11% of the time, Pallas kernels for 18%

profile of v1, /device:TPU:6, one launch (start us, length us, event | category | flops | bytes accessed | tf_op | source)
XLA Modules:
  0.0 139.3 jit_solution(13882942306900940766)
XLA Ops:
  0.6 0.0 copy-start.1
  0.6 4.2 %fusion = bf16[2,150,2048]{2,0,1:T(2,128)(2,1)} fusion(pred[]{:T(512)S(6)} %eq.3, bf16[300,2,4096]{2,1,0:T(2,128)(2,1)} %param.5), kind=kLoop, calls=%fused_computation.4 | loop fusion | flops 614400 | bytes 3686401 | tf_op jit(solution)/shard_map/transpose | solution.py:349
  4.9 0.8 collective-permute-start
  5.7 0.0 copy-done.1
  5.7 0.0 copy-start
  5.7 3.1 %copy.37 = bf16[150,2,4096]{2,0,1:T(8,128)(2,1)} copy(bf16[150,2,4096]{2,1,0:T(2,128)(2,1)S(1)} %copy-done.1) | data formatting | bytes 4915200 | tf_op args[1]
  8.8 0.0 copy-done
  8.8 5.7 %copy.36 = bf16[2,150,2,4096]{3,1,0,2:T(8,128)(2,1)} copy(bf16[2,150,2,4096]{3,2,1,0:T(2,128)(2,1)S(1)} %bitcast.21) | data formatting | bytes 9830400 | tf_op jit(solution)/shard_map/reshape | solution.py:350
  14.5 0.7 pad_add_fusion.place
  15.1 7.3 %local_products.1 = (f32[512,128]{1,0:T(8,128)}, f32[512,128]{1,0:T(8,128)}, f32[512,128]{1,0:T(8,128)}) custom-call(s32[2]{0:T(128)} %pad_add_fusion.place, bf16[2,2,150,4096]{3,2,1,0:T(8,128)(2,1)} %bitcast.17, bf16[2,150,4096]{2,1,0:T(8,128)(2,1)} %bitcast.22), custom_call_target="tpu_custom_call" | custom-call | flops 4000000000 | bytes 8000000 | tf_op jit(solution)/shard_map/local_products/pallas_call | solution.py:86
  22.4 11.5 %collective-permute-done = bf16[2,150,2048]{2,0,1:T(2,128)(2,1)} collective-permute-done((bf16[2,150,2048]{2,0,1:T(2,128)(2,1)}, bf16[2,150,2048]{2,0,1:T(2,128)(2,1)}, u32[]{:S(2)}, u32[]{:S(2)}) %collective-permute-start) | collective-permute-done | bytes 1228832 | tf_op jit(solution)/shard_map/ppermute | solution.py:349
  33.9 2.9 %copy.27.arrived.near = bf16[2,150,2048]{2,1,0:T(8,128)(2,1)} copy(bf16[2,150,2048]{2,0,1:T(2,128)(2,1)} %collective-permute-done) | data formatting | bytes 2457600 | tf_op jit(solution)/shard_map/ppermute | solution.py:349
  36.8 4.5 %cross_products.1 = (f32[512,128]{1,0:T(8,128)}, f32[512,128]{1,0:T(8,128)}, f32[512,128]{1,0:T(8,128)}) custom-call(s32[2]{0:T(128)} %pad_add_fusion.place, bf16[2,2,150,4096]{3,2,1,0:T(8,128)(2,1)} %bitcast.18, bf16[2,150,2048]{2,1,0:T(8,128)(2,1)} %copy.27.arrived.near, f32[512,128]{1,0:T(8,128)} %get-tuple-element.8.even, ...), custom_call_target="tpu_custom_call" | custom-call | tf_op jit(solution)/shard_map/cross_products/pallas_call | solution.py:124
  41.3 0.0 collective-permute-start.1
  41.3 2.8 %collective-permute-start.3 = (f32[512,128]{1,0:T(8,128)}, f32[512,128]{1,0:T(8,128)S(1)}, u32[]{:S(2)}, u32[]{:S(2)}) collective-permute-start(f32[512,128]{1,0:T(8,128)} %get-tuple-element.13), channel_id=1, source_target_pairs={{1,2},{5,6},{9,10},{13,14},{17,18},{21,22},{25,26},{29,30},{33,34}... | collective-permute-start | bytes 786440 | tf_op jit(solution)/shard_map/ppermute | solution.py:357
  44.2 0.7 collective-permute-start.2
  44.9 0.0 collective-permute-done.1
  44.9 5.6 %collective-permute-done.3 = f32[512,128]{1,0:T(8,128)S(1)} collective-permute-done((f32[512,128]{1,0:T(8,128)}, f32[512,128]{1,0:T(8,128)S(1)}, u32[]{:S(2)}, u32[]{:S(2)}) %collective-permute-start.3) | collective-permute-done | bytes 262176 | tf_op jit(solution)/shard_map/ppermute | solution.py:357
  50.4 0.0 collective-permute-done.2
  50.4 1.7 %add_bitcast_fusion = f32[64,8,128]{2,1,0:T(8,128)} fusion(f32[512,128]{1,0:T(8,128)S(1)} %collective-permute-done.3, f32[512,128]{1,0:T(8,128)S(1)} %collective-permute-done.2, f32[512,128]{1,0:T(8,128)} %get-tuple-element.11, f32[512,128]{1,0:T(8,128)S(1)} %collective-permute-done.1), kind=kLoop, calls=%fused_computation.5 | loop fusion | flops 196608 | bytes 1310720 | tf_op jit(solution)/shard_map/reshape | solution.py:359
  52.2 14.7 %all-to-all-start = ((f32[64,8,128]{2,1,0:T(8,128)}), f32[64,8,128]{2,1,0:T(8,128)S(1)}, u32[]{:S(2)}, u32[]{:S(2)}) async-start(f32[64,8,128]{2,1,0:T(8,128)} %add_bitcast_fusion), calls=%async_computation | async-start | bytes 524288 | tf_op jit(solution)/shard_map/all_to_all | solution.py:359
  66.9 1.4 %slice_bitcast_fusion = bf16[2,150,2048]{2,1,0:T(8,128)(2,1)S(1)} fusion(bf16[2,2,150,4096]{3,2,1,0:T(8,128)(2,1)} %bitcast.19), kind=kLoop, calls=%fused_computation.3 | loop fusion | bytes 2457600 | tf_op jit(solution)/shard_map/squeeze | solution.py:354
  68.3 0.0 copy-start.3
  68.3 1.3 copy.29
  69.6 1.4 collective-permute-start.5
  71.0 8.1 %all-to-all-done = f32[64,8,128]{2,1,0:T(8,128)S(1)} async-done(((f32[64,8,128]{2,1,0:T(8,128)}), f32[64,8,128]{2,1,0:T(8,128)S(1)}, u32[]{:S(2)}, u32[]{:S(2)}) %all-to-all-start) | async-done | bytes 262176 | tf_op jit(solution)/shard_map/all_to_all | solution.py:359
  79.1 0.1 reduce_sum.9
  79.1 0.7 broadcast_in_dim.12
  79.9 8.3 %all-to-all-start.1 = ((f32[64,8,128]{2,1,0:T(8,128)}), f32[64,8,128]{2,1,0:T(8,128)S(1)}, u32[]{:S(2)}, u32[]{:S(2)}) async-start(f32[64,8,128]{2,1,0:T(8,128)} %broadcast_in_dim.12), calls=%async_computation.1 | async-start | bytes 524288 | tf_op jit(solution)/shard_map/all_to_all | solution.py:361
  88.2 0.0 copy-done.3
  88.2 0.1 copy.28
  88.4 0.1 fusion.2
  88.5 0.1 fusion.1
  88.6 0.8 concatenate.3.start
  89.4 14.3 %all-to-all-done.1 = f32[64,8,128]{2,1,0:T(8,128)S(1)} async-done(((f32[64,8,128]{2,1,0:T(8,128)}), f32[64,8,128]{2,1,0:T(8,128)S(1)}, u32[]{:S(2)}, u32[]{:S(2)}) %all-to-all-start.1) | async-done | bytes 262176 | tf_op jit(solution)/shard_map/all_to_all | solution.py:361
  103.7 0.0 copy-start.2
  103.7 0.7 copy-done.2
  104.4 17.5 %iterate.1.mine = f32[128,384]{1,0:T(8,128)} custom-call(f32[512,128]{1,0:T(8,128)} %bitcast.26, f32[128,384]{1,0:T(8,128)} %concatenate.3.start), custom_call_target="tpu_custom_call" | custom-call | flops 2000000000 | bytes 1000000 | tf_op jit(solution)/shard_map/iterate/pallas_call | solution.py:233
  121.9 1.7 %collective-permute-start.4 = (f32[128,384]{1,0:T(8,128)}, f32[128,384]{1,0:T(8,128)S(1)}, u32[]{:S(2)}, u32[]{:S(2)}) collective-permute-start(f32[128,384]{1,0:T(8,128)} %iterate.1.mine), channel_id=1, source_target_pairs={{0,2},{2,0},{1,3},{3,1},{4,6},{6,4},{5,7},{7,5},{8,10},{10,8},{9,1... | collective-permute-start | bytes 589832 | tf_op jit(solution)/shard_map/ppermute | solution.py:365
  123.6 0.0 collective-permute-done.5
  123.6 1.5 %copy.31.far = bf16[2,150,2048]{2,1,0:T(8,128)(2,1)} copy(bf16[2,150,2048]{2,0,1:T(2,128)(2,1)S(1)} %collective-permute-done.5) | data formatting | bytes 2457600 | tf_op jit(solution)/shard_map/ppermute | solution.py:354
  125.1 0.0 collective-permute-done.4.other
  125.2 0.0 copy-start.4
  125.2 0.7 copy-done.4
  125.8 11.6 %finish.1 = (f32[2,4096]{1,0:T(2,128)}, f32[2,300,128]{2,1,0:T(8,128)}) custom-call(s32[2]{0:T(128)} %pad_add_fusion.place, s32[2]{0:T(128)} %low.1, s32[2]{0:T(128)} %high.1, f32[128,384]{1,0:T(8,128)} %iterate.1.mine, f32[128,384]{1,0:T(8,128)} %copy-done.4, bf16[2,2,150,4096]{3,2,1,0:T(8,128)(2,1)} %bitcast.20, bf16[2,150,4096]{2,1,0:T(8,128)(2,1)} %bitcast.23, ...), custom_call_target="tpu_custom_call" | custom-call | flops 7000000000 | bytes 10000000 | tf_op jit(solution)/shard_map/finish/pallas_call | solution.py:294
  137.4 1.8 %copy.32 = f32[2,300,128]{2,0,1:T(2,128)} copy(f32[2,300,128]{2,1,0:T(8,128)} %get-tuple-element.19) | data formatting | bytes 614400 | tf_op jit(solution)/shard_map/finish/pallas_call | solution.py:294
  (2 shorter events, 0.0 us)
Async XLA Ops:
  0.6 5.1 %copy-start.1 = (bf16[150,2,4096]{2,1,0:T(2,128)(2,1)S(1)}, bf16[150,2,4096]{2,1,0:T(2,128)(2,1)}, u32[]{:S(2)}) copy-start(bf16[150,2,4096]{2,1,0:T(2,128)(2,1)} %param.6) | copy-start | bytes 7372804
  4.9 29.1 %collective-permute-start = (bf16[2,150,2048]{2,0,1:T(2,128)(2,1)}, bf16[2,150,2048]{2,0,1:T(2,128)(2,1)}, u32[]{:S(2)}, u32[]{:S(2)}) collective-permute-start(bf16[2,150,2048]{2,0,1:T(2,128)(2,1)} %fusion), channel_id=1, source_target_pairs={{0,1},{1,0},{2,3},{3,2},{4,5},{5,4},{6,7},{7,6},{8,9},{9,8},{10,11... | collective-permute-start | bytes 3686408 | tf_op jit(solution)/shard_map/ppermute | solution.py:349
  5.7 3.1 %copy-start = (bf16[300,2,4096]{2,1,0:T(2,128)(2,1)S(1)}, bf16[300,2,4096]{2,1,0:T(2,128)(2,1)}, u32[]{:S(2)}) copy-start(bf16[300,2,4096]{2,1,0:T(2,128)(2,1)} %param.5) | copy-start | bytes 14745604
  41.3 3.5 %collective-permute-start.1 = (f32[512,128]{1,0:T(8,128)}, f32[512,128]{1,0:T(8,128)S(1)}, u32[]{:S(2)}, u32[]{:S(2)}) collective-permute-start(f32[512,128]{1,0:T(8,128)} %get-tuple-element.12), channel_id=1, source_target_pairs={{0,2},{2,0},{1,3},{3,1},{4,6},{6,4},{5,7},{7,5},{8,10},{10,8},{9,1... | collective-permute-start | bytes 786440 | tf_op jit(solution)/shard_map/ppermute | solution.py:355
  41.3 9.1 %collective-permute-start.3 = (f32[512,128]{1,0:T(8,128)}, f32[512,128]{1,0:T(8,128)S(1)}, u32[]{:S(2)}, u32[]{:S(2)}) collective-permute-start(f32[512,128]{1,0:T(8,128)} %get-tuple-element.13), channel_id=1, source_target_pairs={{1,2},{5,6},{9,10},{13,14},{17,18},{21,22},{25,26},{29,30},{33,34}... | collective-permute-start | bytes 786440 | tf_op jit(solution)/shard_map/ppermute | solution.py:357
  44.2 6.3 %collective-permute-start.2 = (f32[512,128]{1,0:T(8,128)}, f32[512,128]{1,0:T(8,128)S(1)}, u32[]{:S(2)}, u32[]{:S(2)}) collective-permute-start(f32[512,128]{1,0:T(8,128)} %get-tuple-element.13), channel_id=1, source_target_pairs={{3,2},{7,6},{11,10},{15,14},{19,18},{23,22},{27,26},{31,30},{35,34... | collective-permute-start | bytes 786440 | tf_op jit(solution)/shard_map/ppermute | solution.py:356
  52.2 26.9 %all-to-all-start = ((f32[64,8,128]{2,1,0:T(8,128)}), f32[64,8,128]{2,1,0:T(8,128)S(1)}, u32[]{:S(2)}, u32[]{:S(2)}) async-start(f32[64,8,128]{2,1,0:T(8,128)} %add_bitcast_fusion), calls=%async_computation | async-start | bytes 524288 | tf_op jit(solution)/shard_map/all_to_all | solution.py:359
  68.3 19.9 %copy-start.3 = (f32[300,128]{1,0:T(8,128)S(1)}, f32[300,128]{1,0:T(8,128)}, u32[]{:S(2)}) copy-start(f32[300,128]{1,0:T(8,128)} %param.7) | copy-start | bytes 460804
  69.6 54.0 %collective-permute-start.5 = (bf16[2,150,2048]{2,0,1:T(2,128)(2,1)S(1)}, bf16[2,150,2048]{2,0,1:T(2,128)(2,1)S(1)}, u32[]{:S(2)}, u32[]{:S(2)}) collective-permute-start(bf16[2,150,2048]{2,0,1:T(2,128)(2,1)S(1)} %copy.29), channel_id=1, source_target_pairs={{1,0},{3,2},{5,4},{7,6},{9,8},{11,10},{13,12},{15,14},{17,16},{19,... | collective-permute-start | bytes 3686408 | tf_op jit(solution)/shard_map/ppermute | solution.py:354
  79.9 23.9 %all-to-all-start.1 = ((f32[64,8,128]{2,1,0:T(8,128)}), f32[64,8,128]{2,1,0:T(8,128)S(1)}, u32[]{:S(2)}, u32[]{:S(2)}) async-start(f32[64,8,128]{2,1,0:T(8,128)} %broadcast_in_dim.12), calls=%async_computation.1 | async-start | bytes 524288 | tf_op jit(solution)/shard_map/all_to_all | solution.py:361
  103.7 0.7 copy-start.2
  121.9 3.2 %collective-permute-start.4 = (f32[128,384]{1,0:T(8,128)}, f32[128,384]{1,0:T(8,128)S(1)}, u32[]{:S(2)}, u32[]{:S(2)}) collective-permute-start(f32[128,384]{1,0:T(8,128)} %iterate.1.mine), channel_id=1, source_target_pairs={{0,2},{2,0},{1,3},{3,1},{4,6},{6,4},{5,7},{7,5},{8,10},{10,8},{9,1... | collective-permute-start | bytes 589832 | tf_op jit(solution)/shard_map/ppermute | solution.py:365
  125.2 0.7 copy-start.4

commit v2 on v1

v2 whole, which is shorter than its diff:
```python
import functools

import jax
import jax.numpy as jnp
from jax import lax
from jax.experimental import pallas as pl
from jax.experimental.pallas import tpu as pltpu
from jax.sharding import Mesh
from jax.sharding import PartitionSpec as P

K = 128
ITERS = 3
WINDOW = 300
HALF = 150
MAIN = 128
REM = HALF - MAIN
SPAN = 384
USED = 320
TILE = 32
PACKED = 512
EXTRA = 288
LATE = 184
CHUNK = 512
LIMIT = 20 * 2**20
HI = lax.Precision.HIGHEST
F32 = jnp.float32
BF16 = jnp.bfloat16
PIX = ("pix_0", "pix_1", "pix_2", "pix_3")
CHIPS = ("pix_0", "pix_1", "pix_2")
SMEM = pl.BlockSpec(memory_space=pltpu.SMEM)
VMEM = pl.BlockSpec(memory_space=pltpu.VMEM)


def grid_of(shape, axis):
    return lax.broadcasted_iota(jnp.int32, shape, axis)


def across(a, b):
    return lax.dot_general(a, b, (((1,), (1,)), ((), ())), preferred_element_type=F32)


def parameters():
    return pltpu.CompilerParams(vmem_limit_bytes=LIMIT)


def pick_kernel(place, source, out, done):
    first = 1 - place[1]
    width = out.shape[-1]
    copy = pltpu.make_async_copy(
        source.at[
            pl.ds(first * HALF, HALF), :, pl.ds(pl.multiple_of(first * width, 128), width)
        ],
        out,
        done,
    )
    copy.start()
    copy.wait()


def picked(place, iq):
    half = iq.shape[-1] // 2
    return pl.pallas_call(
        pick_kernel,
        out_shape=jax.ShapeDtypeStruct((HALF, 2, half), iq.dtype),
        in_specs=[SMEM, pl.BlockSpec(memory_space=pltpu.HBM)],
        out_specs=VMEM,
        scratch_shapes=[pltpu.SemaphoreType.DMA],
        name="picked",
    )(place, iq)


def lower_and_diagonal(block):
    row = grid_of((MAIN, 128), 0)
    lane = grid_of((MAIN, 128), 1)
    diagonal = jnp.where(
        grid_of((8, 128), 0) == 0,
        jnp.sum(jnp.where(lane == row, block, 0.0), axis=0, keepdims=True),
        0.0,
    )
    return jnp.where(lane < row, block, 0.0), diagonal


def packed_rows(first, cross, second):
    row = grid_of((MAIN, 128), 0)
    lane = grid_of((MAIN, 128), 1)
    lower, diagonal = lower_and_diagonal(second[0:MAIN, 0:128])
    corner = jnp.where(lane >= row, first[0:MAIN, 0:128], lower)
    side = (
        first[0:152, 128:256]
        + pltpu.roll(cross[0:152, 128:256], 32, 1)
        + pltpu.roll(second[0:152, 128:256], 64, 1)
    )
    return corner, cross[0:152, 0:128], side, diagonal


def local_kernel(place, frames, tail, keep, swap, extra, mine, sums):
    sums[...] = jnp.zeros_like(sums)
    width = 1024
    half = mine.shape[-1]
    part_of = pl.ds(pl.multiple_of(place[1] * half, 128), half)
    for part in range(2):
        mine[part] = frames[part, 1 - place[1], :, part_of]

    def step(i, carry):
        at = pl.ds(pl.multiple_of(i * width, 128), width)
        for part in range(2):
            a = frames[part, 0, :, at]
            b = frames[part, 1, :, at]
            c = tail[part, :, at]
            for index, (left, right) in enumerate(((a, a), (a, b), (b, b), (b, c), (c, c))):
                sums[index, 0:HALF, 0:HALF] += across(left, right)
        return carry

    lax.fori_loop(0, frames.shape[-1] // width, step, 0)
    core = place[0] == 1
    scale = place[1].astype(F32)
    even = packed_rows(sums[0], sums[1], sums[2])
    odd = packed_rows(sums[2], sums[3] * scale, sums[4] * scale)
    at = 0
    for one, two in zip(even, odd):
        rows = one.shape[0]
        keep[at : at + rows] = jnp.where(core, two, one)
        swap[at : at + rows] = jnp.where(core, one, two)
        at += rows
    keep[440:] = jnp.zeros((PACKED - 440, 128), F32)
    swap[440:] = jnp.zeros((PACKED - 440, 128), F32)
    lower, diagonal = lower_and_diagonal(sums[0, 0:MAIN, 0:128])
    extra[0:MAIN] = lower
    extra[MAIN : MAIN + 152] = pltpu.roll(sums[0, 0:152, 128:256], 64, 1)
    extra[MAIN + 152 : EXTRA] = diagonal


def local_products(place, frames, tail):
    shape = jax.ShapeDtypeStruct((PACKED, 128), F32)
    return pl.pallas_call(
        local_kernel,
        out_shape=(
            shape,
            shape,
            jax.ShapeDtypeStruct((EXTRA, 128), F32),
            jax.ShapeDtypeStruct((2, HALF, frames.shape[-1] // 2), BF16),
        ),
        in_specs=[SMEM, VMEM, VMEM],
        out_specs=(VMEM, VMEM, VMEM, VMEM),
        scratch_shapes=[pltpu.VMEM((5, 152, 256), F32)],
        cost_estimate=pl.CostEstimate(flops=4 * 10**9, bytes_accessed=8 * 10**6, transcendentals=0),
        compiler_params=parameters(),
        name="local_products",
    )(place, frames, tail)


def cross_kernel(place, own, arrived, late, sums):
    total = jnp.zeros((HALF, HALF), F32)
    for part in range(2):
        total += across(own[part], arrived[part])
    sums[...] = jnp.zeros_like(sums)
    sums[0:HALF, 0:HALF] = total

    @pl.when(place[1] == 1)
    def _():
        sums[0:256] = sums[...].T

    late[0:152] = sums[0:152, 0:128]
    side = jnp.zeros((32, 128), F32)
    for g in range(5):
        rows = sums[32 * g : 32 * g + 32, 128:256]
        side += pltpu.roll(rows, 24 * g, 1) if g else rows
    late[152:LATE] = side


def cross_products(place, own, arrived):
    return pl.pallas_call(
        cross_kernel,
        out_shape=jax.ShapeDtypeStruct((LATE, 128), F32),
        in_specs=[SMEM, VMEM, VMEM],
        out_specs=VMEM,
        scratch_shapes=[pltpu.VMEM((256, 256), F32)],
        cost_estimate=pl.CostEstimate(flops=4 * 10**8, bytes_accessed=3 * 10**6, transcendentals=0),
        compiler_params=parameters(),
        name="cross_products",
    )(place, own, arrived)


def merge_kernel(place, keep, swapped, extra_one, extra_two, own, one, two, three, out):
    out[...] = keep[...] + swapped[...]
    extra = extra_one[...] + extra_two[...]
    out[0:MAIN] += extra[0:MAIN]
    out[280:440] += extra[MAIN:EXTRA]

    @pl.when((place[0] == 1) & (place[1] == 0))
    def _():
        late = own[...] + one[...] + two[...] + three[...]
        out[128:280] += late[0:152]
        lane = grid_of((32, 128), 1)
        valid = (lane >= 32) & (lane < 56)
        for g in range(5):
            rows = 24 if g == 4 else 32
            moved = jnp.where(valid, pltpu.roll(late[152:LATE], (32 - 24 * g) % 128, 1), 0.0)
            out[280 + 32 * g : 280 + 32 * g + rows] += moved[0:rows]


def merged(place, *parts):
    return pl.pallas_call(
        merge_kernel,
        out_shape=jax.ShapeDtypeStruct((PACKED, 128), F32),
        in_specs=[SMEM] + [VMEM] * len(parts),
        out_specs=VMEM,
        compiler_params=parameters(),
        name="merged",
    )(place, *parts)


def unpack(rows, gram):
    row = grid_of((128, 128), 0)
    lane = grid_of((128, 128), 1)
    both = rows[0:128]
    turned = both.T
    gram[0:128, 0:128] = jnp.where(lane >= row, both, turned)
    gram[128:256, 128:256] = jnp.where(
        lane < row, both, jnp.where(lane == row, rows[432:433], turned)
    )
    cross = rows[128:256]
    gram[0:128, 128:256] = cross
    gram[128:256, 0:128] = cross.T
    side = rows[280:408]
    turn = jnp.concatenate([rows[256:280], jnp.zeros((104, 128), F32)], axis=0).T
    first = jnp.where(lane < 64, side, 0.0)
    second = jnp.where(lane < 32, turn, jnp.where(lane < 64, pltpu.roll(side, 96, 1), 0.0))
    gram[0:128, 256:384] = first
    gram[128:256, 256:384] = second
    gram[256:384, 0:128] = first.T
    gram[256:384, 128:256] = second.T
    corner = rows[408:432]
    gram[256:384, 256:384] = jnp.zeros((128, 128), F32)
    short = grid_of((24, 128), 1)
    gram[256:280, 256:384] = jnp.where(short < 64, corner, 0.0)
    moved = pltpu.roll(corner, 96, 1)
    square = jnp.concatenate(
        [jnp.where(short < 32, moved, 0.0), jnp.zeros((104, 128), F32)], axis=0
    ).T[0:24]
    gram[288:312, 256:384] = jnp.where(
        short < 32, square, jnp.where(short < 64, moved, 0.0)
    )


def row_of(vector, index):
    return jnp.broadcast_to(vector[index : index + 1, :], vector.shape)


def eliminate(work, step):
    first = TILE * step
    sub = grid_of((8, 128), 0)
    lane = grid_of((8, 128), 1)
    groups = TILE // 8
    cols = {}
    for g in range(groups):
        top = first + 8 * g
        block = work[top : top + 8, 0:128]
        for k in range(8 * (g + 1)):
            at = first + k
            cols[g, k] = jnp.broadcast_to(block[:, at : at + 1], (8, 128))
    inverse = [jnp.where(lane == sub + 8 * g, 1.0, 0.0).astype(F32) for g in range(groups)]
    for j in range(TILE):
        gj, rj = divmod(j, 8)
        scale = lax.rsqrt(row_of(cols[gj, j], rj))
        for g in range(gj, groups):
            cols[g, j] = cols[g, j] * scale
        for k in range(j + 1, TILE):
            gk, rk = divmod(k, 8)
            factor = row_of(cols[gk, j], rk)
            for g in range(gk, groups):
                cols[g, k] = cols[g, k] - cols[g, j] * factor
        pivot = row_of(inverse[gj], rj) * scale
        for g in range(gj, groups):
            if g == gj:
                below = jnp.where(sub > rj, cols[g, j], 0.0)
                inverse[g] = jnp.where(sub == rj, pivot, inverse[g] - below * pivot)
            else:
                inverse[g] = inverse[g] - cols[g, j] * pivot
    lhs = jnp.concatenate(inverse, axis=0)[:, 0:TILE]
    rows = jnp.dot(
        lhs, work[first : first + TILE, :], precision=HI, preferred_element_type=F32
    )
    work[first : first + TILE, :] = rows
    if first + TILE < K:
        change = lax.dot_general(
            rows[:, 0:128], rows, (((0,), (0,)), ((), ())), precision=HI,
            preferred_element_type=F32,
        )
        work[first + TILE :, :] = work[first + TILE :, :] - change[first + TILE :, :]


def iterate_kernel(packed, start, basis, gram, work):
    unpack(packed[...], gram)
    work[:, K:] = start[...]

    def step(_, carry):
        image = jnp.dot(work[:, K:], gram[...], precision=HI, preferred_element_type=F32)
        work[:, 0:K] = lax.dot_general(
            image, image, (((1,), (1,)), ((), ())), precision=HI, preferred_element_type=F32
        )
        work[:, K:] = image
        for index in range(K // TILE):
            eliminate(work, index)
        return carry

    lax.fori_loop(0, ITERS, step, 0)
    basis[...] = work[:, K:]


def iterate(packed, start):
    return pl.pallas_call(
        iterate_kernel,
        out_shape=jax.ShapeDtypeStruct((K, SPAN), F32),
        in_specs=[VMEM, VMEM],
        out_specs=VMEM,
        scratch_shapes=[pltpu.VMEM((SPAN, SPAN), F32), pltpu.VMEM((K, K + SPAN), F32)],
        cost_estimate=pl.CostEstimate(flops=2 * 10**9, bytes_accessed=10**6, transcendentals=0),
        compiler_params=pltpu.CompilerParams(vmem_limit_bytes=LIMIT),
        name="iterate",
    )(packed, start)


def projection(rows, low, high):
    used = rows[:, 0:USED]
    index = grid_of((K, USED), 0)
    kept = jnp.where((index >= low) & (index < high), used, 0.0)
    return lax.dot_general(
        kept, used, (((0,), (0,)), ((), ())), precision=HI, preferred_element_type=F32
    ).astype(BF16)


def powers(proj, chunk, power, first, second, begin, pixels):
    def step(i, carry):
        at = i * CHUNK
        total = jnp.zeros((1, CHUNK), F32)
        for part in range(2):
            for side, (ref, index, offset) in enumerate((first, second)):
                where = pl.ds(pl.multiple_of(offset + at, 128), CHUNK)
                block = ref[part, :, where] if index is None else ref[part, index, :, where]
                chunk[part, 128 * side : 128 * side + MAIN, :] = block[0:MAIN]
                chunk[part, 256 + 32 * side : 256 + 32 * side + REM, :] = block[MAIN:HALF]
            out = jnp.dot(proj[...], chunk[part], preferred_element_type=F32)
            total += jnp.sum(out * out, axis=0, keepdims=True)
        power[:, pl.ds(pl.multiple_of(begin + at, 128), CHUNK)] = total / WINDOW
        return carry

    lax.fori_loop(0, pixels // CHUNK, step, 0, unroll=2)


def whole_window(place, proj, chunk, power, frames, tail, odd):
    pixels = frames.shape[-1]

    @pl.when(jnp.logical_not(odd))
    def _():
        powers(proj, chunk, power, (frames, 0, 0), (frames, 1, 0), 0, pixels)

    @pl.when(odd & (place[1] == 1))
    def _():
        powers(proj, chunk, power, (frames, 1, 0), (tail, None, 0), 0, pixels)


def own_kernel(place, low, high, mine, frames, tail, power, proj, chunk):
    chunk[...] = jnp.zeros_like(chunk)
    which = place[0]
    proj[...] = projection(mine[...], low[which], high[which])
    whole_window(place, proj, chunk, power, frames, tail, which == 1)


def shared_kernel(place, low, high, mine, other, one, two, frames, near, power, proj, chunk):
    chunk[...] = jnp.zeros_like(chunk)
    pixels = near.shape[-1]
    last = place[1] == 1
    found = jnp.where(
        last, one[...] + two[...], jnp.where(place[0] == 1, mine[...], other[...])
    )
    proj[...] = projection(found, low[2], high[2])

    @pl.when(last)
    def _():
        powers(proj, chunk, power, (near, None, 0), (frames, 0, pixels), 0, pixels)

    @pl.when(jnp.logical_not(last))
    def _():
        powers(proj, chunk, power, (frames, 1, 0), (near, None, 0), 0, pixels)


def other_kernel(place, low, high, mine, other, frames, tail, power, basis, proj, chunk):
    chunk[...] = jnp.zeros_like(chunk)
    which = 1 - place[0]
    proj[...] = projection(other[...], low[which], high[which])
    whole_window(place, proj, chunk, power, frames, tail, which == 1)
    core = place[0] == 1
    for window in range(2):
        own = core if window else jnp.logical_not(core)
        rows = jnp.where(own, mine[...], other[...])
        ends = rows[:, 256:384].T
        basis[0:MAIN, window, :] = rows[:, 0:128].T
        basis[MAIN:HALF, window, :] = ends[0:REM]
        basis[HALF : HALF + MAIN, window, :] = rows[:, 128:256].T
        basis[HALF + MAIN : WINDOW, window, :] = ends[32 : 32 + REM]


def power_call(kernel, name, pixels, flops, with_basis, *arrays):
    shape = jax.ShapeDtypeStruct((1, pixels), F32)
    return pl.pallas_call(
        kernel,
        out_shape=(shape, jax.ShapeDtypeStruct((WINDOW, 2, K), F32)) if with_basis else shape,
        in_specs=[SMEM] * 3 + [VMEM] * (len(arrays) - 3),
        out_specs=(VMEM, VMEM) if with_basis else VMEM,
        scratch_shapes=[pltpu.VMEM((USED, USED), BF16), pltpu.VMEM((2, USED, CHUNK), BF16)],
        cost_estimate=pl.CostEstimate(flops=flops, bytes_accessed=10**7, transcendentals=0),
        compiler_params=parameters(),
        name=name,
    )(*arrays)


def in_lanes(start):
    rows = start.T
    gap = jnp.zeros((K, 32 - REM), F32)
    rest = jnp.zeros((K, 64), F32)
    return jnp.concatenate(
        [
            rows[:, 0:MAIN],
            rows[:, HALF : HALF + MAIN],
            rows[:, MAIN:HALF],
            gap,
            rows[:, HALF + MAIN :],
            gap,
            rest,
        ],
        axis=1,
    )


def body(iq, tail_frames, start_basis, low_rank, high_rank):
    pixels = iq.shape[-1]
    half = pixels // 2
    core = lax.axis_index("pix_3")
    block = lax.axis_index("tm")
    place = jnp.stack([core, block]).astype(jnp.int32)
    chips = lax.axis_size(CHIPS)
    pair = ("pix_3", "tm")

    near = lax.ppermute(picked(place, iq), "tm", [(0, 1), (1, 0)])
    frames = jnp.transpose(iq.reshape(2, HALF, 2, pixels), (2, 0, 1, 3))
    tail = jnp.swapaxes(tail_frames, 0, 1)
    keep, swap, extra, own_half = local_products(place, frames, tail)
    swapped = lax.ppermute(swap, "pix_3", [(0, 1), (1, 0)])
    extra_one = lax.ppermute(extra, pair, [(3, 2)])
    extra_two = lax.ppermute(extra, pair, [(1, 2)])
    near = jnp.swapaxes(near, 0, 1)
    late = cross_products(place, own_half, near)
    one = lax.ppermute(late, pair, [(3, 2)])
    two = lax.ppermute(late, pair, [(1, 2)])
    three = lax.ppermute(late, pair, [(0, 2)])
    mine = merged(place, keep, swapped, extra_one, extra_two, late, one, two, three)
    pieces = lax.all_to_all(mine.reshape(chips, PACKED // chips, 128), CHIPS, 0, 0, tiled=True)
    piece = pieces.sum(axis=0)
    packed = lax.all_to_all(
        jnp.broadcast_to(piece[None], pieces.shape), CHIPS, 0, 0, tiled=True
    ).reshape(PACKED, 128)
    found = iterate(packed, in_lanes(start_basis))
    one = lax.ppermute(found, pair, [(2, 3)])
    two = lax.ppermute(found, pair, [(2, 1)])
    other = lax.ppermute(found, "pix_3", [(0, 1), (1, 0)])
    lows = jnp.concatenate([low_rank, lax.ppermute(low_rank[1:], "tm", [(0, 1)])])
    highs = jnp.concatenate([high_rank, lax.ppermute(high_rank[1:], "tm", [(0, 1)])])
    lows = jnp.where(block == 0, jnp.concatenate([low_rank, low_rank[1:]]), lows)
    highs = jnp.where(block == 0, jnp.concatenate([high_rank, high_rank[1:]]), highs)
    flops = 3 * 10**9
    own = power_call(
        own_kernel, "own", pixels, flops, False, place, lows, highs, found, frames, tail
    )
    shared = power_call(
        shared_kernel, "shared", half, flops // 2, False,
        place, lows, highs, found, other, one, two, frames, near,
    )
    back = lax.ppermute(shared, "tm", [(1, 0)])
    rest, basis = power_call(
        other_kernel, "other", pixels, flops, True,
        place, lows, highs, found, other, frames, tail,
    )
    even = jnp.where(core == 0, own, rest)
    odd = jnp.where(core == 0, rest, own)
    odd = jnp.where(block == 0, jnp.concatenate([shared, back], axis=1), odd)
    return jnp.concatenate([even, odd], axis=0), jnp.swapaxes(basis, 0, 1)


def solution(mesh):
    torus = Mesh(
        mesh.devices.reshape(2, 8, 4, 2, mesh.shape["tm"]),
        ("pix_0", "pix_1", "pix_2", "pix_3", "tm"),
    )
    return jax.shard_map(
        body,
        mesh=torus,
        in_specs=(P("tm", None, PIX), P(None, None, PIX), P(), P("tm"), P("tm")),
        out_specs=(P("tm", PIX), P("tm", None, None)),
        check_vma=False,
    )
```

time: 142 us -> 130 us (0.915)
  waiting for transfers between devices: 39.5 us -> 27.3 us
  starting transfers between devices: 30.5 us -> 41 us
  local copies, waits for them, and re-layouts: 21 us -> 14.7 us
  other arithmetic: 6.67 us -> 4.11 us
    ppermute x4 -> x11, starting transfers between devices: 5.72 us -> 17.7 us  [the longest x1 5.28 us: body(): back = lax.ppermute(shared, 'tm', [(1, 0)])]
    ppermute x4 -> x11, waiting for transfers between devices: 17.1 us -> 10.7 us  [the longest x1 9.02 us: body(): near = lax.ppermute(picked(place, iq), 'tm', [(0, 1), (1, 0)])]
    all_to_all x1, waiting for transfers between devices: 14.3 us -> 8.48 us  [body(): lax.all_to_all(jnp.broadcast_to(piece[None], pieces.shape), CHIPS, 0, 0,...]
    transpose x1 -> x0, other arithmetic: 4.22 us -> none  [body(): near = lax.ppermute(jnp.swapaxes(sent, 0, 1), 'tm', [(0, 1), (1, 0)])]
    ppermute x2 -> x1, local copies, waits for them, and re-layouts: 4.41 us -> 0.45 us  [body(): near = lax.ppermute(picked(place, iq), 'tm', [(0, 1), (1, 0)])]
    select_n x0 -> x3, other arithmetic: none -> 2.81 us  [the longest x1 1.39 us: body(): jnp.where(block == 0, jnp.concatenate([low_rank, low_rank[1:]]), lows)]
    squeeze x2 -> x0, local copies, waits for them, and re-layouts: 2.69 us -> none  [body(): far = lax.ppermute(frames[:, 0, :, half:], 'tm', [(1, 0)])]
    pallas_call x1 -> x0, local copies, waits for them, and re-layouts: 1.84 us -> none  [finish(): pl.pallas_call(finish_kernel, grid=(steps,), out_shape=(jax.ShapeDtypeStr...]
  transfers between devices with their start and end apart: 8 -> 15, of which waited for: 4 -> 4; matrix products, arithmetic and copies ran while one was open for 11% -> 12% of each run, Pallas kernels for 18% -> 13%
where the time goes in v2:
time: 130 us; the launch traced here: 128 us
  starting transfers between devices  41 us (32%)
  Pallas kernels  39.8 us (31%)
  waiting for transfers between devices  27.3 us (21%)
  local copies, waits for them, and re-layouts  14.7 us (11%)
  other arithmetic  4.11 us (3%)
    pallas_call x1, Pallas kernels, iterate(): pl.pallas_call(iterate_kernel, out_shape=jax.ShapeDtypeStruct((K, SPAN),...  15.8 us
    all_to_all x1, starting transfers between devices, body(): lax.all_to_all(mine.reshape(chips, PACKED // chips, 128), CHIPS, 0, 0, ti...  14.7 us
    pallas_call x3, Pallas kernels, power_call(): pl.pallas_call(kernel, out_shape=(shape, jax.ShapeDtypeStruct((WINDOW, 2,...  13.4 us
    ppermute x1, waiting for transfers between devices, body(): near = lax.ppermute(picked(place, iq), 'tm', [(0, 1), (1, 0)])  9.02 us
    all_to_all x1, waiting for transfers between devices, body(): lax.all_to_all(jnp.broadcast_to(piece[None], pieces.shape), CHIPS, 0, 0,...  8.48 us
    all_to_all x1, starting transfers between devices, body(): lax.all_to_all(jnp.broadcast_to(piece[None], pieces.shape), CHIPS, 0, 0,...  8.37 us
    all_to_all x1, waiting for transfers between devices, body(): lax.all_to_all(mine.reshape(chips, PACKED // chips, 128), CHIPS, 0, 0, ti...  8.14 us
    reshape x1, local copies, waits for them, and re-layouts, body(): frames = jnp.transpose(iq.reshape(2, HALF, 2, pixels), (2, 0, 1, 3))  6.81 us
  transfers between devices with their start and end apart: 15, of which 4 were waited for; matrix products, arithmetic and copies ran while one was open for 12% of the time, Pallas kernels for 13%

profile of v2, /device:TPU:6, one launch (start us, length us, event | category | flops | bytes accessed | tf_op | source)
XLA Modules:
  0.0 128.0 jit_solution(5239632977622516113)
XLA Ops:
  0.6 0.6 pad_add_fusion.place
  1.2 3.1 %picked.1 = bf16[150,2,2048]{2,1,0:T(2,128)(2,1)} custom-call(s32[2]{0:T(128)} %pad_add_fusion.place, bf16[300,2,4096]{2,1,0:T(2,128)(2,1)} %source.1), custom_call_target="tpu_custom_call" | custom-call | tf_op jit(solution)/shard_map/picked/pallas_call | solution.py:62
  4.3 0.9 collective-permute-start.5
  5.2 3.3 %copy.24 = bf16[150,2,4096]{2,0,1:T(8,128)(2,1)S(1)} copy(bf16[150,2,4096]{2,1,0:T(2,128)(2,1)} %param.6) | data formatting | bytes 4915200 | tf_op args[1]
  8.5 0.0 copy-start.2
  8.5 0.0 copy-start.4
  8.5 6.8 %copy.23 = bf16[2,150,2,4096]{3,1,0,2:T(8,128)(2,1)S(1)} copy(bf16[2,150,2,4096]{3,2,1,0:T(2,128)(2,1)} %bitcast.26) | data formatting | bytes 9830400 | tf_op jit(solution)/shard_map/reshape | solution.py:446
  15.3 0.0 copy-start
  15.3 0.0 copy-done.2
  15.3 0.0 copy-done.4
  15.4 5.0 %local_products.1 = (f32[512,128]{1,0:T(8,128)S(1)}, f32[512,128]{1,0:T(8,128)S(1)}, f32[288,128]{1,0:T(8,128)S(1)}, bf16[2,150,2048]{2,1,0:T(8,128)(2,1)S(1)}) custom-call(s32[2]{0:T(128)S(1)} %copy-done.4, bf16[2,2,150,4096]{3,2,1,0:T(8,128)(2,1)S(1)} %bitcast.16, bf16[2,150,4096]{2,1,0:T(8,128)(2,1)S(1)} %bitcast.22), custom_call_target="tpu_custom_call" | custom-call | flops 4000000000 | bytes 8000000 | tf_op jit(solution)/shard_map/local_products/pallas_call | solution.py:135
  20.4 0.1 collective-permute-start.2
  20.5 3.2 %collective-permute-start.4 = (f32[288,128]{1,0:T(8,128)S(1)}, f32[288,128]{1,0:T(8,128)S(1)}, u32[]{:S(2)}, u32[]{:S(2)}) collective-permute-start(f32[288,128]{1,0:T(8,128)S(1)} %get-tuple-element.10), channel_id=1, source_target_pairs={{1,2},{5,6},{9,10},{13,14},{17,18},{21,22},{25,26},{29,30},{33,34}... | collective-permute-start | bytes 442376 | tf_op jit(solution)/shard_map/ppermute | solution.py:451
  23.7 0.7 collective-permute-start.3
  24.4 9.0 %collective-permute-done.5 = bf16[150,2,2048]{2,1,0:T(2,128)(2,1)S(1)} collective-permute-done((bf16[150,2,2048]{2,1,0:T(2,128)(2,1)}, bf16[150,2,2048]{2,1,0:T(2,128)(2,1)S(1)}, u32[]{:S(2)}, u32[]{:S(2)}) %collective-permute-start.5) | collective-permute-done | bytes 1228832 | tf_op jit(solution)/shard_map/ppermute | solution.py:445
  33.4 0.5 copy.25
  33.8 0.0 copy-start.6
  33.8 0.0 copy-start.7
  33.9 0.0 copy-start.5
  33.9 1.3 cross_products.1.own
  35.1 0.7 collective-permute-start.8
  35.8 1.8 %collective-permute-start.7 = (f32[184,128]{1,0:T(8,128)S(1)}, f32[184,128]{1,0:T(8,128)S(1)}, u32[]{:S(2)}, u32[]{:S(2)}) collective-permute-start(f32[184,128]{1,0:T(8,128)S(1)} %cross_products.1.own), channel_id=1, source_target_pairs={{1,2},{5,6},{9,10},{13,14},{17,18},{21,22},{25,26},{29,30},{33,34}... | collective-permute-start | bytes 282632 | tf_op jit(solution)/shard_map/ppermute | solution.py:455
  37.6 0.0 collective-permute-done.4.extra_two
  37.6 0.7 collective-permute-start.6
  38.3 0.0 collective-permute-done.3.extra_one
  38.3 0.0 collective-permute-done.2.swapped
  38.3 0.0 collective-permute-done.8.three
  38.4 1.6 %collective-permute-done.7.two = f32[184,128]{1,0:T(8,128)S(1)} collective-permute-done((f32[184,128]{1,0:T(8,128)S(1)}, f32[184,128]{1,0:T(8,128)S(1)}, u32[]{:S(2)}, u32[]{:S(2)}) %collective-permute-start.7) | collective-permute-done | bytes 94240 | tf_op jit(solution)/shard_map/ppermute | solution.py:455
  40.0 0.0 collective-permute-done.6.one
  40.0 1.3 %merged.1 = f32[512,128]{1,0:T(8,128)} custom-call(s32[2]{0:T(128)S(1)} %copy-done.4, f32[512,128]{1,0:T(8,128)S(1)} %get-tuple-element.8.keep, f32[512,128]{1,0:T(8,128)S(1)} %collective-permute-done.2.swapped, f32[288,128]{1,0:T(8,128)S(1)} %collective-permute-done.3.extra_one, f32[288,128]{1,0:T(8,128)S(1)} %collective-permute-done.4.extra_two, ...), custom_call_target="tpu_custom_call" | custom-call | tf_op jit(solution)/shard_map/merged/pallas_call | solution.py:203
  41.3 14.7 %all-to-all-start = ((f32[64,8,128]{2,1,0:T(8,128)}), f32[64,8,128]{2,1,0:T(8,128)S(1)}, u32[]{:S(2)}, u32[]{:S(2)}) async-start(f32[64,8,128]{2,1,0:T(8,128)} %bitcast.6), calls=%async_computation | async-start | bytes 524288 | tf_op jit(solution)/shard_map/all_to_all | solution.py:458
  56.0 0.7 slice.20
  56.7 1.3 %collective-permute-start = (s32[1]{0:T(128)}, s32[1]{0:T(128)}, u32[]{:S(2)}, u32[]{:S(2)}) collective-permute-start(s32[1]{0:T(128)} %slice.20), channel_id=1, source_target_pairs={{0,1},{2,3},{4,5},{6,7},{8,9},{10,11},{12,13},{14,15},{16,17},{18,... | collective-permute-start | bytes 20 | tf_op jit(solution)/shard_map/ppermute | solution.py:467
  58.0 0.7 slice.21
  58.6 1.3 %collective-permute-start.1 = (s32[1]{0:T(128)}, s32[1]{0:T(128)}, u32[]{:S(2)}, u32[]{:S(2)}) collective-permute-start(s32[1]{0:T(128)} %slice.21), channel_id=1, source_target_pairs={{0,1},{2,3},{4,5},{6,7},{8,9},{10,11},{12,13},{14,15},{16,17},{18,... | collective-permute-start | bytes 20 | tf_op jit(solution)/shard_map/ppermute | solution.py:468
  59.9 0.1 copy.18
  60.0 8.1 %all-to-all-done = f32[64,8,128]{2,1,0:T(8,128)S(1)} async-done(((f32[64,8,128]{2,1,0:T(8,128)}), f32[64,8,128]{2,1,0:T(8,128)S(1)}, u32[]{:S(2)}, u32[]{:S(2)}) %all-to-all-start) | async-done | bytes 262176 | tf_op jit(solution)/shard_map/all_to_all | solution.py:458
  68.2 0.1 reduce_sum.9
  68.3 0.7 broadcast_in_dim.12
  69.0 8.4 %all-to-all-start.1 = ((f32[64,8,128]{2,1,0:T(8,128)}), f32[64,8,128]{2,1,0:T(8,128)S(1)}, u32[]{:S(2)}, u32[]{:S(2)}) async-start(f32[64,8,128]{2,1,0:T(8,128)} %broadcast_in_dim.12), calls=%async_computation.1 | async-start | bytes 524288 | tf_op jit(solution)/shard_map/all_to_all | solution.py:460
  77.4 0.1 fusion.1
  77.4 0.1 fusion
  77.6 0.1 concatenate.25.start
  77.7 0.0 collective-permute-done
  77.7 1.4 %broadcast_select_fusion.4.low = s32[3]{0:T(128)S(1)} fusion(pred[]{:T(512)S(6)} %eq.10, s32[1]{0:T(128)} %slice.20, s32[2]{0:T(128)S(1)} %copy-done.6, s32[1]{0:T(128)} %collective-permute-done), kind=kLoop, calls=%fused_computation.8 | loop fusion | flops 9 | bytes 29 | tf_op jit(solution)/shard_map/jit(_where)/select_n | solution.py:469
  79.1 0.0 collective-permute-done.1
  79.1 1.4 %broadcast_select_fusion.3.high = s32[3]{0:T(128)S(1)} fusion(pred[]{:T(512)S(6)} %eq.10, s32[1]{0:T(128)} %slice.21, s32[2]{0:T(128)S(1)} %copy-done.7, s32[1]{0:T(128)} %collective-permute-done.1), kind=kLoop, calls=%fused_computation.7 | loop fusion | flops 9 | bytes 29 | tf_op jit(solution)/shard_map/jit(_where)/select_n | solution.py:470
  80.5 8.5 %all-to-all-done.1 = f32[64,8,128]{2,1,0:T(8,128)S(1)} async-done(((f32[64,8,128]{2,1,0:T(8,128)}), f32[64,8,128]{2,1,0:T(8,128)S(1)}, u32[]{:S(2)}, u32[]{:S(2)}) %all-to-all-start.1) | async-done | bytes 262176 | tf_op jit(solution)/shard_map/all_to_all | solution.py:460
  89.0 15.8 %iterate.1.mine = f32[128,384]{1,0:T(8,128)S(1)} custom-call(f32[512,128]{1,0:T(8,128)S(1)} %bitcast.25, f32[128,384]{1,0:T(8,128)S(1)} %concatenate.25.start), custom_call_target="tpu_custom_call" | custom-call | flops 2000000000 | bytes 1000000 | tf_op jit(solution)/shard_map/iterate/pallas_call | solution.py:312
  104.8 1.3 %collective-permute-start.11 = (f32[128,384]{1,0:T(8,128)S(1)}, f32[128,384]{1,0:T(8,128)S(1)}, u32[]{:S(2)}, u32[]{:S(2)}) collective-permute-start(f32[128,384]{1,0:T(8,128)S(1)} %iterate.1.mine), channel_id=1, source_target_pairs={{2,1},{6,5},{10,9},{14,13},{18,17},{22,21},{26,25},{30,29},{34,33}... | collective-permute-start | bytes 589832 | tf_op jit(solution)/shard_map/ppermute | solution.py:465
  106.1 0.7 collective-permute-start.10
  106.7 0.1 collective-permute-start.9
  106.8 0.0 copy-done.1
  106.9 0.0 copy-start.3
  106.9 1.7 %copy-done.3 = bf16[150,2,4096]{2,0,1:T(8,128)(2,1)S(1)} copy-done((bf16[150,2,4096]{2,0,1:T(8,128)(2,1)S(1)}, bf16[150,2,4096]{2,0,1:T(8,128)(2,1)}, u32[]{:S(2)}) %copy-start.3) | copy-done | bytes 2457624
  108.6 4.7 %own.1 = f32[1,4096]{1,0:T(1,128)S(1)} custom-call(s32[2]{0:T(128)S(1)} %copy-done.4, s32[3]{0:T(128)S(1)} %broadcast_select_fusion.4.low, s32[3]{0:T(128)S(1)} %broadcast_select_fusion.3.high, f32[128,384]{1,0:T(8,128)S(1)} %iterate.1.mine, bf16[2,2,150,4096]{3,2,1,0:T(8,128)(2,1)S(1)} %bitcast.17, bf16[2,150,4096]{2,1,0:T(8,128)(2,1)S(1)} %bitcast.23), custom_call_target="tpu_custom_call" | custom-call | flops 3000000000 | bytes 10000000 | tf_op jit(solution)/shard_map/own/pallas_call | solution.py:406
  113.3 0.0 collective-permute-done.11.two
  113.3 0.0 collective-permute-done.10.one
  113.3 0.0 collective-permute-done.9.other
  113.3 3.0 %shared.1 = f32[1,2048]{1,0:T(1,128)S(1)} custom-call(s32[2]{0:T(128)S(1)} %copy-done.4, s32[3]{0:T(128)S(1)} %broadcast_select_fusion.4.low, s32[3]{0:T(128)S(1)} %broadcast_select_fusion.3.high, f32[128,384]{1,0:T(8,128)S(1)} %iterate.1.mine, f32[128,384]{1,0:T(8,128)S(1)} %collective-permute-done.9.other, f32[128,384]{1,0:T(8,128)S(1)} %collective-permute-done.10.one, ...), custom_call_target="tpu_custom_call" | custom-call | flops 1500000000 | bytes 10000000 | tf_op jit(solution)/shard_map/shared/pallas_call | solution.py:406
  116.3 5.3 %collective-permute-start.12 = (f32[1,2048]{1,0:T(1,128)S(1)}, f32[1,2048]{1,0:T(1,128)S(1)}, u32[]{:S(2)}, u32[]{:S(2)}) collective-permute-start(f32[1,2048]{1,0:T(1,128)S(1)} %shared.1), channel_id=1, source_target_pairs={{1,0},{3,2},{5,4},{7,6},{9,8},{11,10},{13,12},{15,14},{17,16},{19,... | collective-permute-start | bytes 24584 | tf_op jit(solution)/shard_map/ppermute | solution.py:479
  121.6 5.7 %other.1 = (f32[1,4096]{1,0:T(1,128)S(1)}, f32[300,2,128]{2,1,0:T(2,128)}) custom-call(s32[2]{0:T(128)S(1)} %copy-done.4, s32[3]{0:T(128)S(1)} %broadcast_select_fusion.4.low, s32[3]{0:T(128)S(1)} %broadcast_select_fusion.3.high, f32[128,384]{1,0:T(8,128)S(1)} %iterate.1.mine, f32[128,384]{1,0:T(8,128)S(1)} %collective-permute-done.9.other, ...), custom_call_target="tpu_custom_call" | custom-call | flops 3000000000 | bytes 10000000 | tf_op jit(solution)/shard_map/other/pallas_call | solution.py:406
  127.3 0.0 collective-permute-done.12
  127.3 0.6 pad_maximum_fusion
  (8 shorter events, 0.1 us)
Async XLA Ops:
  4.3 29.1 %collective-permute-start.5 = (bf16[150,2,2048]{2,1,0:T(2,128)(2,1)}, bf16[150,2,2048]{2,1,0:T(2,128)(2,1)S(1)}, u32[]{:S(2)}, u32[]{:S(2)}) collective-permute-start(bf16[150,2,2048]{2,1,0:T(2,128)(2,1)} %picked.1), channel_id=1, source_target_pairs={{0,1},{1,0},{2,3},{3,2},{4,5},{5,4},{6,7},{7,6},{8,9},{9,8},{10,11... | collective-permute-start | bytes 3686408 | tf_op jit(solution)/shard_map/ppermute | solution.py:445
  8.5 6.8 %copy-start.2 = (bf16[150,2,4096]{2,0,1:T(8,128)(2,1)}, bf16[150,2,4096]{2,0,1:T(8,128)(2,1)S(1)}, u32[]{:S(2)}) copy-start(bf16[150,2,4096]{2,0,1:T(8,128)(2,1)S(1)} %copy.24) | copy-start | bytes 7372804
  8.5 6.8 %copy-start.4 = (s32[2]{0:T(128)S(1)}, s32[2]{0:T(128)}, u32[]{:S(2)}) copy-start(s32[2]{0:T(128)} %pad_add_fusion.place) | copy-start | bytes 28
  15.3 5.0 %copy-start = (bf16[2,150,2,4096]{3,1,0,2:T(8,128)(2,1)}, bf16[2,150,2,4096]{3,1,0,2:T(8,128)(2,1)S(1)}, u32[]{:S(2)}) copy-start(bf16[2,150,2,4096]{3,1,0,2:T(8,128)(2,1)S(1)} %copy.23) | copy-start | bytes 14745604
  20.4 18.0 %collective-permute-start.2 = (f32[512,128]{1,0:T(8,128)S(1)}, f32[512,128]{1,0:T(8,128)S(1)}, u32[]{:S(2)}, u32[]{:S(2)}) collective-permute-start(f32[512,128]{1,0:T(8,128)S(1)} %get-tuple-element.9), channel_id=1, source_target_pairs={{0,2},{2,0},{1,3},{3,1},{4,6},{6,4},{5,7},{7,5},{8,10},{10,8},{9,1... | collective-permute-start | bytes 786440 | tf_op jit(solution)/shard_map/ppermute | solution.py:449
  20.5 17.2 %collective-permute-start.4 = (f32[288,128]{1,0:T(8,128)S(1)}, f32[288,128]{1,0:T(8,128)S(1)}, u32[]{:S(2)}, u32[]{:S(2)}) collective-permute-start(f32[288,128]{1,0:T(8,128)S(1)} %get-tuple-element.10), channel_id=1, source_target_pairs={{1,2},{5,6},{9,10},{13,14},{17,18},{21,22},{25,26},{29,30},{33,34}... | collective-permute-start | bytes 442376 | tf_op jit(solution)/shard_map/ppermute | solution.py:451
  23.7 14.6 %collective-permute-start.3 = (f32[288,128]{1,0:T(8,128)S(1)}, f32[288,128]{1,0:T(8,128)S(1)}, u32[]{:S(2)}, u32[]{:S(2)}) collective-permute-start(f32[288,128]{1,0:T(8,128)S(1)} %get-tuple-element.10), channel_id=1, source_target_pairs={{3,2},{7,6},{11,10},{15,14},{19,18},{23,22},{27,26},{31,30},{35,34... | collective-permute-start | bytes 442376 | tf_op jit(solution)/shard_map/ppermute | solution.py:450
  33.8 22.2 %copy-start.6 = (s32[2]{0:T(128)S(1)}, s32[2]{0:T(128)}, u32[]{:S(2)}) copy-start(s32[2]{0:T(128)} %param.8) | copy-start | bytes 28
  33.8 24.1 %copy-start.7 = (s32[2]{0:T(128)S(1)}, s32[2]{0:T(128)}, u32[]{:S(2)}) copy-start(s32[2]{0:T(128)} %param.9) | copy-start | bytes 28
  33.9 26.1 %copy-start.5 = (f32[300,128]{1,0:T(8,128)S(1)}, f32[300,128]{1,0:T(8,128)}, u32[]{:S(2)}) copy-start(f32[300,128]{1,0:T(8,128)} %param.7) | copy-start | bytes 460804
  35.1 3.2 %collective-permute-start.8 = (f32[184,128]{1,0:T(8,128)S(1)}, f32[184,128]{1,0:T(8,128)S(1)}, u32[]{:S(2)}, u32[]{:S(2)}) collective-permute-start(f32[184,128]{1,0:T(8,128)S(1)} %cross_products.1.own), channel_id=1, source_target_pairs={{0,2},{4,6},{8,10},{12,14},{16,18},{20,22},{24,26},{28,30},{32,34}... | collective-permute-start | bytes 282632 | tf_op jit(solution)/shard_map/ppermute | solution.py:456
  35.8 4.2 %collective-permute-start.7 = (f32[184,128]{1,0:T(8,128)S(1)}, f32[184,128]{1,0:T(8,128)S(1)}, u32[]{:S(2)}, u32[]{:S(2)}) collective-permute-start(f32[184,128]{1,0:T(8,128)S(1)} %cross_products.1.own), channel_id=1, source_target_pairs={{1,2},{5,6},{9,10},{13,14},{17,18},{21,22},{25,26},{29,30},{33,34}... | collective-permute-start | bytes 282632 | tf_op jit(solution)/shard_map/ppermute | solution.py:455
  37.6 2.3 %collective-permute-start.6 = (f32[184,128]{1,0:T(8,128)S(1)}, f32[184,128]{1,0:T(8,128)S(1)}, u32[]{:S(2)}, u32[]{:S(2)}) collective-permute-start(f32[184,128]{1,0:T(8,128)S(1)} %cross_products.1.own), channel_id=1, source_target_pairs={{3,2},{7,6},{11,10},{15,14},{19,18},{23,22},{27,26},{31,30},{35,34... | collective-permute-start | bytes 282632 | tf_op jit(solution)/shard_map/ppermute | solution.py:454
  41.3 26.9 %all-to-all-start = ((f32[64,8,128]{2,1,0:T(8,128)}), f32[64,8,128]{2,1,0:T(8,128)S(1)}, u32[]{:S(2)}, u32[]{:S(2)}) async-start(f32[64,8,128]{2,1,0:T(8,128)} %bitcast.6), calls=%async_computation | async-start | bytes 524288 | tf_op jit(solution)/shard_map/all_to_all | solution.py:458
  56.7 21.0 %collective-permute-start = (s32[1]{0:T(128)}, s32[1]{0:T(128)}, u32[]{:S(2)}, u32[]{:S(2)}) collective-permute-start(s32[1]{0:T(128)} %slice.20), channel_id=1, source_target_pairs={{0,1},{2,3},{4,5},{6,7},{8,9},{10,11},{12,13},{14,15},{16,17},{18,... | collective-permute-start | bytes 20 | tf_op jit(solution)/shard_map/ppermute | solution.py:467
  58.6 20.5 %collective-permute-start.1 = (s32[1]{0:T(128)}, s32[1]{0:T(128)}, u32[]{:S(2)}, u32[]{:S(2)}) collective-permute-start(s32[1]{0:T(128)} %slice.21), channel_id=1, source_target_pairs={{0,1},{2,3},{4,5},{6,7},{8,9},{10,11},{12,13},{14,15},{16,17},{18,... | collective-permute-start | bytes 20 | tf_op jit(solution)/shard_map/ppermute | solution.py:468
  69.0 20.0 %all-to-all-start.1 = ((f32[64,8,128]{2,1,0:T(8,128)}), f32[64,8,128]{2,1,0:T(8,128)S(1)}, u32[]{:S(2)}, u32[]{:S(2)}) async-start(f32[64,8,128]{2,1,0:T(8,128)} %broadcast_in_dim.12), calls=%async_computation.1 | async-start | bytes 524288 | tf_op jit(solution)/shard_map/all_to_all | solution.py:460
  89.0 17.9 %copy-start.1 = (bf16[2,150,2,4096]{3,1,0,2:T(8,128)(2,1)S(1)}, bf16[2,150,2,4096]{3,1,0,2:T(8,128)(2,1)}, u32[]{:S(2)}) copy-start(bf16[2,150,2,4096]{3,1,0,2:T(8,128)(2,1)} %copy-done) | copy-start | bytes 14745604
  104.8 8.5 %collective-permute-start.11 = (f32[128,384]{1,0:T(8,128)S(1)}, f32[128,384]{1,0:T(8,128)S(1)}, u32[]{:S(2)}, u32[]{:S(2)}) collective-permute-start(f32[128,384]{1,0:T(8,128)S(1)} %iterate.1.mine), channel_id=1, source_target_pairs={{2,1},{6,5},{10,9},{14,13},{18,17},{22,21},{26,25},{30,29},{34,33}... | collective-permute-start | bytes 589832 | tf_op jit(solution)/shard_map/ppermute | solution.py:465
  106.1 7.3 %collective-permute-start.10 = (f32[128,384]{1,0:T(8,128)S(1)}, f32[128,384]{1,0:T(8,128)S(1)}, u32[]{:S(2)}, u32[]{:S(2)}) collective-permute-start(f32[128,384]{1,0:T(8,128)S(1)} %iterate.1.mine), channel_id=1, source_target_pairs={{2,3},{6,7},{10,11},{14,15},{18,19},{22,23},{26,27},{30,31},{34,35... | collective-permute-start | bytes 589832 | tf_op jit(solution)/shard_map/ppermute | solution.py:464
  106.7 6.6 %collective-permute-start.9 = (f32[128,384]{1,0:T(8,128)S(1)}, f32[128,384]{1,0:T(8,128)S(1)}, u32[]{:S(2)}, u32[]{:S(2)}) collective-permute-start(f32[128,384]{1,0:T(8,128)S(1)} %iterate.1.mine), channel_id=1, source_target_pairs={{0,2},{2,0},{1,3},{3,1},{4,6},{6,4},{5,7},{7,5},{8,10},{10,8},{9,1... | collective-permute-start | bytes 589832 | tf_op jit(solution)/shard_map/ppermute | solution.py:466
  106.9 1.7 %copy-start.3 = (bf16[150,2,4096]{2,0,1:T(8,128)(2,1)S(1)}, bf16[150,2,4096]{2,0,1:T(8,128)(2,1)}, u32[]{:S(2)}) copy-start(bf16[150,2,4096]{2,0,1:T(8,128)(2,1)} %copy-done.2) | copy-start | bytes 7372804
  116.3 11.0 %collective-permute-start.12 = (f32[1,2048]{1,0:T(1,128)S(1)}, f32[1,2048]{1,0:T(1,128)S(1)}, u32[]{:S(2)}, u32[]{:S(2)}) collective-permute-start(f32[1,2048]{1,0:T(1,128)S(1)} %shared.1), channel_id=1, source_target_pairs={{1,0},{3,2},{5,4},{7,6},{9,8},{11,10},{13,12},{15,14},{17,16},{19,... | collective-permute-start | bytes 24584 | tf_op jit(solution)/shard_map/ppermute | solution.py:479

commit v3 on v2

--- a/solution.py
+++ b/solution.py
@@ -16,17 +16,18 @@
 REM = HALF - MAIN
 SPAN = 384
 USED = 320
+FLAG = 320
 TILE = 32
 PACKED = 512
 EXTRA = 288
 LATE = 184
-CHUNK = 512
+CHUNK = 1024
 LIMIT = 20 * 2**20
 HI = lax.Precision.HIGHEST
 F32 = jnp.float32
 BF16 = jnp.bfloat16
 PIX = ("pix_0", "pix_1", "pix_2", "pix_3")
-CHIPS = ("pix_0", "pix_1", "pix_2")
+PLANE = ("pix_1", "pix_2")
 SMEM = pl.BlockSpec(memory_space=pltpu.SMEM)
 VMEM = pl.BlockSpec(memory_space=pltpu.VMEM)
 
@@ -247,8 +248,44 @@
     return jnp.broadcast_to(vector[index : index + 1, :], vector.shape)
 
 
+def thirds(x):
+    one = x.astype(BF16)
+    rest = x - one.astype(F32)
+    two = rest.astype(BF16)
+    return one, two, (rest - two.astype(F32)).astype(BF16)
+
+
+def wide_first(x):
+    one, two, three = thirds(x)
+    group = grid_of(x.shape, 1) // TILE
+    head = jnp.where(group == 2, two.astype(F32), one.astype(F32)).astype(BF16)
+    tail = jnp.where(
+        group == 0, two.astype(F32), jnp.where(group == 1, three.astype(F32), 0.0)
+    ).astype(BF16)
+    return jnp.concatenate([head, tail], axis=1)
+
+
+def wide_second(x):
+    one, two, three = thirds(x)
+    group = grid_of(x.shape, 1) // TILE
+    head = jnp.where(
+        group == 1, two.astype(F32), jnp.where(group == 3, three.astype(F32), one.astype(F32))
+    ).astype(BF16)
+    tail = jnp.where(
+        group == 0, two.astype(F32), jnp.where(group == 1, one.astype(F32), 0.0)
+    ).astype(BF16)
+    return jnp.concatenate([head, tail], axis=1)
+
+
+def tall_second(x):
+    one, two, three = thirds(x)
+    zero = jnp.zeros((2 * TILE, x.shape[1]), BF16)
+    return jnp.concatenate([one, two, one, three, two, one, zero], axis=0)
+
+
 def eliminate(work, step):
     first = TILE * step
+    left = first + TILE
     sub = grid_of((8, 128), 0)
     lane = grid_of((8, 128), 1)
     groups = TILE // 8
@@ -259,7 +296,18 @@
         for k in range(8 * (g + 1)):
             at = first + k
             cols[g, k] = jnp.broadcast_to(block[:, at : at + 1], (8, 128))
-    inverse = [jnp.where(lane == sub + 8 * g, 1.0, 0.0).astype(F32) for g in range(groups)]
+    if left < K:
+        below = work[left:, 0:128]
+        group = grid_of(below.shape, 1) // TILE
+        repeated = jnp.zeros_like(below)
+        for c in range(4):
+            shift = (TILE * (c - step)) % 128
+            moved = pltpu.roll(below, shift, 1) if shift else below
+            repeated = jnp.where(group == c, moved, repeated)
+        under = wide_first(repeated)
+    inverse = [
+        jnp.where(lane % TILE == sub + 8 * g, 1.0, 0.0).astype(F32) for g in range(groups)
+    ]
     for j in range(TILE):
         gj, rj = divmod(j, 8)
         scale = lax.rsqrt(row_of(cols[gj, j], rj))
@@ -273,24 +321,24 @@
         pivot = row_of(inverse[gj], rj) * scale
         for g in range(gj, groups):
             if g == gj:
-                below = jnp.where(sub > rj, cols[g, j], 0.0)
-                inverse[g] = jnp.where(sub == rj, pivot, inverse[g] - below * pivot)
+                below_pivot = jnp.where(sub > rj, cols[g, j], 0.0)
+                inverse[g] = jnp.where(sub == rj, pivot, inverse[g] - below_pivot * pivot)
             else:
                 inverse[g] = inverse[g] - cols[g, j] * pivot
-    lhs = jnp.concatenate(inverse, axis=0)[:, 0:TILE]
+    turn = jnp.concatenate(inverse, axis=0)
     rows = jnp.dot(
-        lhs, work[first : first + TILE, :], precision=HI, preferred_element_type=F32
-    )
-    work[first : first + TILE, :] = rows
-    if first + TILE < K:
-        change = lax.dot_general(
-            rows[:, 0:128], rows, (((0,), (0,)), ((), ())), precision=HI,
-            preferred_element_type=F32,
+        wide_first(turn), tall_second(work[first:left, :]), preferred_element_type=F32
+    )
+    work[first:left, :] = rows
+    if left < K:
+        tall = wide_second(turn)
+        factors = across(under, jnp.concatenate([tall] * 4, axis=0))
+        work[left:, :] = work[left:, :] - jnp.dot(
+            wide_first(factors), tall_second(rows), preferred_element_type=F32
         )
-        work[first + TILE :, :] = work[first + TILE :, :] - change[first + TILE :, :]
-
-
-def iterate_kernel(packed, start, basis, gram, work):
+
+
+def iterate_kernel(place, low, high, packed, start, basis, gram, work):
     unpack(packed[...], gram)
     work[:, K:] = start[...]
 
@@ -305,26 +353,31 @@
         return carry
 
     lax.fori_loop(0, ITERS, step, 0)
-    basis[...] = work[:, K:]
-
-
-def iterate(packed, start):
+    which = place[0]
+    index = grid_of((K, 128), 0)
+    kept = (index >= low[which]) & (index < high[which])
+    basis[:, 0:256] = work[:, K : K + 256]
+    basis[:, 256:384] = jnp.where(
+        grid_of((K, 128), 1) == FLAG - 256, jnp.where(kept, 1.0, 0.0), work[:, K + 256 :]
+    )
+
+
+def iterate(place, low, high, packed, start):
     return pl.pallas_call(
         iterate_kernel,
         out_shape=jax.ShapeDtypeStruct((K, SPAN), F32),
-        in_specs=[VMEM, VMEM],
+        in_specs=[SMEM, SMEM, SMEM, VMEM, VMEM],
         out_specs=VMEM,
         scratch_shapes=[pltpu.VMEM((SPAN, SPAN), F32), pltpu.VMEM((K, K + SPAN), F32)],
         cost_estimate=pl.CostEstimate(flops=2 * 10**9, bytes_accessed=10**6, transcendentals=0),
         compiler_params=pltpu.CompilerParams(vmem_limit_bytes=LIMIT),
         name="iterate",
-    )(packed, start)
-
-
-def projection(rows, low, high):
+    )(place, low, high, packed, start)
+
+
+def projection(rows):
     used = rows[:, 0:USED]
-    index = grid_of((K, USED), 0)
-    kept = jnp.where((index >= low) & (index < high), used, 0.0)
+    kept = used * rows[:, FLAG : FLAG + 1]
     return lax.dot_general(
         kept, used, (((0,), (0,)), ((), ())), precision=HI, preferred_element_type=F32
     ).astype(BF16)
@@ -360,21 +413,20 @@
         powers(proj, chunk, power, (frames, 1, 0), (tail, None, 0), 0, pixels)
 
 
-def own_kernel(place, low, high, mine, frames, tail, power, proj, chunk):
+def own_kernel(place, mine, frames, tail, power, proj, chunk):
     chunk[...] = jnp.zeros_like(chunk)
-    which = place[0]
-    proj[...] = projection(mine[...], low[which], high[which])
-    whole_window(place, proj, chunk, power, frames, tail, which == 1)
-
-
-def shared_kernel(place, low, high, mine, other, one, two, frames, near, power, proj, chunk):
+    proj[...] = projection(mine[...])
+    whole_window(place, proj, chunk, power, frames, tail, place[0] == 1)
+
+
+def shared_kernel(place, mine, other, one, two, frames, near, power, proj, chunk):
     chunk[...] = jnp.zeros_like(chunk)
     pixels = near.shape[-1]
     last = place[1] == 1
     found = jnp.where(
         last, one[...] + two[...], jnp.where(place[0] == 1, mine[...], other[...])
     )
-    proj[...] = projection(found, low[2], high[2])
+    proj[...] = projection(found)
 
     @pl.when(last)
     def _():
@@ -385,11 +437,10 @@
         powers(proj, chunk, power, (frames, 1, 0), (near, None, 0), 0, pixels)
 
 
-def other_kernel(place, low, high, mine, other, frames, tail, power, basis, proj, chunk):
+def other_kernel(place, mine, other, frames, tail, power, basis, proj, chunk):
     chunk[...] = jnp.zeros_like(chunk)
-    which = 1 - place[0]
-    proj[...] = projection(other[...], low[which], high[which])
-    whole_window(place, proj, chunk, power, frames, tail, which == 1)
+    proj[...] = projection(other[...])
+    whole_window(place, proj, chunk, power, frames, tail, place[0] == 0)
     core = place[0] == 1
     for window in range(2):
         own = core if window else jnp.logical_not(core)
@@ -406,7 +457,7 @@
     return pl.pallas_call(
         kernel,
         out_shape=(shape, jax.ShapeDtypeStruct((WINDOW, 2, K), F32)) if with_basis else shape,
-        in_specs=[SMEM] * 3 + [VMEM] * (len(arrays) - 3),
+        in_specs=[SMEM] + [VMEM] * (len(arrays) - 1),
         out_specs=(VMEM, VMEM) if with_basis else VMEM,
         scratch_shapes=[pltpu.VMEM((USED, USED), BF16), pltpu.VMEM((2, USED, CHUNK), BF16)],
         cost_estimate=pl.CostEstimate(flops=flops, bytes_accessed=10**7, transcendentals=0),
@@ -439,7 +490,7 @@
     core = lax.axis_index("pix_3")
     block = lax.axis_index("tm")
     place = jnp.stack([core, block]).astype(jnp.int32)
-    chips = lax.axis_size(CHIPS)
+    chips = lax.axis_size(PLANE)
     pair = ("pix_3", "tm")
 
     near = lax.ppermute(picked(place, iq), "tm", [(0, 1), (1, 0)])
@@ -455,31 +506,28 @@
     two = lax.ppermute(late, pair, [(1, 2)])
     three = lax.ppermute(late, pair, [(0, 2)])
     mine = merged(place, keep, swapped, extra_one, extra_two, late, one, two, three)
-    pieces = lax.all_to_all(mine.reshape(chips, PACKED // chips, 128), CHIPS, 0, 0, tiled=True)
+    pieces = lax.all_to_all(mine.reshape(chips, PACKED // chips, 128), PLANE, 0, 0, tiled=True)
     piece = pieces.sum(axis=0)
+    piece = piece + lax.ppermute(piece, "pix_0", [(0, 1), (1, 0)])
     packed = lax.all_to_all(
-        jnp.broadcast_to(piece[None], pieces.shape), CHIPS, 0, 0, tiled=True
+        jnp.broadcast_to(piece[None], pieces.shape), PLANE, 0, 0, tiled=True
     ).reshape(PACKED, 128)
-    found = iterate(packed, in_lanes(start_basis))
+    found = iterate(place, low_rank, high_rank, packed, in_lanes(start_basis))
     one = lax.ppermute(found, pair, [(2, 3)])
     two = lax.ppermute(found, pair, [(2, 1)])
     other = lax.ppermute(found, "pix_3", [(0, 1), (1, 0)])
-    lows = jnp.concatenate([low_rank, lax.ppermute(low_rank[1:], "tm", [(0, 1)])])
-    highs = jnp.concatenate([high_rank, lax.ppermute(high_rank[1:], "tm", [(0, 1)])])
-    lows = jnp.where(block == 0, jnp.concatenate([low_rank, low_rank[1:]]), lows)
-    highs = jnp.where(block == 0, jnp.concatenate([high_rank, high_rank[1:]]), highs)
     flops = 3 * 10**9
     own = power_call(
-        own_kernel, "own", pixels, flops, False, place, lows, highs, found, frames, tail
+        own_kernel, "own", pixels, flops, False, place, found, frames, tail
     )
     shared = power_call(
         shared_kernel, "shared", half, flops // 2, False,
-        place, lows, highs, found, other, one, two, frames, near,
+        place, found, other, one, two, frames, near,
     )
     back = lax.ppermute(shared, "tm", [(1, 0)])
     rest, basis = power_call(
         other_kernel, "other", pixels, flops, True,
-        place, lows, highs, found, other, frames, tail,
+        place, found, other, frames, tail,
     )
     even = jnp.where(core == 0, own, rest)
     odd = jnp.where(core == 0, rest, own)

time: 130 us -> 124 us (0.954); the launches traced: 128 us -> 124 us
  blocking collectives: 0 us -> 25.2 us
  starting transfers between devices: 41 us -> 20.7 us
  Pallas kernels: 39.8 us -> 36.7 us
  other arithmetic: 4.11 us -> 1.31 us
  waiting for transfers between devices: 27.3 us -> 25.8 us
    all_to_all x0 -> x1, blocking collectives: none -> 25.2 us  [body(): lax.all_to_all(mine.reshape(chips, PACKED // chips, 128), PLANE, 0, 0, ti...]
    all_to_all x2 -> x1, starting transfers between devices: 23.1 us -> 4.11 us  [body(): lax.all_to_all(jnp.broadcast_to(piece[None], pieces.shape), PLANE, 0, 0,...]
    all_to_all x2 -> x1, waiting for transfers between devices: 16.6 us -> 11.1 us  [body(): lax.all_to_all(jnp.broadcast_to(piece[None], pieces.shape), PLANE, 0, 0,...]
    ppermute x2 -> x1, waiting for transfers between devices: 0.01 us -> 4.04 us  [body(): piece = piece + lax.ppermute(piece, 'pix_0', [(0, 1), (1, 0)])]
    select_n x2 -> x0, other arithmetic: 2.77 us -> none  [the longest x1 1.39 us: body(): jnp.where(block == 0, jnp.concatenate([low_rank, low_rank[1:]]), lows)]
    pallas_call x1, Pallas kernels: 15.8 us -> 13.9 us  [iterate(): pl.pallas_call(iterate_kernel, out_shape=jax.ShapeDtypeStruct((K, SPAN),...]
    ppermute x2 -> x1, starting transfers between devices: 2.56 us -> 1.2 us  [body(): piece = piece + lax.ppermute(piece, 'pix_0', [(0, 1), (1, 0)])]
    slice x2 -> x0, local copies, waits for them, and re-layouts: 1.31 us -> none  [the longest x1 0.66 us: body(): high_rank[1:]]
  transfers between devices with their start and end apart: 15 -> 13, of which waited for: 4 -> 4; matrix products, arithmetic and copies ran while one was open for 12% -> 9% of each run, Pallas kernels for 13% -> 13%
where the time goes in v3:
time: 124 us
  Pallas kernels  36.7 us (30%)
  waiting for transfers between devices  25.8 us (21%)
  blocking collectives  25.2 us (20%)
  starting transfers between devices  20.7 us (17%)
  local copies, waits for them, and re-layouts  13.4 us (11%)
  other arithmetic  1.31 us (1%)
    all_to_all x1, blocking collectives, body(): lax.all_to_all(mine.reshape(chips, PACKED // chips, 128), PLANE, 0, 0, ti...  25.2 us
    pallas_call x1, Pallas kernels, iterate(): pl.pallas_call(iterate_kernel, out_shape=jax.ShapeDtypeStruct((K, SPAN),...  13.9 us
    pallas_call x3, Pallas kernels, power_call(): pl.pallas_call(kernel, out_shape=(shape, jax.ShapeDtypeStruct((WINDOW, 2,...  12.8 us
    all_to_all x1, waiting for transfers between devices, body(): lax.all_to_all(jnp.broadcast_to(piece[None], pieces.shape), PLANE, 0, 0,...  11.1 us
    ppermute x1, waiting for transfers between devices, body(): near = lax.ppermute(picked(place, iq), 'tm', [(0, 1), (1, 0)])  9.01 us
    reshape x1, local copies, waits for them, and re-layouts, body(): frames = jnp.transpose(iq.reshape(2, HALF, 2, pixels), (2, 0, 1, 3))  6.81 us
    ppermute x1, starting transfers between devices, body(): back = lax.ppermute(shared, 'tm', [(1, 0)])  5.27 us
    unnamed x18, local copies, waits for them, and re-layouts  5.12 us
  transfers between devices with their start and end apart: 13, of which 4 were waited for; matrix products, arithmetic and copies ran while one was open for 9% of the time, Pallas kernels for 13%

profile of v3, /device:TPU:6, one launch (start us, length us, event | category | flops | bytes accessed | tf_op | source)
XLA Modules:
  0.0 124.0 jit_solution(6717403952413669785)
XLA Ops:
  0.6 0.6 pad_add_fusion.place
  1.2 3.1 %picked.1 = bf16[150,2,2048]{2,1,0:T(2,128)(2,1)} custom-call(s32[2]{0:T(128)} %pad_add_fusion.place, bf16[300,2,4096]{2,1,0:T(2,128)(2,1)} %source.1), custom_call_target="tpu_custom_call" | custom-call | tf_op jit(solution)/shard_map/picked/pallas_call | solution.py:63
  4.3 0.9 collective-permute-start.3
  5.2 3.3 %copy.24 = bf16[150,2,4096]{2,0,1:T(8,128)(2,1)S(1)} copy(bf16[150,2,4096]{2,1,0:T(2,128)(2,1)} %param.6) | data formatting | bytes 4915200 | tf_op args[1]
  8.5 0.0 copy-start.2
  8.5 0.0 copy-start.4
  8.5 6.8 %copy.23 = bf16[2,150,2,4096]{3,1,0,2:T(8,128)(2,1)S(1)} copy(bf16[2,150,2,4096]{3,2,1,0:T(2,128)(2,1)} %bitcast.27) | data formatting | bytes 9830400 | tf_op jit(solution)/shard_map/reshape | solution.py:497
  15.3 0.0 copy-start
  15.3 0.0 copy-done.2
  15.4 0.0 copy-done.4
  15.4 5.0 %local_products.1 = (f32[512,128]{1,0:T(8,128)S(1)}, f32[512,128]{1,0:T(8,128)S(1)}, f32[288,128]{1,0:T(8,128)S(1)}, bf16[2,150,2048]{2,1,0:T(8,128)(2,1)S(1)}) custom-call(s32[2]{0:T(128)S(1)} %copy-done.4, bf16[2,2,150,4096]{3,2,1,0:T(8,128)(2,1)S(1)} %bitcast.16, bf16[2,150,4096]{2,1,0:T(8,128)(2,1)S(1)} %bitcast.22), custom_call_target="tpu_custom_call" | custom-call | flops 4000000000 | bytes 8000000 | tf_op jit(solution)/shard_map/local_products/pallas_call | solution.py:136
  20.4 0.0 copy-done
  20.4 0.1 collective-permute-start
  20.5 3.2 %collective-permute-start.2 = (f32[288,128]{1,0:T(8,128)S(1)}, f32[288,128]{1,0:T(8,128)S(1)}, u32[]{:S(2)}, u32[]{:S(2)}) collective-permute-start(f32[288,128]{1,0:T(8,128)S(1)} %get-tuple-element.10), channel_id=1, source_target_pairs={{1,2},{5,6},{9,10},{13,14},{17,18},{21,22},{25,26},{29,30},{33,34}... | collective-permute-start | bytes 442376 | tf_op jit(solution)/shard_map/ppermute | solution.py:502
  23.7 0.7 collective-permute-start.1
  24.4 9.0 %collective-permute-done.3 = bf16[150,2,2048]{2,1,0:T(2,128)(2,1)S(1)} collective-permute-done((bf16[150,2,2048]{2,1,0:T(2,128)(2,1)}, bf16[150,2,2048]{2,1,0:T(2,128)(2,1)S(1)}, u32[]{:S(2)}, u32[]{:S(2)}) %collective-permute-start.3) | collective-permute-done | bytes 1228832 | tf_op jit(solution)/shard_map/ppermute | solution.py:496
  33.4 0.5 copy.25
  33.8 0.0 copy-start.7
  33.9 1.3 %cross_products.1.own = f32[184,128]{1,0:T(8,128)S(1)} custom-call(s32[2]{0:T(128)S(1)} %copy-done.4, bf16[2,150,2048]{2,1,0:T(8,128)(2,1)S(1)} %get-tuple-element.11.own, bf16[2,150,2048]{2,1,0:T(8,128)(2,1)S(1)} %bitcast.20), custom_call_target="tpu_custom_call" | custom-call | flops 400000000 | bytes 3000000 | tf_op jit(solution)/shard_map/cross_products/pallas_call | solution.py:173
  35.1 0.0 copy-start.5
  35.1 0.0 copy-start.6
  35.1 0.7 collective-permute-start.6
  35.8 1.8 %collective-permute-start.5 = (f32[184,128]{1,0:T(8,128)S(1)}, f32[184,128]{1,0:T(8,128)S(1)}, u32[]{:S(2)}, u32[]{:S(2)}) collective-permute-start(f32[184,128]{1,0:T(8,128)S(1)} %cross_products.1.own), channel_id=1, source_target_pairs={{1,2},{5,6},{9,10},{13,14},{17,18},{21,22},{25,26},{29,30},{33,34}... | collective-permute-start | bytes 282632 | tf_op jit(solution)/shard_map/ppermute | solution.py:506
  37.7 0.0 collective-permute-done.2.extra_two
  37.7 0.7 collective-permute-start.4
  38.3 0.0 collective-permute-done.1.extra_one
  38.4 0.0 collective-permute-done.swapped
  38.4 0.0 collective-permute-done.6.three
  38.4 1.6 %collective-permute-done.5.two = f32[184,128]{1,0:T(8,128)S(1)} collective-permute-done((f32[184,128]{1,0:T(8,128)S(1)}, f32[184,128]{1,0:T(8,128)S(1)}, u32[]{:S(2)}, u32[]{:S(2)}) %collective-permute-start.5) | collective-permute-done | bytes 94240 | tf_op jit(solution)/shard_map/ppermute | solution.py:506
  40.0 0.0 collective-permute-done.4.one
  40.0 0.6 merged.1
  40.6 25.2 %all_to_all.10 = f32[32,16,128]{2,1,0:T(8,128)S(1)} all-to-all(f32[32,16,128]{2,1,0:T(8,128)S(1)} %bitcast.25), channel_id=1, replica_groups=mesh['pix_0'=2,'pix_1'=8,'pix_2'=4,'pix_3'=2,'tm'=2] {'pix_1','pix_2'}, dimensions={0} | all-to-all | bytes 524288 | tf_op jit(solution)/shard_map/all_to_all | solution.py:509
  65.8 1.2 collective-permute-start.7
  67.0 4.0 %collective-permute-done.7 = f32[16,128]{1,0:T(8,128)S(1)} collective-permute-done((f32[16,128]{1,0:T(8,128)S(1)}, f32[16,128]{1,0:T(8,128)S(1)}, u32[]{:S(2)}, u32[]{:S(2)}) %collective-permute-start.7) | collective-permute-done | bytes 8224 | tf_op jit(solution)/shard_map/ppermute | solution.py:511
  71.0 0.7 broadcast_in_dim.12
  71.8 4.1 %all-to-all-start.1 = ((f32[32,16,128]{2,1,0:T(8,128)}), f32[32,16,128]{2,1,0:T(8,128)S(1)}, u32[]{:S(2)}, u32[]{:S(2)}) async-start(f32[32,16,128]{2,1,0:T(8,128)} %broadcast_in_dim.12), calls=%async_computation.1 | async-start | bytes 524288 | tf_op jit(solution)/shard_map/all_to_all | solution.py:512
  75.9 0.0 copy-done.7
  75.9 0.1 copy.18
  76.0 0.1 fusion.1
  76.1 0.1 fusion
  76.2 0.1 concatenate.9.start
  76.4 11.1 %all-to-all-done.1 = f32[32,16,128]{2,1,0:T(8,128)S(1)} async-done(((f32[32,16,128]{2,1,0:T(8,128)}), f32[32,16,128]{2,1,0:T(8,128)S(1)}, u32[]{:S(2)}, u32[]{:S(2)}) %all-to-all-start.1) | async-done | bytes 262176 | tf_op jit(solution)/shard_map/all_to_all | solution.py:512
  87.4 0.0 copy-done.5
  87.4 0.0 copy-done.6
  87.4 0.0 copy-start.1
  87.4 13.9 %iterate.1.mine = f32[128,384]{1,0:T(8,128)S(1)} custom-call(s32[2]{0:T(128)S(1)} %copy-done.4, s32[2]{0:T(128)S(1)} %copy-done.5, s32[2]{0:T(128)S(1)} %copy-done.6, f32[512,128]{1,0:T(8,128)S(1)} %bitcast.26, f32[128,384]{1,0:T(8,128)S(1)} %concatenate.9.start), custom_call_target="tpu_custom_call" | custom-call | flops 2000000000 | bytes 1000000 | tf_op jit(solution)/shard_map/iterate/pallas_call | solution.py:366
  101.4 1.3 %collective-permute-start.10 = (f32[128,384]{1,0:T(8,128)S(1)}, f32[128,384]{1,0:T(8,128)S(1)}, u32[]{:S(2)}, u32[]{:S(2)}) collective-permute-start(f32[128,384]{1,0:T(8,128)S(1)} %iterate.1.mine), channel_id=1, source_target_pairs={{2,1},{6,5},{10,9},{14,13},{18,17},{22,21},{26,25},{30,29},{34,33}... | collective-permute-start | bytes 589832 | tf_op jit(solution)/shard_map/ppermute | solution.py:517
  102.7 0.7 collective-permute-start.9
  103.3 0.1 collective-permute-start.8
  103.4 0.0 copy-done.1
  103.5 0.0 copy-start.3
  103.5 1.7 %copy-done.3 = bf16[150,2,4096]{2,0,1:T(8,128)(2,1)S(1)} copy-done((bf16[150,2,4096]{2,0,1:T(8,128)(2,1)S(1)}, bf16[150,2,4096]{2,0,1:T(8,128)(2,1)}, u32[]{:S(2)}) %copy-start.3) | copy-done | bytes 2457624
  105.2 4.4 %own.1 = f32[1,4096]{1,0:T(1,128)S(1)} custom-call(s32[2]{0:T(128)S(1)} %copy-done.4, f32[128,384]{1,0:T(8,128)S(1)} %iterate.1.mine, bf16[2,2,150,4096]{3,2,1,0:T(8,128)(2,1)S(1)} %bitcast.17, bf16[2,150,4096]{2,1,0:T(8,128)(2,1)S(1)} %bitcast.23), custom_call_target="tpu_custom_call" | custom-call | flops 3000000000 | bytes 10000000 | tf_op jit(solution)/shard_map/own/pallas_call | solution.py:457
  109.6 0.0 collective-permute-done.10.two
  109.6 0.0 collective-permute-done.9.one
  109.6 0.0 collective-permute-done.8.other
  109.6 2.8 %shared.1 = f32[1,2048]{1,0:T(1,128)S(1)} custom-call(s32[2]{0:T(128)S(1)} %copy-done.4, f32[128,384]{1,0:T(8,128)S(1)} %iterate.1.mine, f32[128,384]{1,0:T(8,128)S(1)} %collective-permute-done.8.other, f32[128,384]{1,0:T(8,128)S(1)} %collective-permute-done.9.one, f32[128,384]{1,0:T(8,128)S(1)} %collective-permute-done.10.two, ...), custom_call_target="tpu_custom_call" | custom-call | flops 1500000000 | bytes 10000000 | tf_op jit(solution)/shard_map/shared/pallas_call | solution.py:457
  112.4 5.3 %collective-permute-start.11 = (f32[1,2048]{1,0:T(1,128)S(1)}, f32[1,2048]{1,0:T(1,128)S(1)}, u32[]{:S(2)}, u32[]{:S(2)}) collective-permute-start(f32[1,2048]{1,0:T(1,128)S(1)} %shared.1), channel_id=1, source_target_pairs={{1,0},{3,2},{5,4},{7,6},{9,8},{11,10},{13,12},{15,14},{17,16},{19,... | collective-permute-start | bytes 24584 | tf_op jit(solution)/shard_map/ppermute | solution.py:527
  117.7 5.6 %other.1 = (f32[1,4096]{1,0:T(1,128)S(1)}, f32[300,2,128]{2,1,0:T(2,128)}) custom-call(s32[2]{0:T(128)S(1)} %copy-done.4, f32[128,384]{1,0:T(8,128)S(1)} %iterate.1.mine, f32[128,384]{1,0:T(8,128)S(1)} %collective-permute-done.8.other, bf16[2,2,150,4096]{3,2,1,0:T(8,128)(2,1)S(1)} %bitcast.19, bf16[2,150,4096]{2,1,0:T(8,128)(2,1)S(1)} %bitcast.24), custom_call_target="tpu_custom_call" | custom-call | flops 3000000000 | bytes 10000000 | tf_op jit(solution)/shard_map/other/pallas_call | solution.py:457
  123.3 0.0 collective-permute-done.11
  123.4 0.6 pad_maximum_fusion
  (5 shorter events, 0.1 us)
Async XLA Ops:
  4.3 29.1 %collective-permute-start.3 = (bf16[150,2,2048]{2,1,0:T(2,128)(2,1)}, bf16[150,2,2048]{2,1,0:T(2,128)(2,1)S(1)}, u32[]{:S(2)}, u32[]{:S(2)}) collective-permute-start(bf16[150,2,2048]{2,1,0:T(2,128)(2,1)} %picked.1), channel_id=1, source_target_pairs={{0,1},{1,0},{2,3},{3,2},{4,5},{5,4},{6,7},{7,6},{8,9},{9,8},{10,11... | collective-permute-start | bytes 3686408 | tf_op jit(solution)/shard_map/ppermute | solution.py:496
  8.5 6.8 %copy-start.2 = (bf16[150,2,4096]{2,0,1:T(8,128)(2,1)}, bf16[150,2,4096]{2,0,1:T(8,128)(2,1)S(1)}, u32[]{:S(2)}) copy-start(bf16[150,2,4096]{2,0,1:T(8,128)(2,1)S(1)} %copy.24) | copy-start | bytes 7372804
  8.5 6.8 %copy-start.4 = (s32[2]{0:T(128)S(1)}, s32[2]{0:T(128)}, u32[]{:S(2)}) copy-start(s32[2]{0:T(128)} %pad_add_fusion.place) | copy-start | bytes 28
  15.3 5.0 %copy-start = (bf16[2,150,2,4096]{3,1,0,2:T(8,128)(2,1)}, bf16[2,150,2,4096]{3,1,0,2:T(8,128)(2,1)S(1)}, u32[]{:S(2)}) copy-start(bf16[2,150,2,4096]{3,1,0,2:T(8,128)(2,1)S(1)} %copy.23) | copy-start | bytes 14745604
  20.4 18.0 %collective-permute-start = (f32[512,128]{1,0:T(8,128)S(1)}, f32[512,128]{1,0:T(8,128)S(1)}, u32[]{:S(2)}, u32[]{:S(2)}) collective-permute-start(f32[512,128]{1,0:T(8,128)S(1)} %get-tuple-element.9), channel_id=1, source_target_pairs={{0,2},{2,0},{1,3},{3,1},{4,6},{6,4},{5,7},{7,5},{8,10},{10,8},{9,1... | collective-permute-start | bytes 786440 | tf_op jit(solution)/shard_map/ppermute | solution.py:500
  20.5 17.2 %collective-permute-start.2 = (f32[288,128]{1,0:T(8,128)S(1)}, f32[288,128]{1,0:T(8,128)S(1)}, u32[]{:S(2)}, u32[]{:S(2)}) collective-permute-start(f32[288,128]{1,0:T(8,128)S(1)} %get-tuple-element.10), channel_id=1, source_target_pairs={{1,2},{5,6},{9,10},{13,14},{17,18},{21,22},{25,26},{29,30},{33,34}... | collective-permute-start | bytes 442376 | tf_op jit(solution)/shard_map/ppermute | solution.py:502
  23.7 14.6 %collective-permute-start.1 = (f32[288,128]{1,0:T(8,128)S(1)}, f32[288,128]{1,0:T(8,128)S(1)}, u32[]{:S(2)}, u32[]{:S(2)}) collective-permute-start(f32[288,128]{1,0:T(8,128)S(1)} %get-tuple-element.10), channel_id=1, source_target_pairs={{3,2},{7,6},{11,10},{15,14},{19,18},{23,22},{27,26},{31,30},{35,34... | collective-permute-start | bytes 442376 | tf_op jit(solution)/shard_map/ppermute | solution.py:501
  33.8 42.0 %copy-start.7 = (f32[300,128]{1,0:T(8,128)S(1)}, f32[300,128]{1,0:T(8,128)}, u32[]{:S(2)}) copy-start(f32[300,128]{1,0:T(8,128)} %param.7) | copy-start | bytes 460804
  35.1 52.3 %copy-start.5 = (s32[2]{0:T(128)S(1)}, s32[2]{0:T(128)}, u32[]{:S(2)}) copy-start(s32[2]{0:T(128)} %low.1) | copy-start | bytes 28
  35.1 52.3 %copy-start.6 = (s32[2]{0:T(128)S(1)}, s32[2]{0:T(128)}, u32[]{:S(2)}) copy-start(s32[2]{0:T(128)} %high.1) | copy-start | bytes 28
  35.1 3.2 %collective-permute-start.6 = (f32[184,128]{1,0:T(8,128)S(1)}, f32[184,128]{1,0:T(8,128)S(1)}, u32[]{:S(2)}, u32[]{:S(2)}) collective-permute-start(f32[184,128]{1,0:T(8,128)S(1)} %cross_products.1.own), channel_id=1, source_target_pairs={{0,2},{4,6},{8,10},{12,14},{16,18},{20,22},{24,26},{28,30},{32,34}... | collective-permute-start | bytes 282632 | tf_op jit(solution)/shard_map/ppermute | solution.py:507
  35.8 4.2 %collective-permute-start.5 = (f32[184,128]{1,0:T(8,128)S(1)}, f32[184,128]{1,0:T(8,128)S(1)}, u32[]{:S(2)}, u32[]{:S(2)}) collective-permute-start(f32[184,128]{1,0:T(8,128)S(1)} %cross_products.1.own), channel_id=1, source_target_pairs={{1,2},{5,6},{9,10},{13,14},{17,18},{21,22},{25,26},{29,30},{33,34}... | collective-permute-start | bytes 282632 | tf_op jit(solution)/shard_map/ppermute | solution.py:506
  37.7 2.3 %collective-permute-start.4 = (f32[184,128]{1,0:T(8,128)S(1)}, f32[184,128]{1,0:T(8,128)S(1)}, u32[]{:S(2)}, u32[]{:S(2)}) collective-permute-start(f32[184,128]{1,0:T(8,128)S(1)} %cross_products.1.own), channel_id=1, source_target_pairs={{3,2},{7,6},{11,10},{15,14},{19,18},{23,22},{27,26},{31,30},{35,34... | collective-permute-start | bytes 282632 | tf_op jit(solution)/shard_map/ppermute | solution.py:505
  65.8 5.2 %collective-permute-start.7 = (f32[16,128]{1,0:T(8,128)S(1)}, f32[16,128]{1,0:T(8,128)S(1)}, u32[]{:S(2)}, u32[]{:S(2)}) collective-permute-start(f32[16,128]{1,0:T(8,128)S(1)} %reduce_sum.9), channel_id=1, source_target_pairs={{0,128},{128,0},{1,129},{129,1},{2,130},{130,2},{3,131},{131,3},{4... | collective-permute-start | bytes 24584 | tf_op jit(solution)/shard_map/ppermute | solution.py:511
  71.8 15.7 %all-to-all-start.1 = ((f32[32,16,128]{2,1,0:T(8,128)}), f32[32,16,128]{2,1,0:T(8,128)S(1)}, u32[]{:S(2)}, u32[]{:S(2)}) async-start(f32[32,16,128]{2,1,0:T(8,128)} %broadcast_in_dim.12), calls=%async_computation.1 | async-start | bytes 524288 | tf_op jit(solution)/shard_map/all_to_all | solution.py:512
  87.4 16.0 %copy-start.1 = (bf16[2,150,2,4096]{3,1,0,2:T(8,128)(2,1)S(1)}, bf16[2,150,2,4096]{3,1,0,2:T(8,128)(2,1)}, u32[]{:S(2)}) copy-start(bf16[2,150,2,4096]{3,1,0,2:T(8,128)(2,1)} %copy-done) | copy-start | bytes 14745604
  101.4 8.2 %collective-permute-start.10 = (f32[128,384]{1,0:T(8,128)S(1)}, f32[128,384]{1,0:T(8,128)S(1)}, u32[]{:S(2)}, u32[]{:S(2)}) collective-permute-start(f32[128,384]{1,0:T(8,128)S(1)} %iterate.1.mine), channel_id=1, source_target_pairs={{2,1},{6,5},{10,9},{14,13},{18,17},{22,21},{26,25},{30,29},{34,33}... | collective-permute-start | bytes 589832 | tf_op jit(solution)/shard_map/ppermute | solution.py:517
  102.7 6.9 %collective-permute-start.9 = (f32[128,384]{1,0:T(8,128)S(1)}, f32[128,384]{1,0:T(8,128)S(1)}, u32[]{:S(2)}, u32[]{:S(2)}) collective-permute-start(f32[128,384]{1,0:T(8,128)S(1)} %iterate.1.mine), channel_id=1, source_target_pairs={{2,3},{6,7},{10,11},{14,15},{18,19},{22,23},{26,27},{30,31},{34,35... | collective-permute-start | bytes 589832 | tf_op jit(solution)/shard_map/ppermute | solution.py:516
  103.3 6.2 %collective-permute-start.8 = (f32[128,384]{1,0:T(8,128)S(1)}, f32[128,384]{1,0:T(8,128)S(1)}, u32[]{:S(2)}, u32[]{:S(2)}) collective-permute-start(f32[128,384]{1,0:T(8,128)S(1)} %iterate.1.mine), channel_id=1, source_target_pairs={{0,2},{2,0},{1,3},{3,1},{4,6},{6,4},{5,7},{7,5},{8,10},{10,8},{9,1... | collective-permute-start | bytes 589832 | tf_op jit(solution)/shard_map/ppermute | solution.py:518
  103.5 1.7 %copy-start.3 = (bf16[150,2,4096]{2,0,1:T(8,128)(2,1)S(1)}, bf16[150,2,4096]{2,0,1:T(8,128)(2,1)}, u32[]{:S(2)}) copy-start(bf16[150,2,4096]{2,0,1:T(8,128)(2,1)} %copy-done.2) | copy-start | bytes 7372804
  112.4 10.9 %collective-permute-start.11 = (f32[1,2048]{1,0:T(1,128)S(1)}, f32[1,2048]{1,0:T(1,128)S(1)}, u32[]{:S(2)}, u32[]{:S(2)}) collective-permute-start(f32[1,2048]{1,0:T(1,128)S(1)} %shared.1), channel_id=1, source_target_pairs={{1,0},{3,2},{5,4},{7,6},{9,8},{11,10},{13,12},{15,14},{17,16},{19,... | collective-permute-start | bytes 24584 | tf_op jit(solution)/shard_map/ppermute | solution.py:527

commit v4 on v3

--- a/solution.py
+++ b/solution.py
@@ -44,8 +44,8 @@
     return pltpu.CompilerParams(vmem_limit_bytes=LIMIT)
 
 
-def pick_kernel(place, source, out, done):
-    first = 1 - place[1]
+def pick_kernel(source, out, done):
+    first = 1 - lax.axis_index("tm")
     width = out.shape[-1]
     copy = pltpu.make_async_copy(
         source.at[
@@ -58,16 +58,17 @@
     copy.wait()
 
 
-def picked(place, iq):
+def picked(iq):
     half = iq.shape[-1] // 2
     return pl.pallas_call(
         pick_kernel,
         out_shape=jax.ShapeDtypeStruct((HALF, 2, half), iq.dtype),
-        in_specs=[SMEM, pl.BlockSpec(memory_space=pltpu.HBM)],
+        in_specs=[pl.BlockSpec(memory_space=pltpu.HBM)],
         out_specs=VMEM,
         scratch_shapes=[pltpu.SemaphoreType.DMA],
+        compiler_params=parameters(),
         name="picked",
-    )(place, iq)
+    )(pltpu.with_memory_space_constraint(iq, pltpu.HBM))
 
 
 def lower_and_diagonal(block):
@@ -369,7 +370,7 @@
         in_specs=[SMEM, SMEM, SMEM, VMEM, VMEM],
         out_specs=VMEM,
         scratch_shapes=[pltpu.VMEM((SPAN, SPAN), F32), pltpu.VMEM((K, K + SPAN), F32)],
-        cost_estimate=pl.CostEstimate(flops=2 * 10**9, bytes_accessed=10**6, transcendentals=0),
+        cost_estimate=pl.CostEstimate(flops=14 * 10**9, bytes_accessed=10**6, transcendentals=0),
         compiler_params=pltpu.CompilerParams(vmem_limit_bytes=LIMIT),
         name="iterate",
     )(place, low, high, packed, start)
@@ -437,29 +438,38 @@
         powers(proj, chunk, power, (frames, 1, 0), (near, None, 0), 0, pixels)
 
 
-def other_kernel(place, mine, other, frames, tail, power, basis, proj, chunk):
-    chunk[...] = jnp.zeros_like(chunk)
-    proj[...] = projection(other[...])
-    whole_window(place, proj, chunk, power, frames, tail, place[0] == 0)
+def other_kernel(place, mine, other, frames, tail, power, basis, proj, chunk, held, done):
     core = place[0] == 1
     for window in range(2):
         own = core if window else jnp.logical_not(core)
         rows = jnp.where(own, mine[...], other[...])
         ends = rows[:, 256:384].T
-        basis[0:MAIN, window, :] = rows[:, 0:128].T
-        basis[MAIN:HALF, window, :] = ends[0:REM]
-        basis[HALF : HALF + MAIN, window, :] = rows[:, 128:256].T
-        basis[HALF + MAIN : WINDOW, window, :] = ends[32 : 32 + REM]
+        held[0:MAIN, window, :] = rows[:, 0:128].T
+        held[MAIN:HALF, window, :] = ends[0:REM]
+        held[HALF : HALF + MAIN, window, :] = rows[:, 128:256].T
+        held[HALF + MAIN : WINDOW, window, :] = ends[32 : 32 + REM]
+    copy = pltpu.make_async_copy(held, basis, done)
+    copy.start()
+    chunk[...] = jnp.zeros_like(chunk)
+    proj[...] = projection(other[...])
+    whole_window(place, proj, chunk, power, frames, tail, place[0] == 0)
+    copy.wait()
 
 
 def power_call(kernel, name, pixels, flops, with_basis, *arrays):
     shape = jax.ShapeDtypeStruct((1, pixels), F32)
+    scratch = [pltpu.VMEM((USED, USED), BF16), pltpu.VMEM((2, USED, CHUNK), BF16)]
+    outs, specs = shape, VMEM
+    if with_basis:
+        outs = (shape, jax.ShapeDtypeStruct((WINDOW, 2, K), F32))
+        specs = (VMEM, pl.BlockSpec(memory_space=pl.ANY))
+        scratch += [pltpu.VMEM((WINDOW, 2, K), F32), pltpu.SemaphoreType.DMA]
     return pl.pallas_call(
         kernel,
-        out_shape=(shape, jax.ShapeDtypeStruct((WINDOW, 2, K), F32)) if with_basis else shape,
+        out_shape=outs,
         in_specs=[SMEM] + [VMEM] * (len(arrays) - 1),
-        out_specs=(VMEM, VMEM) if with_basis else VMEM,
-        scratch_shapes=[pltpu.VMEM((USED, USED), BF16), pltpu.VMEM((2, USED, CHUNK), BF16)],
+        out_specs=specs,
+        scratch_shapes=scratch,
         cost_estimate=pl.CostEstimate(flops=flops, bytes_accessed=10**7, transcendentals=0),
         compiler_params=parameters(),
         name=name,
@@ -493,7 +503,7 @@
     chips = lax.axis_size(PLANE)
     pair = ("pix_3", "tm")
 
-    near = lax.ppermute(picked(place, iq), "tm", [(0, 1), (1, 0)])
+    near = lax.ppermute(picked(iq), "tm", [(0, 1), (1, 0)])
     frames = jnp.transpose(iq.reshape(2, HALF, 2, pixels), (2, 0, 1, 3))
     tail = jnp.swapaxes(tail_frames, 0, 1)
     keep, swap, extra, own_half = local_products(place, frames, tail)

time: 124 us -> 121 us (0.976)
  local copies, waits for them, and re-layouts: 13.4 us -> 9.98 us
  waiting for transfers between devices: 25.8 us -> 29.1 us
  Pallas kernels: 36.7 us -> 34 us
    reshape x1, local copies, waits for them, and re-layouts: 6.81 us -> 3.59 us  [body(): frames = jnp.transpose(iq.reshape(2, HALF, 2, pixels), (2, 0, 1, 3))]
    ppermute x1, waiting for transfers between devices: 9.01 us -> 11.9 us  [body(): near = lax.ppermute(picked(iq), 'tm', [(0, 1), (1, 0)])]
    pallas_call x1, Pallas kernels: 3.1 us -> 1.31 us  [picked(): pl.pallas_call(pick_kernel, out_shape=jax.ShapeDtypeStruct((HALF, 2, half...]
    unnamed x18 -> x20, local copies, waits for them, and re-layouts: 5.12 us -> 3.6 us
    ppermute x1, local copies, waits for them, and re-layouts: 0.45 us -> 1.74 us  [body(): near = lax.ppermute(picked(iq), 'tm', [(0, 1), (1, 0)])]
  transfers between devices with their start and end apart: 13 -> 13, of which waited for: 4 -> 5; matrix products, arithmetic and copies ran while one was open for 9% -> 8% of each run, Pallas kernels for 13% -> 13%
where the time goes in v4:
time: 121 us; the launch traced here: 120 us
  Pallas kernels  34 us (28%)
  waiting for transfers between devices  29.1 us (24%)
  blocking collectives  25.2 us (21%)
  starting transfers between devices  20.2 us (17%)
  local copies, waits for them, and re-layouts  9.98 us (8%)
    all_to_all x1, blocking collectives, body(): lax.all_to_all(mine.reshape(chips, PACKED // chips, 128), PLANE, 0, 0, ti...  25.2 us
    pallas_call x1, Pallas kernels, iterate(): pl.pallas_call(iterate_kernel, out_shape=jax.ShapeDtypeStruct((K, SPAN),...  13.9 us
    ppermute x1, waiting for transfers between devices, body(): near = lax.ppermute(picked(iq), 'tm', [(0, 1), (1, 0)])  11.9 us
    pallas_call x3, Pallas kernels, power_call(): pl.pallas_call(kernel, out_shape=outs, in_specs=[SMEM] + [VMEM] * (len(ar...  11.9 us
    all_to_all x1, waiting for transfers between devices, body(): lax.all_to_all(jnp.broadcast_to(piece[None], pieces.shape), PLANE, 0, 0,...  11 us
    pallas_call x1, Pallas kernels, local_products(): pl.pallas_call(local_kernel, out_shape=(shape, shape, jax.ShapeDtypeStruc...  4.97 us
    ppermute x1, starting transfers between devices, body(): back = lax.ppermute(shared, 'tm', [(1, 0)])  4.83 us
    all_to_all x1, starting transfers between devices, body(): lax.all_to_all(jnp.broadcast_to(piece[None], pieces.shape), PLANE, 0, 0,...  4.1 us
  transfers between devices with their start and end apart: 13, of which 5 were waited for; matrix products, arithmetic and copies ran while one was open for 8% of the time, Pallas kernels for 13%

profile of v4, /device:TPU:6, one launch (start us, length us, event | category | flops | bytes accessed | tf_op | source)
XLA Modules:
  0.0 120.3 jit_solution(9945766203953426771)
XLA Ops:
  0.6 1.3 %picked.1 = bf16[150,2,2048]{2,1,0:T(2,128)(2,1)S(1)} custom-call(bf16[300,2,4096]{2,1,0:T(2,128)(2,1)} %source.1), custom_call_target="tpu_custom_call" | custom-call | tf_op jit(solution)/shard_map/picked/pallas_call | solution.py:63
  1.9 0.9 collective-permute-start.3
  2.9 0.0 copy-start.5
  2.9 3.4 %copy.24 = bf16[150,2,4096]{2,0,1:T(8,128)(2,1)S(1)} copy(bf16[150,2,4096]{2,1,0:T(2,128)(2,1)} %param.6) | data formatting | bytes 4915200 | tf_op args[1]
  6.3 0.0 copy-start.1
  6.3 0.0 copy-done.5
  6.3 3.6 %copy.23 = bf16[2,150,2,4096]{3,1,0,2:T(8,128)(2,1)S(1)} copy(bf16[2,150,2,4096]{3,2,1,0:T(2,128)(2,1)S(1)} %bitcast.29) | data formatting | bytes 9830400 | tf_op jit(solution)/shard_map/reshape | solution.py:507
  9.9 0.0 copy-start
  9.9 0.1 pad_add_fusion.place
  10.0 0.0 copy-done.1
  10.0 5.0 %local_products.1 = (f32[512,128]{1,0:T(8,128)S(1)}, f32[512,128]{1,0:T(8,128)S(1)}, f32[288,128]{1,0:T(8,128)S(1)}, bf16[2,150,2048]{2,1,0:T(8,128)(2,1)S(1)}) custom-call(s32[2]{0:T(128)S(1)} %pad_add_fusion.place, bf16[2,2,150,4096]{3,2,1,0:T(8,128)(2,1)S(1)} %bitcast.16, bf16[2,150,4096]{2,1,0:T(8,128)(2,1)S(1)} %bitcast.24), custom_call_target="tpu_custom_call" | custom-call | flops 4000000000 | bytes 8000000 | tf_op jit(solution)/shard_map/local_products/pallas_call | solution.py:137
  15.0 0.0 copy-done
  15.0 0.1 collective-permute-start
  15.1 3.2 %collective-permute-start.2 = (f32[288,128]{1,0:T(8,128)S(1)}, f32[288,128]{1,0:T(8,128)S(1)}, u32[]{:S(2)}, u32[]{:S(2)}) collective-permute-start(f32[288,128]{1,0:T(8,128)S(1)} %get-tuple-element.10), channel_id=1, source_target_pairs={{1,2},{5,6},{9,10},{13,14},{17,18},{21,22},{25,26},{29,30},{33,34}... | collective-permute-start | bytes 442376 | tf_op jit(solution)/shard_map/ppermute | solution.py:512
  18.3 0.7 collective-permute-start.1
  19.0 11.9 %collective-permute-done.3 = bf16[150,2,2048]{2,1,0:T(2,128)(2,1)} collective-permute-done((bf16[150,2,2048]{2,1,0:T(2,128)(2,1)S(1)}, bf16[150,2,2048]{2,1,0:T(2,128)(2,1)}, u32[]{:S(2)}, u32[]{:S(2)}) %collective-permute-start.3) | collective-permute-done | bytes 1228832 | tf_op jit(solution)/shard_map/ppermute | solution.py:506
  30.9 1.7 %copy.25 = bf16[150,2,2048]{2,0,1:T(8,128)(2,1)S(1)} copy(bf16[150,2,2048]{2,1,0:T(2,128)(2,1)} %collective-permute-done.3) | data formatting | bytes 2457600 | tf_op jit(solution)/shard_map/ppermute | solution.py:506
  32.6 0.0 copy-start.6
  32.7 1.3 %cross_products.1.own = f32[184,128]{1,0:T(8,128)S(1)} custom-call(s32[2]{0:T(128)S(1)} %pad_add_fusion.place, bf16[2,150,2048]{2,1,0:T(8,128)(2,1)S(1)} %get-tuple-element.11.own, bf16[2,150,2048]{2,1,0:T(8,128)(2,1)S(1)} %bitcast.22), custom_call_target="tpu_custom_call" | custom-call | flops 400000000 | bytes 3000000 | tf_op jit(solution)/shard_map/cross_products/pallas_call | solution.py:174
  33.9 0.0 copy-start.3
  34.0 0.0 copy-start.4
  34.0 0.7 collective-permute-start.6
  34.6 1.8 %collective-permute-start.5 = (f32[184,128]{1,0:T(8,128)S(1)}, f32[184,128]{1,0:T(8,128)S(1)}, u32[]{:S(2)}, u32[]{:S(2)}) collective-permute-start(f32[184,128]{1,0:T(8,128)S(1)} %cross_products.1.own), channel_id=1, source_target_pairs={{1,2},{5,6},{9,10},{13,14},{17,18},{21,22},{25,26},{29,30},{33,34}... | collective-permute-start | bytes 282632 | tf_op jit(solution)/shard_map/ppermute | solution.py:516
  36.5 0.0 collective-permute-done.2.extra_two
  36.5 0.7 collective-permute-start.4
  37.2 0.0 collective-permute-done.1.extra_one
  37.2 0.0 collective-permute-done.swapped
  37.2 0.0 collective-permute-done.6.three
  37.2 1.6 %collective-permute-done.5.two = f32[184,128]{1,0:T(8,128)S(1)} collective-permute-done((f32[184,128]{1,0:T(8,128)S(1)}, f32[184,128]{1,0:T(8,128)S(1)}, u32[]{:S(2)}, u32[]{:S(2)}) %collective-permute-start.5) | collective-permute-done | bytes 94240 | tf_op jit(solution)/shard_map/ppermute | solution.py:516
  38.8 0.0 collective-permute-done.4.one
  38.8 0.6 merged.1
  39.4 25.2 %all_to_all.10 = f32[32,16,128]{2,1,0:T(8,128)S(1)} all-to-all(f32[32,16,128]{2,1,0:T(8,128)S(1)} %bitcast.27), channel_id=1, replica_groups=mesh['pix_0'=2,'pix_1'=8,'pix_2'=4,'pix_3'=2,'tm'=2] {'pix_1','pix_2'}, dimensions={0} | all-to-all | bytes 524288 | tf_op jit(solution)/shard_map/all_to_all | solution.py:519
  64.6 1.2 collective-permute-start.7
  65.8 4.0 %collective-permute-done.7 = f32[16,128]{1,0:T(8,128)S(1)} collective-permute-done((f32[16,128]{1,0:T(8,128)S(1)}, f32[16,128]{1,0:T(8,128)S(1)}, u32[]{:S(2)}, u32[]{:S(2)}) %collective-permute-start.7) | collective-permute-done | bytes 8224 | tf_op jit(solution)/shard_map/ppermute | solution.py:521
  69.9 0.7 broadcast_in_dim.12
  70.6 4.1 %all-to-all-start.1 = ((f32[32,16,128]{2,1,0:T(8,128)}), f32[32,16,128]{2,1,0:T(8,128)S(1)}, u32[]{:S(2)}, u32[]{:S(2)}) async-start(f32[32,16,128]{2,1,0:T(8,128)} %broadcast_in_dim.12), calls=%async_computation.1 | async-start | bytes 524288 | tf_op jit(solution)/shard_map/all_to_all | solution.py:522
  74.7 0.0 copy-done.6
  74.7 0.1 copy.18
  74.8 0.1 fusion.1
  74.9 0.1 fusion
  75.0 0.0 slice-start
  75.1 0.1 concatenate.9.start
  75.2 11.0 %all-to-all-done.1 = f32[32,16,128]{2,1,0:T(8,128)S(1)} async-done(((f32[32,16,128]{2,1,0:T(8,128)}), f32[32,16,128]{2,1,0:T(8,128)S(1)}, u32[]{:S(2)}, u32[]{:S(2)}) %all-to-all-start.1) | async-done | bytes 262176 | tf_op jit(solution)/shard_map/all_to_all | solution.py:522
  86.2 0.0 copy-done.3
  86.2 0.0 copy-done.4
  86.2 0.0 slice-start.1
  86.2 0.0 copy-start.2
  86.3 13.9 %iterate.1.mine = f32[128,384]{1,0:T(8,128)S(1)} custom-call(s32[2]{0:T(128)S(1)} %pad_add_fusion.place, s32[2]{0:T(128)S(1)} %copy-done.3, s32[2]{0:T(128)S(1)} %copy-done.4, f32[512,128]{1,0:T(8,128)S(1)} %bitcast.28, f32[128,384]{1,0:T(8,128)S(1)} %concatenate.9.start), custom_call_target="tpu_custom_call" | custom-call | flops 14000000000 | bytes 1000000 | tf_op jit(solution)/shard_map/iterate/pallas_call | solution.py:367
  100.2 1.3 %collective-permute-start.10 = (f32[128,384]{1,0:T(8,128)S(1)}, f32[128,384]{1,0:T(8,128)S(1)}, u32[]{:S(2)}, u32[]{:S(2)}) collective-permute-start(f32[128,384]{1,0:T(8,128)S(1)} %iterate.1.mine), channel_id=1, source_target_pairs={{2,1},{6,5},{10,9},{14,13},{18,17},{22,21},{26,25},{30,29},{34,33}... | collective-permute-start | bytes 589832 | tf_op jit(solution)/shard_map/ppermute | solution.py:527
  101.5 0.7 collective-permute-start.9
  102.2 0.1 collective-permute-start.8
  102.3 0.0 slice-done
  102.3 0.0 slice-done.1
  102.3 0.0 copy-done.2
  102.3 4.4 %own.1 = f32[1,4096]{1,0:T(1,128)S(1)} custom-call(s32[2]{0:T(128)S(1)} %pad_add_fusion.place, f32[128,384]{1,0:T(8,128)S(1)} %iterate.1.mine, bf16[2,2,150,4096]{3,2,1,0:T(8,128)(2,1)S(1)} %bitcast.19, bf16[2,150,4096]{2,1,0:T(8,128)(2,1)S(1)} %bitcast.25), custom_call_target="tpu_custom_call" | custom-call | flops 3000000000 | bytes 10000000 | tf_op jit(solution)/shard_map/own/pallas_call | solution.py:467
  106.7 0.5 collective-permute-done.10.two
  107.2 0.0 collective-permute-done.9.one
  107.2 0.0 collective-permute-done.8.other
  107.2 2.8 %shared.1 = f32[1,2048]{1,0:T(1,128)S(1)} custom-call(s32[2]{0:T(128)S(1)} %pad_add_fusion.place, f32[128,384]{1,0:T(8,128)S(1)} %iterate.1.mine, f32[128,384]{1,0:T(8,128)S(1)} %collective-permute-done.8.other, f32[128,384]{1,0:T(8,128)S(1)} %collective-permute-done.9.one, f32[128,384]{1,0:T(8,128)S(1)} %collective-permute-done.10.two, ...), custom_call_target="tpu_custom_call" | custom-call | flops 1500000000 | bytes 10000000 | tf_op jit(solution)/shard_map/shared/pallas_call | solution.py:467
  110.0 4.8 %collective-permute-start.11 = (f32[1,2048]{1,0:T(1,128)S(1)}, f32[1,2048]{1,0:T(1,128)S(1)}, u32[]{:S(2)}, u32[]{:S(2)}) collective-permute-start(f32[1,2048]{1,0:T(1,128)S(1)} %shared.1), channel_id=1, source_target_pairs={{1,0},{3,2},{5,4},{7,6},{9,8},{11,10},{13,12},{15,14},{17,16},{19,... | collective-permute-start | bytes 24584 | tf_op jit(solution)/shard_map/ppermute | solution.py:537
  114.9 4.7 %other.1 = (f32[1,4096]{1,0:T(1,128)S(1)}, f32[300,2,128]{2,1,0:T(2,128)}) custom-call(s32[2]{0:T(128)S(1)} %pad_add_fusion.place, f32[128,384]{1,0:T(8,128)S(1)} %iterate.1.mine, f32[128,384]{1,0:T(8,128)S(1)} %collective-permute-done.8.other, bf16[2,2,150,4096]{3,2,1,0:T(8,128)(2,1)S(1)} %bitcast.21, bf16[2,150,4096]{2,1,0:T(8,128)(2,1)S(1)} %bitcast.26), custom_call_target="tpu_custom_call" | custom-call | flops 3000000000 | bytes 10000000 | tf_op jit(solution)/shard_map/other/pallas_call | solution.py:467
  119.6 0.0 collective-permute-done.11
  119.6 0.6 pad_maximum_fusion
  (6 shorter events, 0.1 us)
Async XLA Ops:
  1.9 29.0 %collective-permute-start.3 = (bf16[150,2,2048]{2,1,0:T(2,128)(2,1)S(1)}, bf16[150,2,2048]{2,1,0:T(2,128)(2,1)}, u32[]{:S(2)}, u32[]{:S(2)}) collective-permute-start(bf16[150,2,2048]{2,1,0:T(2,128)(2,1)S(1)} %picked.1), channel_id=1, source_target_pairs={{0,1},{1,0},{2,3},{3,2},{4,5},{5,4},{6,7},{7,6},{8,9},{9,8},{10,11... | collective-permute-start | bytes 3686408 | tf_op jit(solution)/shard_map/ppermute | solution.py:506
  2.9 3.5 %copy-start.5 = (bf16[300,2,4096]{2,1,0:T(2,128)(2,1)S(1)}, bf16[300,2,4096]{2,1,0:T(2,128)(2,1)}, u32[]{:S(2)}) copy-start(bf16[300,2,4096]{2,1,0:T(2,128)(2,1)} %source.1) | copy-start | bytes 14745604
  6.3 3.7 %copy-start.1 = (bf16[150,2,4096]{2,0,1:T(8,128)(2,1)}, bf16[150,2,4096]{2,0,1:T(8,128)(2,1)S(1)}, u32[]{:S(2)}) copy-start(bf16[150,2,4096]{2,0,1:T(8,128)(2,1)S(1)} %copy.24) | copy-start | bytes 7372804
  9.9 5.1 %copy-start = (bf16[2,150,2,4096]{3,1,0,2:T(8,128)(2,1)}, bf16[2,150,2,4096]{3,1,0,2:T(8,128)(2,1)S(1)}, u32[]{:S(2)}) copy-start(bf16[2,150,2,4096]{3,1,0,2:T(8,128)(2,1)S(1)} %copy.23) | copy-start | bytes 14745604
  15.0 22.2 %collective-permute-start = (f32[512,128]{1,0:T(8,128)S(1)}, f32[512,128]{1,0:T(8,128)S(1)}, u32[]{:S(2)}, u32[]{:S(2)}) collective-permute-start(f32[512,128]{1,0:T(8,128)S(1)} %get-tuple-element.9), channel_id=1, source_target_pairs={{0,2},{2,0},{1,3},{3,1},{4,6},{6,4},{5,7},{7,5},{8,10},{10,8},{9,1... | collective-permute-start | bytes 786440 | tf_op jit(solution)/shard_map/ppermute | solution.py:510
  15.1 21.4 %collective-permute-start.2 = (f32[288,128]{1,0:T(8,128)S(1)}, f32[288,128]{1,0:T(8,128)S(1)}, u32[]{:S(2)}, u32[]{:S(2)}) collective-permute-start(f32[288,128]{1,0:T(8,128)S(1)} %get-tuple-element.10), channel_id=1, source_target_pairs={{1,2},{5,6},{9,10},{13,14},{17,18},{21,22},{25,26},{29,30},{33,34}... | collective-permute-start | bytes 442376 | tf_op jit(solution)/shard_map/ppermute | solution.py:512
  18.3 18.9 %collective-permute-start.1 = (f32[288,128]{1,0:T(8,128)S(1)}, f32[288,128]{1,0:T(8,128)S(1)}, u32[]{:S(2)}, u32[]{:S(2)}) collective-permute-start(f32[288,128]{1,0:T(8,128)S(1)} %get-tuple-element.10), channel_id=1, source_target_pairs={{3,2},{7,6},{11,10},{15,14},{19,18},{23,22},{27,26},{31,30},{35,34... | collective-permute-start | bytes 442376 | tf_op jit(solution)/shard_map/ppermute | solution.py:511
  32.6 42.1 %copy-start.6 = (f32[300,128]{1,0:T(8,128)S(1)}, f32[300,128]{1,0:T(8,128)}, u32[]{:S(2)}) copy-start(f32[300,128]{1,0:T(8,128)} %param.7) | copy-start | bytes 460804
  33.9 52.3 %copy-start.3 = (s32[2]{0:T(128)S(1)}, s32[2]{0:T(128)}, u32[]{:S(2)}) copy-start(s32[2]{0:T(128)} %low.1) | copy-start | bytes 28
  34.0 52.3 %copy-start.4 = (s32[2]{0:T(128)S(1)}, s32[2]{0:T(128)}, u32[]{:S(2)}) copy-start(s32[2]{0:T(128)} %high.1) | copy-start | bytes 28
  34.0 3.2 %collective-permute-start.6 = (f32[184,128]{1,0:T(8,128)S(1)}, f32[184,128]{1,0:T(8,128)S(1)}, u32[]{:S(2)}, u32[]{:S(2)}) collective-permute-start(f32[184,128]{1,0:T(8,128)S(1)} %cross_products.1.own), channel_id=1, source_target_pairs={{0,2},{4,6},{8,10},{12,14},{16,18},{20,22},{24,26},{28,30},{32,34}... | collective-permute-start | bytes 282632 | tf_op jit(solution)/shard_map/ppermute | solution.py:517
  34.6 4.2 %collective-permute-start.5 = (f32[184,128]{1,0:T(8,128)S(1)}, f32[184,128]{1,0:T(8,128)S(1)}, u32[]{:S(2)}, u32[]{:S(2)}) collective-permute-start(f32[184,128]{1,0:T(8,128)S(1)} %cross_products.1.own), channel_id=1, source_target_pairs={{1,2},{5,6},{9,10},{13,14},{17,18},{21,22},{25,26},{29,30},{33,34}... | collective-permute-start | bytes 282632 | tf_op jit(solution)/shard_map/ppermute | solution.py:516
  36.5 2.3 %collective-permute-start.4 = (f32[184,128]{1,0:T(8,128)S(1)}, f32[184,128]{1,0:T(8,128)S(1)}, u32[]{:S(2)}, u32[]{:S(2)}) collective-permute-start(f32[184,128]{1,0:T(8,128)S(1)} %cross_products.1.own), channel_id=1, source_target_pairs={{3,2},{7,6},{11,10},{15,14},{19,18},{23,22},{27,26},{31,30},{35,34... | collective-permute-start | bytes 282632 | tf_op jit(solution)/shard_map/ppermute | solution.py:515
  64.6 5.2 %collective-permute-start.7 = (f32[16,128]{1,0:T(8,128)S(1)}, f32[16,128]{1,0:T(8,128)S(1)}, u32[]{:S(2)}, u32[]{:S(2)}) collective-permute-start(f32[16,128]{1,0:T(8,128)S(1)} %reduce_sum.9), channel_id=1, source_target_pairs={{0,128},{128,0},{1,129},{129,1},{2,130},{130,2},{3,131},{131,3},{4... | collective-permute-start | bytes 24584 | tf_op jit(solution)/shard_map/ppermute | solution.py:521
  70.6 15.7 %all-to-all-start.1 = ((f32[32,16,128]{2,1,0:T(8,128)}), f32[32,16,128]{2,1,0:T(8,128)S(1)}, u32[]{:S(2)}, u32[]{:S(2)}) async-start(f32[32,16,128]{2,1,0:T(8,128)} %broadcast_in_dim.12), calls=%async_computation.1 | async-start | bytes 524288 | tf_op jit(solution)/shard_map/all_to_all | solution.py:522
  75.0 27.2 %slice-start = ((s8[4980736]{0:T(1024)(128)(4,1)}), s8[786432]{0:T(1024)(128)(4,1)S(1)}, s32[]{:S(2)}) async-start(s8[4980736]{0:T(1024)(128)(4,1)} %bitcast.17), calls=%async_computation.2 | async-start | bytes 1572864
  86.2 16.0 %slice-start.1 = ((s8[4980736]{0:T(1024)(128)(4,1)}), s8[4194304]{0:T(1024)(128)(4,1)S(1)}, s32[]{:S(2)}) async-start(s8[4980736]{0:T(1024)(128)(4,1)} %bitcast.17), calls=%async_computation.3 | async-start | bytes 8388608
  86.2 16.0 %copy-start.2 = (bf16[150,2,4096]{2,0,1:T(8,128)(2,1)S(1)}, bf16[150,2,4096]{2,0,1:T(8,128)(2,1)}, u32[]{:S(2)}) copy-start(bf16[150,2,4096]{2,0,1:T(8,128)(2,1)} %copy-done.1) | copy-start | bytes 7372804
  100.2 7.0 %collective-permute-start.10 = (f32[128,384]{1,0:T(8,128)S(1)}, f32[128,384]{1,0:T(8,128)S(1)}, u32[]{:S(2)}, u32[]{:S(2)}) collective-permute-start(f32[128,384]{1,0:T(8,128)S(1)} %iterate.1.mine), channel_id=1, source_target_pairs={{2,1},{6,5},{10,9},{14,13},{18,17},{22,21},{26,25},{30,29},{34,33}... | collective-permute-start | bytes 589832 | tf_op jit(solution)/shard_map/ppermute | solution.py:527
  101.5 5.7 %collective-permute-start.9 = (f32[128,384]{1,0:T(8,128)S(1)}, f32[128,384]{1,0:T(8,128)S(1)}, u32[]{:S(2)}, u32[]{:S(2)}) collective-permute-start(f32[128,384]{1,0:T(8,128)S(1)} %iterate.1.mine), channel_id=1, source_target_pairs={{2,3},{6,7},{10,11},{14,15},{18,19},{22,23},{26,27},{30,31},{34,35... | collective-permute-start | bytes 589832 | tf_op jit(solution)/shard_map/ppermute | solution.py:526
  102.2 5.0 %collective-permute-start.8 = (f32[128,384]{1,0:T(8,128)S(1)}, f32[128,384]{1,0:T(8,128)S(1)}, u32[]{:S(2)}, u32[]{:S(2)}) collective-permute-start(f32[128,384]{1,0:T(8,128)S(1)} %iterate.1.mine), channel_id=1, source_target_pairs={{0,2},{2,0},{1,3},{3,1},{4,6},{6,4},{5,7},{7,5},{8,10},{10,8},{9,1... | collective-permute-start | bytes 589832 | tf_op jit(solution)/shard_map/ppermute | solution.py:528
  110.0 9.5 %collective-permute-start.11 = (f32[1,2048]{1,0:T(1,128)S(1)}, f32[1,2048]{1,0:T(1,128)S(1)}, u32[]{:S(2)}, u32[]{:S(2)}) collective-permute-start(f32[1,2048]{1,0:T(1,128)S(1)} %shared.1), channel_id=1, source_target_pairs={{1,0},{3,2},{5,4},{7,6},{9,8},{11,10},{13,12},{15,14},{17,16},{19,... | collective-permute-start | bytes 24584 | tf_op jit(solution)/shard_map/ppermute | solution.py:537

commit v5 on v4

--- a/solution.py
+++ b/solution.py
@@ -210,6 +210,21 @@
         compiler_params=parameters(),
         name="merged",
     )(place, *parts)
+
+
+def spread_kernel(one, two, out):
+    out[...] = jnp.broadcast_to((one[...] + two[...])[None], out.shape)
+
+
+def spread(one, two, copies):
+    return pl.pallas_call(
+        spread_kernel,
+        out_shape=jax.ShapeDtypeStruct((copies, *one.shape), F32),
+        in_specs=[VMEM, VMEM],
+        out_specs=VMEM,
+        compiler_params=parameters(),
+        name="spread",
+    )(one, two)
 
 
 def unpack(rows, gram):
@@ -339,14 +354,28 @@
         )
 
 
-def iterate_kernel(place, low, high, packed, start, basis, gram, work):
+FIRST = (0, 0, 1, 0, 1, 2)
+SECOND = (0, 1, 0, 2, 1, 0)
+
+
+def iterate_kernel(place, low, high, packed, start, basis, gram, work, deep):
     unpack(packed[...], gram)
+    split = thirds(gram[...])
+    for block, index in enumerate(SECOND):
+        deep[SPAN * block : SPAN * (block + 1), :] = split[index]
     work[:, K:] = start[...]
 
     def step(_, carry):
-        image = jnp.dot(work[:, K:], gram[...], precision=HI, preferred_element_type=F32)
-        work[:, 0:K] = lax.dot_general(
-            image, image, (((1,), (1,)), ((), ())), precision=HI, preferred_element_type=F32
+        split = thirds(work[:, K:])
+        image = jnp.dot(
+            jnp.concatenate([split[index] for index in FIRST], axis=1),
+            deep[...],
+            preferred_element_type=F32,
+        )
+        split = thirds(image)
+        work[:, 0:K] = across(
+            jnp.concatenate([split[index] for index in FIRST], axis=1),
+            jnp.concatenate([split[index] for index in SECOND], axis=1),
         )
         work[:, K:] = image
         for index in range(K // TILE):
@@ -369,7 +398,11 @@
         out_shape=jax.ShapeDtypeStruct((K, SPAN), F32),
         in_specs=[SMEM, SMEM, SMEM, VMEM, VMEM],
         out_specs=VMEM,
-        scratch_shapes=[pltpu.VMEM((SPAN, SPAN), F32), pltpu.VMEM((K, K + SPAN), F32)],
+        scratch_shapes=[
+            pltpu.VMEM((SPAN, SPAN), F32),
+            pltpu.VMEM((K, K + SPAN), F32),
+            pltpu.VMEM((len(SECOND) * SPAN, SPAN), BF16),
+        ],
         cost_estimate=pl.CostEstimate(flops=14 * 10**9, bytes_accessed=10**6, transcendentals=0),
         compiler_params=pltpu.CompilerParams(vmem_limit_bytes=LIMIT),
         name="iterate",
@@ -394,7 +427,7 @@
                 block = ref[part, :, where] if index is None else ref[part, index, :, where]
                 chunk[part, 128 * side : 128 * side + MAIN, :] = block[0:MAIN]
                 chunk[part, 256 + 32 * side : 256 + 32 * side + REM, :] = block[MAIN:HALF]
-            out = jnp.dot(proj[...], chunk[part], preferred_element_type=F32)
+            out = jnp.dot(proj[0:312], chunk[part], preferred_element_type=F32)
             total += jnp.sum(out * out, axis=0, keepdims=True)
         power[:, pl.ds(pl.multiple_of(begin + at, 128), CHUNK)] = total / WINDOW
         return carry
@@ -518,10 +551,8 @@
     mine = merged(place, keep, swapped, extra_one, extra_two, late, one, two, three)
     pieces = lax.all_to_all(mine.reshape(chips, PACKED // chips, 128), PLANE, 0, 0, tiled=True)
     piece = pieces.sum(axis=0)
-    piece = piece + lax.ppermute(piece, "pix_0", [(0, 1), (1, 0)])
-    packed = lax.all_to_all(
-        jnp.broadcast_to(piece[None], pieces.shape), PLANE, 0, 0, tiled=True
-    ).reshape(PACKED, 128)
+    copies = spread(piece, lax.ppermute(piece, "pix_0", [(0, 1), (1, 0)]), chips)
+    packed = lax.all_to_all(copies, PLANE, 0, 0, tiled=True).reshape(PACKED, 128)
     found = iterate(place, low_rank, high_rank, packed, in_lanes(start_basis))
     one = lax.ppermute(found, pair, [(2, 3)])
     two = lax.ppermute(found, pair, [(2, 1)])

time: 121 us -> 121 us (level)
  no operation moved by 1% of the time
where the time goes in v5:
time: 121 us; the launch traced here: 120 us
  Pallas kernels  34.6 us (29%)
  waiting for transfers between devices  29.1 us (24%)
  blocking collectives  25.2 us (21%)
  starting transfers between devices  20.2 us (17%)
  local copies, waits for them, and re-layouts  9.26 us (8%)
    all_to_all x1, blocking collectives, body(): lax.all_to_all(mine.reshape(chips, PACKED // chips, 128), PLANE, 0, 0, ti...  25.2 us
    pallas_call x1, Pallas kernels, iterate(): pl.pallas_call(iterate_kernel, out_shape=jax.ShapeDtypeStruct((K, SPAN),...  13.8 us
    ppermute x1, waiting for transfers between devices, body(): near = lax.ppermute(picked(iq), 'tm', [(0, 1), (1, 0)])  11.9 us
    pallas_call x3, Pallas kernels, power_call(): pl.pallas_call(kernel, out_shape=outs, in_specs=[SMEM] + [VMEM] * (len(ar...  11.9 us
    all_to_all x1, waiting for transfers between devices, body(): lax.all_to_all(copies, PLANE, 0, 0, tiled=True).reshape(PACKED, 128)  11 us
    pallas_call x1, Pallas kernels, local_products(): pl.pallas_call(local_kernel, out_shape=(shape, shape, jax.ShapeDtypeStruc...  4.97 us
    ppermute x1, starting transfers between devices, body(): back = lax.ppermute(shared, 'tm', [(1, 0)])  4.82 us
    all_to_all x1, starting transfers between devices, body(): lax.all_to_all(copies, PLANE, 0, 0, tiled=True).reshape(PACKED, 128)  4.1 us
  transfers between devices with their start and end apart: 13, of which 5 were waited for; matrix products, arithmetic and copies ran while one was open for 8% of the time, Pallas kernels for 13%

profile of v5, /device:TPU:6, one launch (start us, length us, event | category | flops | bytes accessed | tf_op | source)
XLA Modules:
  0.0 120.2 jit_solution(4715178802604992894)
XLA Ops:
  0.6 1.3 %picked.1 = bf16[150,2,2048]{2,1,0:T(2,128)(2,1)S(1)} custom-call(bf16[300,2,4096]{2,1,0:T(2,128)(2,1)} %source.1), custom_call_target="tpu_custom_call" | custom-call | tf_op jit(solution)/shard_map/picked/pallas_call | solution.py:63
  1.9 0.9 collective-permute-start.3
  2.9 0.0 copy-start.5
  2.9 3.4 %copy.24 = bf16[150,2,4096]{2,0,1:T(8,128)(2,1)S(1)} copy(bf16[150,2,4096]{2,1,0:T(2,128)(2,1)} %param.6) | data formatting | bytes 4915200 | tf_op args[1]
  6.3 0.0 copy-start.1
  6.3 0.0 copy-done.5
  6.3 3.6 %copy.23 = bf16[2,150,2,4096]{3,1,0,2:T(8,128)(2,1)S(1)} copy(bf16[2,150,2,4096]{3,2,1,0:T(2,128)(2,1)S(1)} %bitcast.29) | data formatting | bytes 9830400 | tf_op jit(solution)/shard_map/reshape | solution.py:540
  9.9 0.0 copy-start
  9.9 0.1 pad_add_fusion.place
  10.0 0.0 copy-done.1
  10.0 5.0 %local_products.1 = (f32[512,128]{1,0:T(8,128)S(1)}, f32[512,128]{1,0:T(8,128)S(1)}, f32[288,128]{1,0:T(8,128)S(1)}, bf16[2,150,2048]{2,1,0:T(8,128)(2,1)S(1)}) custom-call(s32[2]{0:T(128)S(1)} %pad_add_fusion.place, bf16[2,2,150,4096]{3,2,1,0:T(8,128)(2,1)S(1)} %bitcast.16, bf16[2,150,4096]{2,1,0:T(8,128)(2,1)S(1)} %bitcast.24), custom_call_target="tpu_custom_call" | custom-call | flops 4000000000 | bytes 8000000 | tf_op jit(solution)/shard_map/local_products/pallas_call | solution.py:137
  15.0 0.0 copy-done
  15.0 0.1 collective-permute-start
  15.1 3.2 %collective-permute-start.2 = (f32[288,128]{1,0:T(8,128)S(1)}, f32[288,128]{1,0:T(8,128)S(1)}, u32[]{:S(2)}, u32[]{:S(2)}) collective-permute-start(f32[288,128]{1,0:T(8,128)S(1)} %get-tuple-element.10), channel_id=1, source_target_pairs={{1,2},{5,6},{9,10},{13,14},{17,18},{21,22},{25,26},{29,30},{33,34}... | collective-permute-start | bytes 442376 | tf_op jit(solution)/shard_map/ppermute | solution.py:545
  18.3 0.7 collective-permute-start.1
  19.0 11.9 %collective-permute-done.3 = bf16[150,2,2048]{2,1,0:T(2,128)(2,1)} collective-permute-done((bf16[150,2,2048]{2,1,0:T(2,128)(2,1)S(1)}, bf16[150,2,2048]{2,1,0:T(2,128)(2,1)}, u32[]{:S(2)}, u32[]{:S(2)}) %collective-permute-start.3) | collective-permute-done | bytes 1228832 | tf_op jit(solution)/shard_map/ppermute | solution.py:539
  30.9 1.7 %copy.25 = bf16[150,2,2048]{2,0,1:T(8,128)(2,1)S(1)} copy(bf16[150,2,2048]{2,1,0:T(2,128)(2,1)} %collective-permute-done.3) | data formatting | bytes 2457600 | tf_op jit(solution)/shard_map/ppermute | solution.py:539
  32.6 0.0 copy-start.6
  32.7 1.3 %cross_products.1.own = f32[184,128]{1,0:T(8,128)S(1)} custom-call(s32[2]{0:T(128)S(1)} %pad_add_fusion.place, bf16[2,150,2048]{2,1,0:T(8,128)(2,1)S(1)} %get-tuple-element.11.own, bf16[2,150,2048]{2,1,0:T(8,128)(2,1)S(1)} %bitcast.22), custom_call_target="tpu_custom_call" | custom-call | flops 400000000 | bytes 3000000 | tf_op jit(solution)/shard_map/cross_products/pallas_call | solution.py:174
  33.9 0.0 copy-start.3
  34.0 0.0 copy-start.4
  34.0 0.7 collective-permute-start.6
  34.6 1.8 %collective-permute-start.5 = (f32[184,128]{1,0:T(8,128)S(1)}, f32[184,128]{1,0:T(8,128)S(1)}, u32[]{:S(2)}, u32[]{:S(2)}) collective-permute-start(f32[184,128]{1,0:T(8,128)S(1)} %cross_products.1.own), channel_id=1, source_target_pairs={{1,2},{5,6},{9,10},{13,14},{17,18},{21,22},{25,26},{29,30},{33,34}... | collective-permute-start | bytes 282632 | tf_op jit(solution)/shard_map/ppermute | solution.py:549
  36.5 0.0 collective-permute-done.2.extra_two
  36.5 0.7 collective-permute-start.4
  37.2 0.0 collective-permute-done.1.extra_one
  37.2 0.0 collective-permute-done.swapped
  37.2 0.0 collective-permute-done.6.three
  37.2 1.6 %collective-permute-done.5.two = f32[184,128]{1,0:T(8,128)S(1)} collective-permute-done((f32[184,128]{1,0:T(8,128)S(1)}, f32[184,128]{1,0:T(8,128)S(1)}, u32[]{:S(2)}, u32[]{:S(2)}) %collective-permute-start.5) | collective-permute-done | bytes 94240 | tf_op jit(solution)/shard_map/ppermute | solution.py:549
  38.8 0.0 collective-permute-done.4.one
  38.8 0.6 merged.1
  39.4 25.2 %all_to_all.10 = f32[32,16,128]{2,1,0:T(8,128)S(1)} all-to-all(f32[32,16,128]{2,1,0:T(8,128)S(1)} %bitcast.27), channel_id=1, replica_groups=mesh['pix_0'=2,'pix_1'=8,'pix_2'=4,'pix_3'=2,'tm'=2] {'pix_1','pix_2'}, dimensions={0} | all-to-all | bytes 524288 | tf_op jit(solution)/shard_map/all_to_all | solution.py:552
  64.6 1.2 %collective-permute-start.7 = (f32[16,128]{1,0:T(8,128)S(1)}, f32[16,128]{1,0:T(8,128)S(1)}, u32[]{:S(2)}, u32[]{:S(2)}) collective-permute-start(f32[16,128]{1,0:T(8,128)S(1)} %reduce_sum.9.one), channel_id=1, source_target_pairs={{0,128},{128,0},{1,129},{129,1},{2,130},{130,2},{3,131},{131,3},{4... | collective-permute-start | bytes 24584 | tf_op jit(solution)/shard_map/ppermute | solution.py:554
  65.8 4.0 %collective-permute-done.7.two = f32[16,128]{1,0:T(8,128)S(1)} collective-permute-done((f32[16,128]{1,0:T(8,128)S(1)}, f32[16,128]{1,0:T(8,128)S(1)}, u32[]{:S(2)}, u32[]{:S(2)}) %collective-permute-start.7) | collective-permute-done | bytes 8224 | tf_op jit(solution)/shard_map/ppermute | solution.py:554
  69.9 0.7 spread.1
  70.6 4.1 %all-to-all-start.1 = ((f32[32,16,128]{2,1,0:T(8,128)}), f32[32,16,128]{2,1,0:T(8,128)S(1)}, u32[]{:S(2)}, u32[]{:S(2)}) async-start(f32[32,16,128]{2,1,0:T(8,128)} %spread.1), calls=%async_computation.1 | async-start | bytes 524288 | tf_op jit(solution)/shard_map/all_to_all | solution.py:555
  74.7 0.0 copy-done.6
  74.7 0.1 copy.18
  74.8 0.1 fusion.1
  74.9 0.1 fusion
  75.0 0.0 slice-start
  75.0 0.1 concatenate.9.start
  75.2 11.0 %all-to-all-done.1 = f32[32,16,128]{2,1,0:T(8,128)S(1)} async-done(((f32[32,16,128]{2,1,0:T(8,128)}), f32[32,16,128]{2,1,0:T(8,128)S(1)}, u32[]{:S(2)}, u32[]{:S(2)}) %all-to-all-start.1) | async-done | bytes 262176 | tf_op jit(solution)/shard_map/all_to_all | solution.py:555
  86.2 0.0 copy-done.3
  86.2 0.0 copy-done.4
  86.2 0.0 slice-start.1
  86.2 0.0 copy-start.2
  86.2 13.8 %iterate.1.mine = f32[128,384]{1,0:T(8,128)S(1)} custom-call(s32[2]{0:T(128)S(1)} %pad_add_fusion.place, s32[2]{0:T(128)S(1)} %copy-done.3, s32[2]{0:T(128)S(1)} %copy-done.4, f32[512,128]{1,0:T(8,128)S(1)} %bitcast.28, f32[128,384]{1,0:T(8,128)S(1)} %concatenate.9.start), custom_call_target="tpu_custom_call" | custom-call | flops 14000000000 | bytes 1000000 | tf_op jit(solution)/shard_map/iterate/pallas_call | solution.py:396
  100.1 1.3 %collective-permute-start.10 = (f32[128,384]{1,0:T(8,128)S(1)}, f32[128,384]{1,0:T(8,128)S(1)}, u32[]{:S(2)}, u32[]{:S(2)}) collective-permute-start(f32[128,384]{1,0:T(8,128)S(1)} %iterate.1.mine), channel_id=1, source_target_pairs={{2,1},{6,5},{10,9},{14,13},{18,17},{22,21},{26,25},{30,29},{34,33}... | collective-permute-start | bytes 589832 | tf_op jit(solution)/shard_map/ppermute | solution.py:558
  101.4 0.7 collective-permute-start.9
  102.1 0.1 collective-permute-start.8
  102.2 0.0 slice-done
  102.2 0.0 slice-done.1
  102.2 0.0 copy-done.2
  102.2 4.4 %own.1 = f32[1,4096]{1,0:T(1,128)S(1)} custom-call(s32[2]{0:T(128)S(1)} %pad_add_fusion.place, f32[128,384]{1,0:T(8,128)S(1)} %iterate.1.mine, bf16[2,2,150,4096]{3,2,1,0:T(8,128)(2,1)S(1)} %bitcast.19, bf16[2,150,4096]{2,1,0:T(8,128)(2,1)S(1)} %bitcast.25), custom_call_target="tpu_custom_call" | custom-call | flops 3000000000 | bytes 10000000 | tf_op jit(solution)/shard_map/own/pallas_call | solution.py:500
  106.6 0.5 collective-permute-done.10.two
  107.1 0.0 collective-permute-done.9.one
  107.1 0.0 collective-permute-done.8.other
  107.1 2.8 %shared.1 = f32[1,2048]{1,0:T(1,128)S(1)} custom-call(s32[2]{0:T(128)S(1)} %pad_add_fusion.place, f32[128,384]{1,0:T(8,128)S(1)} %iterate.1.mine, f32[128,384]{1,0:T(8,128)S(1)} %collective-permute-done.8.other, f32[128,384]{1,0:T(8,128)S(1)} %collective-permute-done.9.one, f32[128,384]{1,0:T(8,128)S(1)} %collective-permute-done.10.two, ...), custom_call_target="tpu_custom_call" | custom-call | flops 1500000000 | bytes 10000000 | tf_op jit(solution)/shard_map/shared/pallas_call | solution.py:500
  109.9 4.8 %collective-permute-start.11 = (f32[1,2048]{1,0:T(1,128)S(1)}, f32[1,2048]{1,0:T(1,128)S(1)}, u32[]{:S(2)}, u32[]{:S(2)}) collective-permute-start(f32[1,2048]{1,0:T(1,128)S(1)} %shared.1), channel_id=1, source_target_pairs={{1,0},{3,2},{5,4},{7,6},{9,8},{11,10},{13,12},{15,14},{17,16},{19,... | collective-permute-start | bytes 24584 | tf_op jit(solution)/shard_map/ppermute | solution.py:568
  114.8 4.7 %other.1 = (f32[1,4096]{1,0:T(1,128)S(1)}, f32[300,2,128]{2,1,0:T(2,128)}) custom-call(s32[2]{0:T(128)S(1)} %pad_add_fusion.place, f32[128,384]{1,0:T(8,128)S(1)} %iterate.1.mine, f32[128,384]{1,0:T(8,128)S(1)} %collective-permute-done.8.other, bf16[2,2,150,4096]{3,2,1,0:T(8,128)(2,1)S(1)} %bitcast.21, bf16[2,150,4096]{2,1,0:T(8,128)(2,1)S(1)} %bitcast.26), custom_call_target="tpu_custom_call" | custom-call | flops 3000000000 | bytes 10000000 | tf_op jit(solution)/shard_map/other/pallas_call | solution.py:500
  119.5 0.0 collective-permute-done.11
  119.5 0.6 pad_maximum_fusion
  (5 shorter events, 0.1 us)
Async XLA Ops:
  1.9 29.0 %collective-permute-start.3 = (bf16[150,2,2048]{2,1,0:T(2,128)(2,1)S(1)}, bf16[150,2,2048]{2,1,0:T(2,128)(2,1)}, u32[]{:S(2)}, u32[]{:S(2)}) collective-permute-start(bf16[150,2,2048]{2,1,0:T(2,128)(2,1)S(1)} %picked.1), channel_id=1, source_target_pairs={{0,1},{1,0},{2,3},{3,2},{4,5},{5,4},{6,7},{7,6},{8,9},{9,8},{10,11... | collective-permute-start | bytes 3686408 | tf_op jit(solution)/shard_map/ppermute | solution.py:539
  2.9 3.5 %copy-start.5 = (bf16[300,2,4096]{2,1,0:T(2,128)(2,1)S(1)}, bf16[300,2,4096]{2,1,0:T(2,128)(2,1)}, u32[]{:S(2)}) copy-start(bf16[300,2,4096]{2,1,0:T(2,128)(2,1)} %source.1) | copy-start | bytes 14745604
  6.3 3.7 %copy-start.1 = (bf16[150,2,4096]{2,0,1:T(8,128)(2,1)}, bf16[150,2,4096]{2,0,1:T(8,128)(2,1)S(1)}, u32[]{:S(2)}) copy-start(bf16[150,2,4096]{2,0,1:T(8,128)(2,1)S(1)} %copy.24) | copy-start | bytes 7372804
  9.9 5.1 %copy-start = (bf16[2,150,2,4096]{3,1,0,2:T(8,128)(2,1)}, bf16[2,150,2,4096]{3,1,0,2:T(8,128)(2,1)S(1)}, u32[]{:S(2)}) copy-start(bf16[2,150,2,4096]{3,1,0,2:T(8,128)(2,1)S(1)} %copy.23) | copy-start | bytes 14745604
  15.0 22.2 %collective-permute-start = (f32[512,128]{1,0:T(8,128)S(1)}, f32[512,128]{1,0:T(8,128)S(1)}, u32[]{:S(2)}, u32[]{:S(2)}) collective-permute-start(f32[512,128]{1,0:T(8,128)S(1)} %get-tuple-element.9), channel_id=1, source_target_pairs={{0,2},{2,0},{1,3},{3,1},{4,6},{6,4},{5,7},{7,5},{8,10},{10,8},{9,1... | collective-permute-start | bytes 786440 | tf_op jit(solution)/shard_map/ppermute | solution.py:543
  15.1 21.4 %collective-permute-start.2 = (f32[288,128]{1,0:T(8,128)S(1)}, f32[288,128]{1,0:T(8,128)S(1)}, u32[]{:S(2)}, u32[]{:S(2)}) collective-permute-start(f32[288,128]{1,0:T(8,128)S(1)} %get-tuple-element.10), channel_id=1, source_target_pairs={{1,2},{5,6},{9,10},{13,14},{17,18},{21,22},{25,26},{29,30},{33,34}... | collective-permute-start | bytes 442376 | tf_op jit(solution)/shard_map/ppermute | solution.py:545
  18.3 18.9 %collective-permute-start.1 = (f32[288,128]{1,0:T(8,128)S(1)}, f32[288,128]{1,0:T(8,128)S(1)}, u32[]{:S(2)}, u32[]{:S(2)}) collective-permute-start(f32[288,128]{1,0:T(8,128)S(1)} %get-tuple-element.10), channel_id=1, source_target_pairs={{3,2},{7,6},{11,10},{15,14},{19,18},{23,22},{27,26},{31,30},{35,34... | collective-permute-start | bytes 442376 | tf_op jit(solution)/shard_map/ppermute | solution.py:544
  32.6 42.1 %copy-start.6 = (f32[300,128]{1,0:T(8,128)S(1)}, f32[300,128]{1,0:T(8,128)}, u32[]{:S(2)}) copy-start(f32[300,128]{1,0:T(8,128)} %param.7) | copy-start | bytes 460804
  33.9 52.3 %copy-start.3 = (s32[2]{0:T(128)S(1)}, s32[2]{0:T(128)}, u32[]{:S(2)}) copy-start(s32[2]{0:T(128)} %low.1) | copy-start | bytes 28
  34.0 52.3 %copy-start.4 = (s32[2]{0:T(128)S(1)}, s32[2]{0:T(128)}, u32[]{:S(2)}) copy-start(s32[2]{0:T(128)} %high.1) | copy-start | bytes 28
  34.0 3.2 %collective-permute-start.6 = (f32[184,128]{1,0:T(8,128)S(1)}, f32[184,128]{1,0:T(8,128)S(1)}, u32[]{:S(2)}, u32[]{:S(2)}) collective-permute-start(f32[184,128]{1,0:T(8,128)S(1)} %cross_products.1.own), channel_id=1, source_target_pairs={{0,2},{4,6},{8,10},{12,14},{16,18},{20,22},{24,26},{28,30},{32,34}... | collective-permute-start | bytes 282632 | tf_op jit(solution)/shard_map/ppermute | solution.py:550
  34.6 4.2 %collective-permute-start.5 = (f32[184,128]{1,0:T(8,128)S(1)}, f32[184,128]{1,0:T(8,128)S(1)}, u32[]{:S(2)}, u32[]{:S(2)}) collective-permute-start(f32[184,128]{1,0:T(8,128)S(1)} %cross_products.1.own), channel_id=1, source_target_pairs={{1,2},{5,6},{9,10},{13,14},{17,18},{21,22},{25,26},{29,30},{33,34}... | collective-permute-start | bytes 282632 | tf_op jit(solution)/shard_map/ppermute | solution.py:549
  36.5 2.3 %collective-permute-start.4 = (f32[184,128]{1,0:T(8,128)S(1)}, f32[184,128]{1,0:T(8,128)S(1)}, u32[]{:S(2)}, u32[]{:S(2)}) collective-permute-start(f32[184,128]{1,0:T(8,128)S(1)} %cross_products.1.own), channel_id=1, source_target_pairs={{3,2},{7,6},{11,10},{15,14},{19,18},{23,22},{27,26},{31,30},{35,34... | collective-permute-start | bytes 282632 | tf_op jit(solution)/shard_map/ppermute | solution.py:548
  64.6 5.2 %collective-permute-start.7 = (f32[16,128]{1,0:T(8,128)S(1)}, f32[16,128]{1,0:T(8,128)S(1)}, u32[]{:S(2)}, u32[]{:S(2)}) collective-permute-start(f32[16,128]{1,0:T(8,128)S(1)} %reduce_sum.9.one), channel_id=1, source_target_pairs={{0,128},{128,0},{1,129},{129,1},{2,130},{130,2},{3,131},{131,3},{4... | collective-permute-start | bytes 24584 | tf_op jit(solution)/shard_map/ppermute | solution.py:554
  70.6 15.7 %all-to-all-start.1 = ((f32[32,16,128]{2,1,0:T(8,128)}), f32[32,16,128]{2,1,0:T(8,128)S(1)}, u32[]{:S(2)}, u32[]{:S(2)}) async-start(f32[32,16,128]{2,1,0:T(8,128)} %spread.1), calls=%async_computation.1 | async-start | bytes 524288 | tf_op jit(solution)/shard_map/all_to_all | solution.py:555
  75.0 27.1 %slice-start = ((s8[4980736]{0:T(1024)(128)(4,1)}), s8[786432]{0:T(1024)(128)(4,1)S(1)}, s32[]{:S(2)}) async-start(s8[4980736]{0:T(1024)(128)(4,1)} %bitcast.17), calls=%async_computation.2 | async-start | bytes 1572864
  86.2 15.9 %slice-start.1 = ((s8[4980736]{0:T(1024)(128)(4,1)}), s8[4194304]{0:T(1024)(128)(4,1)S(1)}, s32[]{:S(2)}) async-start(s8[4980736]{0:T(1024)(128)(4,1)} %bitcast.17), calls=%async_computation.3 | async-start | bytes 8388608
  86.2 15.9 %copy-start.2 = (bf16[150,2,4096]{2,0,1:T(8,128)(2,1)S(1)}, bf16[150,2,4096]{2,0,1:T(8,128)(2,1)}, u32[]{:S(2)}) copy-start(bf16[150,2,4096]{2,0,1:T(8,128)(2,1)} %copy-done.1) | copy-start | bytes 7372804
  100.1 7.0 %collective-permute-start.10 = (f32[128,384]{1,0:T(8,128)S(1)}, f32[128,384]{1,0:T(8,128)S(1)}, u32[]{:S(2)}, u32[]{:S(2)}) collective-permute-start(f32[128,384]{1,0:T(8,128)S(1)} %iterate.1.mine), channel_id=1, source_target_pairs={{2,1},{6,5},{10,9},{14,13},{18,17},{22,21},{26,25},{30,29},{34,33}... | collective-permute-start | bytes 589832 | tf_op jit(solution)/shard_map/ppermute | solution.py:558
  101.4 5.7 %collective-permute-start.9 = (f32[128,384]{1,0:T(8,128)S(1)}, f32[128,384]{1,0:T(8,128)S(1)}, u32[]{:S(2)}, u32[]{:S(2)}) collective-permute-start(f32[128,384]{1,0:T(8,128)S(1)} %iterate.1.mine), channel_id=1, source_target_pairs={{2,3},{6,7},{10,11},{14,15},{18,19},{22,23},{26,27},{30,31},{34,35... | collective-permute-start | bytes 589832 | tf_op jit(solution)/shard_map/ppermute | solution.py:557
  102.1 5.0 %collective-permute-start.8 = (f32[128,384]{1,0:T(8,128)S(1)}, f32[128,384]{1,0:T(8,128)S(1)}, u32[]{:S(2)}, u32[]{:S(2)}) collective-permute-start(f32[128,384]{1,0:T(8,128)S(1)} %iterate.1.mine), channel_id=1, source_target_pairs={{0,2},{2,0},{1,3},{3,1},{4,6},{6,4},{5,7},{7,5},{8,10},{10,8},{9,1... | collective-permute-start | bytes 589832 | tf_op jit(solution)/shard_map/ppermute | solution.py:559
  109.9 9.5 %collective-permute-start.11 = (f32[1,2048]{1,0:T(1,128)S(1)}, f32[1,2048]{1,0:T(1,128)S(1)}, u32[]{:S(2)}, u32[]{:S(2)}) collective-permute-start(f32[1,2048]{1,0:T(1,128)S(1)} %shared.1), channel_id=1, source_target_pairs={{1,0},{3,2},{5,4},{7,6},{9,8},{11,10},{13,12},{15,14},{17,16},{19,... | collective-permute-start | bytes 24584 | tf_op jit(solution)/shard_map/ppermute | solution.py:568
